TPU v7x, 128 devices: a whole 4x4x4 slice. The times are simulated.
128 devices in a mesh: gx: 16 (over z_lo, x, core), gy: 8 (over y, z_hi).
Axes of the slice: x: 4, y: 4, z: 4 (z_hi: 2, z_lo: 2; z = z_hi * 2 + z_lo), core: 2. Of those that a mesh axis runs over, the one named last changes fastest.
Arguments:
- pair_in: bfloat16 [1024, 1024, 128], P(('gx', 'gy')), may hold values from -6 to 6
- residue_mask: int32 [1024], P(('gx', 'gy')), may hold values 0 or 1
- norm_start: float32 [128], replicated, may hold values from 0.25 to 1.75
- proj_start: bfloat16 [128, 512], replicated, may hold values from -0.5 to 0.5
- gate_bias_start: float32 [128], replicated, may hold values from -4 to 4
- bias_w_start: bfloat16 [128, 4], replicated, may hold values from -1.5 to 1.5
- out_w_start: bfloat16 [128, 128], replicated, may hold values from -1 to 1
- norm_end: float32 [128], replicated, may hold values from 0.25 to 1.75
- proj_end: bfloat16 [128, 512], replicated, may hold values from -0.5 to 0.5
- gate_bias_end: float32 [128], replicated, may hold values from -4 to 4
- bias_w_end: bfloat16 [128, 4], replicated, may hold values from -1.5 to 1.5
- out_w_end: bfloat16 [128, 128], replicated, may hold values from -1 to 1
- norm_trans: float32 [128], replicated, may hold values from 0.25 to 1.75
- trans_in: bfloat16 [128, 512], replicated, may hold values from -0.5 to 0.5
- trans_bias: float32 [512], replicated, may hold values from -4 to 4
- trans_out: bfloat16 [512, 128], replicated, may hold values from -0.375 to 0.375
Outputs:
- pair_out: bfloat16 [1024, 1024, 128], P(('gx', 'gy'))
Inputs may be any that keep to these rules, and one draw needn't show every extreme that they name: residue_mask holds only 0 and 1.
All inputs are finite; a program needn't handle non-finite values.
Results may differ from a plain program's by a relative error of at most 0.02.
Values may be sent and summed in bfloat16 or wider, within the bound.
A program may use at most 192 MiB of HBM per device.

v0:
```python
import jax
import jax.numpy as jnp
from jax import lax
from jax.sharding import PartitionSpec as P

HEADS = 4
HEAD_DIM = 32


big_negative = 1000000000.0


def layer_norm(values, norm_gain):
    widened = values.astype(jnp.float32)
    row_mean = jnp.mean(widened, axis=-1, keepdims=True)
    row_var = jnp.mean(jnp.square(widened - row_mean), axis=-1, keepdims=True)
    return ((widened - row_mean) * lax.rsqrt(row_var + 1e-05) * norm_gain).astype(jnp.bfloat16)


def project(normed, weight):
    flat = normed.reshape(-1, normed.shape[-1])
    result = jnp.dot(flat, weight, preferred_element_type=jnp.float32)
    return result.reshape(normed.shape[:-1] + (weight.shape[1],))


def split_heads(merged):
    return merged.astype(jnp.bfloat16).reshape(merged.shape[:-1] + (HEADS, HEAD_DIM))


def attend_block(query, keys, values, pair_bias, key_bias):
    score_scale = HEAD_DIM ** (-0.5)
    scores = jnp.einsum("jhd,khd->hjk", query, keys, preferred_element_type=jnp.float32)
    scores = scores * score_scale + pair_bias + key_bias
    attn_weights = jax.nn.softmax(scores, axis=-1)
    mixed = jnp.einsum(
        "hjk,khd->jhd", attn_weights, values.astype(jnp.float32), precision=lax.Precision.DEFAULT
    )
    return mixed.reshape(query.shape[0], HEADS * HEAD_DIM)


def gated_residual(residual, mixed, gate_logit, gate_bias, out_weight):
    gated = (mixed * jax.nn.sigmoid(gate_logit + gate_bias)).astype(jnp.bfloat16)
    return (residual.astype(jnp.float32) + project(gated, out_weight)).astype(jnp.bfloat16)


def projections(normed, weight, channels):
    projected = project(normed, weight)
    query = split_heads(projected[..., :channels])
    keys = split_heads(projected[..., channels : 2 * channels])
    values = split_heads(projected[..., 2 * channels : 3 * channels])
    return (query, keys, values, projected[..., 3 * channels :])


def local(
    pair_in,
    residue_mask,
    norm_start,
    proj_start,
    gate_bias_start,
    bias_w_start,
    out_w_start,
    norm_end,
    proj_end,
    gate_bias_end,
    bias_w_end,
    out_w_end,
    norm_trans,
    trans_in,
    trans_bias,
    trans_out,
):
    row_count, total_res, channels = pair_in.shape
    full_mask = lax.all_gather(residue_mask, ("gx", "gy"), axis=0, tiled=True)
    key_bias = (full_mask.astype(jnp.float32) - 1.0) * big_negative
    normed = layer_norm(pair_in, norm_start)
    query, keys, values, gate_logit = projections(normed, proj_start, channels)
    local_bias = project(normed, bias_w_start).astype(jnp.bfloat16)

    def start_block(portion):
        span = portion.shape[0]
        pair_bias = jnp.transpose(portion, (2, 0, 1)).astype(jnp.float32)
        query_part = lax.slice_in_dim(query, 0, span, axis=1)

        def per_row(operands):
            query_row, key_row, value_row = operands
            return attend_block(query_row, key_row, value_row, pair_bias, key_bias)

        return lax.map(per_row, (query_part, keys, values))

    mixed = start_block(lax.all_gather(local_bias, ("gx", "gy"), axis=0, tiled=True))
    after_start = gated_residual(pair_in, mixed, gate_logit, gate_bias_start, out_w_start)
    column_pair = lax.all_to_all(after_start, ("gx", "gy"), split_axis=1, concat_axis=0, tiled=True)
    normed = layer_norm(column_pair, norm_end)
    query, keys, values, gate_logit = projections(normed, proj_end, channels)
    local_bias = project(normed, bias_w_end).astype(jnp.bfloat16)
    key_cols = jnp.swapaxes(keys, 0, 1)
    value_cols = jnp.swapaxes(values, 0, 1)

    def end_block(portion):
        span = portion.shape[1]
        pair_bias = jnp.transpose(portion, (2, 1, 0)).astype(jnp.float32)
        query_part = jnp.swapaxes(lax.slice_in_dim(query, 0, span, axis=0), 0, 1)

        def per_column(operands):
            query_col, key_col, value_col = operands
            return attend_block(query_col, key_col, value_col, pair_bias, key_bias)

        return jnp.swapaxes(lax.map(per_column, (query_part, key_cols, value_cols)), 0, 1)

    mixed = end_block(lax.all_gather(local_bias, ("gx", "gy"), axis=1, tiled=True))
    after_end = gated_residual(column_pair, mixed, gate_logit, gate_bias_end, out_w_end)
    row_pair = lax.all_to_all(after_end, ("gx", "gy"), split_axis=0, concat_axis=1, tiled=True)
    normed = layer_norm(row_pair, norm_trans)
    hidden = jax.nn.relu(project(normed, trans_in) + trans_bias).astype(jnp.bfloat16)
    return (row_pair.astype(jnp.float32) + project(hidden, trans_out)).astype(jnp.bfloat16)


def solution(mesh):
    placed = (
        P(("gx", "gy"), None, None),
        P(("gx", "gy")),
        P(),
        P(),
        P(),
        P(),
        P(),
        P(),
        P(),
        P(),
        P(),
        P(),
        P(),
        P(),
        P(),
        P(),
    )
    return jax.shard_map(
        local, mesh=mesh, in_specs=placed, out_specs=P(("gx", "gy"), None, None), check_vma=False
    )
```

profile of v0, /device:TPU:12, one launch (start us, length us, event | category | flops | bytes accessed | tf_op | source)
XLA Modules:
  0.0 1319.3 jit_solution(4363286661396572859)
XLA Ops:
  16.5 65.9 %all-reduce = s32[1024]{0:T(1024)S(1)} all-reduce(s32[1024]{0:T(1024)S(1)} %dynamic-update-slice), channel_id=1, replica_groups=mesh['gx'=16,'gy'=8] {'gx','gy'}, use_global_device_ids=true, to_apply=%add | all-reduce | flops 1024 | bytes 8192
  92.4 242.6 %all-gather.3.cloned.1.call-done = bf16[1024,1024,4]{1,2,0:T(4,128)(2,1)} async-done(((bf16[8,1024,4]{1,2,0:T(4,128)(2,1)}), bf16[1024,1024,4]{1,2,0:T(4,128)(2,1)}) %all-gather.3.cloned.1.call-update) | async-done | bytes 8388624 | tf_op jit(solution)/shard_map/all_gather | solution.py:90
  335.1 10.2 convert_bitcast_fusion.1
  345.2 19.2 %copy.60 = f32[4,1024,1024]{1,2,0:T(8,128)} copy(f32[4,1024,1024]{2,0,1:T(4,128)} %convert_bitcast_fusion.1) | data formatting | bytes 33554432 | tf_op jit(solution)/shard_map/while | solution.py:88
  367.1 248.7 %while.20 = (s32[]{:T(128)}, f32[8,1024,128]{1,2,0:T(8,128)}, bf16[8,1024,4,32]{1,3,2,0:T(8,128)(2,1)}, bf16[8,1024,4,32]{1,3,2,0:T(8,128)(2,1)}, bf16[8,1024,4,...) while((s32[]{:T(128)}, f32[8,1024,128]{1,2,0:T(8,128)}, ...), condition=%wide.region_5.6_spmd, body=%wide.region_2.5_spmd.sunk | while | flops 570417152 | bytes 69556312 | solution.py:88
  367.1 15.1 %fusion.109 = (f32[4,1024]{1,0:T(4,128)S(1)}, f32[4,1024,1024]{1,2,0:T(8,128)}) fusion(f32[1024]{0:T(1024)S(1)} %get-tuple-element.271, f32[4,1024,1024]{1,2,0:T(8,128)} %get-tuple-element.270, bf16[8,1024,4,32]{1,3,2,0:T(8,128)(2,1)} %get-tuple-element.269, s32[]{:T(128)} %get-tuple-element.257, bf16[8,1024,4,32]{1,3,2,0:T(8,128)(2,1)} %get-tuple-element.268), kind=kOutput, calls=%fused_computation.109.clone.1 | convolution fusion | flops 285208576 | bytes 34100224 | tf_op jit(solution)/shard_map/while/body/eval_jaxpr/jhd,khd->hjk/dot_general | solution.py:32
  382.1 8.0 fusion.110
  398.2 15.0 %fusion.109 = (f32[4,1024]{1,0:T(4,128)S(1)}, f32[4,1024,1024]{1,2,0:T(8,128)}) fusion(f32[1024]{0:T(1024)S(1)} %get-tuple-element.271, f32[4,1024,1024]{1,2,0:T(8,128)} %get-tuple-element.270, bf16[8,1024,4,32]{1,3,2,0:T(8,128)(2,1)} %get-tuple-element.269, s32[]{:T(128)} %get-tuple-element.257, bf16[8,1024,4,32]{1,3,2,0:T(8,128)(2,1)} %get-tuple-element.268), kind=kOutput, calls=%fused_computation.109.clone.1 | convolution fusion | flops 285208576 | bytes 34100224 | tf_op jit(solution)/shard_map/while/body/eval_jaxpr/jhd,khd->hjk/dot_general | solution.py:32
  413.2 8.0 fusion.110
  429.3 15.0 %fusion.109 = (f32[4,1024]{1,0:T(4,128)S(1)}, f32[4,1024,1024]{1,2,0:T(8,128)}) fusion(f32[1024]{0:T(1024)S(1)} %get-tuple-element.271, f32[4,1024,1024]{1,2,0:T(8,128)} %get-tuple-element.270, bf16[8,1024,4,32]{1,3,2,0:T(8,128)(2,1)} %get-tuple-element.269, s32[]{:T(128)} %get-tuple-element.257, bf16[8,1024,4,32]{1,3,2,0:T(8,128)(2,1)} %get-tuple-element.268), kind=kOutput, calls=%fused_computation.109.clone.1 | convolution fusion | flops 285208576 | bytes 34100224 | tf_op jit(solution)/shard_map/while/body/eval_jaxpr/jhd,khd->hjk/dot_general | solution.py:32
  444.2 8.0 fusion.110
  460.3 15.0 %fusion.109 = (f32[4,1024]{1,0:T(4,128)S(1)}, f32[4,1024,1024]{1,2,0:T(8,128)}) fusion(f32[1024]{0:T(1024)S(1)} %get-tuple-element.271, f32[4,1024,1024]{1,2,0:T(8,128)} %get-tuple-element.270, bf16[8,1024,4,32]{1,3,2,0:T(8,128)(2,1)} %get-tuple-element.269, s32[]{:T(128)} %get-tuple-element.257, bf16[8,1024,4,32]{1,3,2,0:T(8,128)(2,1)} %get-tuple-element.268), kind=kOutput, calls=%fused_computation.109.clone.1 | convolution fusion | flops 285208576 | bytes 34100224 | tf_op jit(solution)/shard_map/while/body/eval_jaxpr/jhd,khd->hjk/dot_general | solution.py:32
  491.4 15.0 %fusion.109 = (f32[4,1024]{1,0:T(4,128)S(1)}, f32[4,1024,1024]{1,2,0:T(8,128)}) fusion(f32[1024]{0:T(1024)S(1)} %get-tuple-element.271, f32[4,1024,1024]{1,2,0:T(8,128)} %get-tuple-element.270, bf16[8,1024,4,32]{1,3,2,0:T(8,128)(2,1)} %get-tuple-element.269, s32[]{:T(128)} %get-tuple-element.257, bf16[8,1024,4,32]{1,3,2,0:T(8,128)(2,1)} %get-tuple-element.268), kind=kOutput, calls=%fused_computation.109.clone.1 | convolution fusion | flops 285208576 | bytes 34100224 | tf_op jit(solution)/shard_map/while/body/eval_jaxpr/jhd,khd->hjk/dot_general | solution.py:32
  522.4 15.0 %fusion.109 = (f32[4,1024]{1,0:T(4,128)S(1)}, f32[4,1024,1024]{1,2,0:T(8,128)}) fusion(f32[1024]{0:T(1024)S(1)} %get-tuple-element.271, f32[4,1024,1024]{1,2,0:T(8,128)} %get-tuple-element.270, bf16[8,1024,4,32]{1,3,2,0:T(8,128)(2,1)} %get-tuple-element.269, s32[]{:T(128)} %get-tuple-element.257, bf16[8,1024,4,32]{1,3,2,0:T(8,128)(2,1)} %get-tuple-element.268), kind=kOutput, calls=%fused_computation.109.clone.1 | convolution fusion | flops 285208576 | bytes 34100224 | tf_op jit(solution)/shard_map/while/body/eval_jaxpr/jhd,khd->hjk/dot_general | solution.py:32
  553.5 15.0 %fusion.109 = (f32[4,1024]{1,0:T(4,128)S(1)}, f32[4,1024,1024]{1,2,0:T(8,128)}) fusion(f32[1024]{0:T(1024)S(1)} %get-tuple-element.271, f32[4,1024,1024]{1,2,0:T(8,128)} %get-tuple-element.270, bf16[8,1024,4,32]{1,3,2,0:T(8,128)(2,1)} %get-tuple-element.269, s32[]{:T(128)} %get-tuple-element.257, bf16[8,1024,4,32]{1,3,2,0:T(8,128)(2,1)} %get-tuple-element.268), kind=kOutput, calls=%fused_computation.109.clone.1 | convolution fusion | flops 285208576 | bytes 34100224 | tf_op jit(solution)/shard_map/while/body/eval_jaxpr/jhd,khd->hjk/dot_general | solution.py:32
  584.5 15.0 %fusion.109 = (f32[4,1024]{1,0:T(4,128)S(1)}, f32[4,1024,1024]{1,2,0:T(8,128)}) fusion(f32[1024]{0:T(1024)S(1)} %get-tuple-element.271, f32[4,1024,1024]{1,2,0:T(8,128)} %get-tuple-element.270, bf16[8,1024,4,32]{1,3,2,0:T(8,128)(2,1)} %get-tuple-element.269, s32[]{:T(128)} %get-tuple-element.257, bf16[8,1024,4,32]{1,3,2,0:T(8,128)(2,1)} %get-tuple-element.268), kind=kOutput, calls=%fused_computation.109.clone.1 | convolution fusion | flops 285208576 | bytes 34100224 | tf_op jit(solution)/shard_map/while/body/eval_jaxpr/jhd,khd->hjk/dot_general | solution.py:32
  622.4 41.8 %all_to_all.8 = bf16[8,1024,128]{2,0,1:T(8,128)(2,1)S(1)} all-to-all(bf16[8,1024,128]{2,0,1:T(8,128)(2,1)S(1)} %copy.62), channel_id=1, replica_groups=mesh['gx'=16,'gy'=8] {'gx','gy'}, dimensions={1} | all-to-all | bytes 4194304 | tf_op jit(solution)/shard_map/all_to_all | solution.py:92
  681.2 8.9 fusion.96
  692.8 302.2 %all-gather.5.cloned.1.call-done = bf16[1024,1024,4]{0,2,1:T(4,128)(2,1)} async-done(((bf16[1024,8,4]{0,2,1:T(4,128)(2,1)}), bf16[1024,1024,4]{0,2,1:T(4,128)(2,1)}) %all-gather.5.cloned.1.call-update) | async-done | bytes 8388624 | tf_op jit(solution)/shard_map/all_gather | solution.py:110
  994.9 10.2 convert_bitcast_fusion
  1005.1 19.2 %copy.71 = f32[4,1024,1024]{1,2,0:T(8,128)} copy(f32[4,1024,1024]{2,0,1:T(4,128)} %convert_bitcast_fusion) | data formatting | bytes 33554432 | tf_op jit(solution)/shard_map/while | solution.py:108
  1026.9 217.3 %while.21 = (s32[]{:T(128)}, f32[8,1024,128]{1,2,0:T(8,128)}, bf16[8,1024,4,32]{1,3,2,0:T(8,128)(2,1)}, bf16[8,1024,4,32]{1,3,2,0:T(8,128)(2,1)}, bf16[8,1024,4,...) while((s32[]{:T(128)}, f32[8,1024,128]{1,2,0:T(8,128)}, ...), condition=%wide.region_11.12_spmd, body=%wide.region_8.11_spmd.sunk | while | flops 570417152 | bytes 69556312 | solution.py:108
  1027.1 11.1 fusion.114
  1054.2 11.1 fusion.114
  1081.4 11.1 fusion.114
  1108.5 11.1 fusion.114
  1135.6 11.1 fusion.114
  1162.8 11.1 fusion.114
  1189.9 11.1 fusion.114
  1217.0 11.1 fusion.114
  1252.1 38.8 %all_to_all.9 = bf16[1024,8,128]{2,1,0:T(8,128)(2,1)S(1)} all-to-all(bf16[1024,8,128]{2,1,0:T(8,128)(2,1)S(1)} %copy.73), channel_id=1, replica_groups=mesh['gx'=16,'gy'=8] {'gx','gy'}, dimensions={0} | all-to-all | bytes 4194304 | tf_op jit(solution)/shard_map/all_to_all | solution.py:112
  1303.1 9.1 fusion.45
  (131 shorter events, 304.5 us)
Async XLA Ops:
  6.5 75.9 %copy-start = (bf16[128,512]{1,0:T(8,128)(2,1)S(1)}, bf16[128,512]{1,0:T(8,128)(2,1)}, u32[]{:S(2)}) copy-start(bf16[128,512]{1,0:T(8,128)(2,1)} %param.23) | copy-start | bytes 393220
  6.5 6.1 copy-start.4
  6.5 6.1 copy-start.7
  6.5 6.1 copy-start.14
  6.5 9.7 copy-start.16
  6.5 328.5 %all-gather.3.cloned.1.call-start = ((), (), s32[]{:S(2)}) async-start(), calls=%async_computation.2 | async-start | bytes 8454144 | tf_op jit(solution)/shard_map/all_gather | solution.py:90
  16.2 978.8 %all-gather.5.cloned.1.call-start = ((), (), s32[]{:S(2)}) async-start(), calls=%async_computation.3 | async-start | bytes 8454144 | tf_op jit(solution)/shard_map/all_gather | solution.py:110
  367.1 248.7 %copy-start.5 = (bf16[8,1024,128]{2,1,0:T(8,128)(2,1)S(1)}, bf16[8,1024,128]{2,1,0:T(8,128)(2,1)}, u32[]{:S(2)}) copy-start(bf16[8,1024,128]{2,1,0:T(8,128)(2,1)} %param.20) | copy-start | bytes 6291460
  367.1 248.7 %copy-start.11 = (bf16[128,128]{1,0:T(8,128)(2,1)S(1)}, bf16[128,128]{1,0:T(8,128)(2,1)}, u32[]{:S(2)}) copy-start(bf16[128,128]{1,0:T(8,128)(2,1)} %param.26) | copy-start | bytes 98308
  367.1 248.7 %copy-start.17 = (f32[128]{0:T(128)S(1)}, f32[128]{0:T(128)}, u32[]{:S(2)}) copy-start(f32[128]{0:T(128)} %param.24) | copy-start | bytes 1540
  666.8 1.9 copy-start.2
  670.1 6.3 copy-start.8
  670.1 6.3 copy-start.15
  675.4 5.8 copy-start.6
  1026.9 217.3 %copy-start.12 = (bf16[128,128]{1,0:T(8,128)(2,1)S(1)}, bf16[128,128]{1,0:T(8,128)(2,1)}, u32[]{:S(2)}) copy-start(bf16[128,128]{1,0:T(8,128)(2,1)} %param.31) | copy-start | bytes 98308
  1026.9 217.3 %copy-start.18 = (f32[128]{0:T(128)S(1)}, f32[128]{0:T(128)}, u32[]{:S(2)}) copy-start(f32[128]{0:T(128)} %param.29) | copy-start | bytes 1540
  1293.4 2.0 copy-start.3
  1296.7 6.3 copy-start.9
  1296.7 6.3 copy-start.10
  1296.8 6.3 copy-start.13
  1296.8 6.3 copy-start.19
  1303.1 9.1 copy-start.1
Sparse Core Ops, SparseCore 0:
  16.3 318.7 all-gather.2
  681.3 313.6 all-gather.4
where the time goes:
time: 1330 us; the launch traced here: 1320 us
  waiting for transfers between devices  545 us (41%)
  matrix products  369 us (28%)
  other arithmetic  171 us (13%)
  blocking collectives  146 us (11%)
  local copies, waits for them, and re-layouts  72.7 us (5%)
  between operations  14 us (1%)
    all_gather x1, waiting for transfers between devices, local(): lax.all_gather(local_bias, ('gx', 'gy'), axis=1, tiled=True)  302 us
    all_gather x1, waiting for transfers between devices, local(): lax.all_gather(local_bias, ('gx', 'gy'), axis=0, tiled=True)  243 us
    dot_general x16, matrix products, attend_block(): jnp.einsum('jhd,khd->hjk', query, keys, preferred_element_type=jnp.float32)  208 us
    reduce_sum x16, other arithmetic, attend_block(): attn_weights = jax.nn.softmax(scores, axis=-1)  128 us
    dot_general x16, matrix products, attend_block(): jnp.einsum('hjk,khd->jhd', attn_weights, values.astype(jnp.float32), prec...  116 us
    unnamed x1, blocking collectives  65.9 us
    dot_general x7, matrix products, project(): result = jnp.dot(flat, weight, preferred_element_type=jnp.float32)  45.1 us
    all_to_all x1, blocking collectives, local(): lax.all_to_all(after_start, ('gx', 'gy'), split_axis=1, concat_axis=0, ti...  41.8 us
  transfers between devices with their start and end apart: 2, of which 2 were waited for; matrix products, arithmetic and copies ran while one was open for 2% of the time, Pallas kernels for 0%

commit v1 on v0

v1 whole, which is shorter than its diff:
```python
import jax
import jax.numpy as jnp
from jax import lax
from jax.experimental import pallas as pl
from jax.experimental.pallas import tpu as pltpu
from jax.sharding import PartitionSpec as P

F32 = jnp.float32
BF = jnp.bfloat16
AX = ("gx", "gy")
HEADS = 4
HEAD_DIM = 32
LOG2E = 1.4426950408889634
LN2 = 0.6931471805599453
big_negative = 1000000000.0


def attn_body(q_ref, k_ref, vt_ref, b_ref, mask_ref, o_ref, den_ref, qs, eye, ps, *accs):
    h = pl.program_id(1)
    NS = 6
    sacc = [accs[m * (NS + 4): m * (NS + 4) + NS] for m in range(2)]
    oacc = [accs[m * (NS + 4) + NS: (m + 1) * (NS + 4)] for m in range(2)]
    qp = pl.program_id(0)
    lane = lax.broadcasted_iota(jnp.int32, (16, 128), 1) // 32
    masks = [jnp.where(lane == lax.rem(h + r, 4), 1.0, 0.0).astype(BF)[0:1] for r in range(4)]
    rowi = lax.broadcasted_iota(jnp.int32, (128, 128), 0)
    coli = lax.broadcasted_iota(jnp.int32, (128, 128), 1)
    eye[...] = jnp.where(rowi == coli, 1.0, 0.0).astype(BF)
    qrow = pl.multiple_of(qp * 512, 512)
    G = 2
    for g in range(G):
        for m in range(2):
            s = None
            for r in range(4):
                t = q_ref[4 * g + r, pl.ds(qrow + m * 256, 256), :] * masks[r]
                s = t if s is None else s + t
            qs[g, m * 256:(m + 1) * 256, :] = s

    pend = []
    LAG = 4
    unit = [0]
    def pop_one():
        (g, kt, r, sl) = pend.pop(0)
        for m in range(2):
            s = pltpu.matmul_pop(sacc[m][sl])
            p = jnp.exp2(s.astype(BF))
            ps[m, r, (g * 4 + kt // 2) % 2, (kt % 2) * 128:(kt % 2) * 128 + 128, :] = p
    def push_qb(g, kt):
        for m in range(2):
            rhs = jnp.concatenate([qs[g, m * 256:(m + 1) * 256, :], b_ref[0, kt, m * 256:(m + 1) * 256, :]], axis=1)
            pltpu.matmul_push_rhs(rhs, 0, m, transpose=True)
    def push_p(g, kp, r):
        for m in range(2):
            pltpu.matmul_push_rhs(ps[m, r, (g * 4 + kp) % 2], 1, m)
    def pv(g, kp, r):
        i = 4 * g + r
        lhs = vt_ref[i, 0, :, kp * 256:(kp + 1) * 256] * mask_ref[0:1, kp * 256:(kp + 1) * 256]
        for m in range(2):
            pltpu.matmul_acc_lhs(oacc[m][r], lhs, 1)
    def out(g, r):
        i = 4 * g + r
        for m in range(2):
            o = pltpu.matmul_pop(oacc[m][r])
            d = o[32:33, :]
            o_ref[i, :, m * 256:(m + 1) * 256] = o[0:32, :] * (1.0 / d)
            den_ref[0, i:i + 1, m * 256:(m + 1) * 256] = d
    pvq = []
    push_qb(0, 0)
    steps = [(g, kt) for g in range(G) for kt in range(8)]
    staged = None
    for n, (g, kt) in enumerate(steps):
        for r in range(4):
            i = 4 * g + r
            lhs = jnp.concatenate([k_ref[i, kt * 128:(kt + 1) * 128, :] * masks[r], eye[...]], axis=1)
            sl = unit[0] % NS
            unit[0] += 1
            for m in range(2):
                pltpu.matmul_acc_lhs(sacc[m][sl], lhs, 0 if r == 0 else None)
            if r == 0 and n + 1 < len(steps):
                push_qb(*steps[n + 1])
            pend.append((g, kt, r, sl))
            if len(pend) > LAG:
                pop_one()
            if r == 1 and pvq and staged is None:
                staged = pvq.pop(0)
                push_p(*staged)
        if staged is not None:
            done = staged
            pv(*staged); staged = None
            if pvq:
                staged = pvq.pop(0); push_p(*staged); pv(*staged); last = staged; staged = None
            else:
                last = done
            for (gg, kp, r) in ([done] if last is done else [done, last]):
                if kp == 3:
                    out(gg, r)
        if kt % 2 == 1:
            pvq += [(g, kt // 2, r) for r in range(4)]
    while pend:
        pop_one()
    while pvq:
        w = pvq.pop(0); push_p(*w); pv(*w)
        if w[1] == 3: out(w[0], w[2])

def attn_kernel(q_ref, k_ref, vt_ref, b_ref, mask_ref, o_ref, den_ref, qs, eye, ps):
    specs = []
    for m in range(2):
        specs += [pltpu.ACC(m)((128, 256), F32)] * 6 + [pltpu.ACC(m)((48, 256), F32)] * 4
    pl.run_scoped(lambda *accs: attn_body(q_ref, k_ref, vt_ref, b_ref, mask_ref, o_ref, den_ref, qs, eye, ps, *accs), *specs)

def attention(q, k, vt, b, mask16):
    return pl.pallas_call(
        attn_kernel,
        grid=(2, 4),
        in_specs=[
            pl.BlockSpec((8, 1024, 128), lambda a, h: (0, 0, 0)),
            pl.BlockSpec((8, 1024, 128), lambda a, h: (0, 0, 0)),
            pl.BlockSpec((8, 1, 48, 1024), lambda a, h: (0, h, 0, 0)),
            pl.BlockSpec((1, 8, 512, 128), lambda a, h: (h, 0, a, 0)),
            pl.BlockSpec((16, 1024), lambda a, h: (0, 0)),
        ],
        out_specs=[
            pl.BlockSpec((8, 32, 512), lambda a, h: (0, h, a)),
            pl.BlockSpec((1, 8, 512), lambda a, h: (h, 0, a)),
        ],
        out_shape=[jax.ShapeDtypeStruct((8, 128, 1024), F32), jax.ShapeDtypeStruct((4, 8, 1024), F32)],
        scratch_shapes=[pltpu.VMEM((2, 512, 128), BF), pltpu.VMEM((128, 128), BF), pltpu.VMEM((2, 4, 2, 256, 256), BF)],
        compiler_params=pltpu.CompilerParams(vmem_limit_bytes=60 * 2**20),
        name="tri_attn",
    )(q, k, vt, b, mask16)


def layer_norm(x, gain):
    mean = jnp.mean(x, axis=-1, keepdims=True)
    c = x - mean
    var = jnp.mean(c * c, axis=-1, keepdims=True)
    return (c * lax.rsqrt(var + 1e-05) * gain).astype(BF)


def pre_kernel(z_ref, gain_ref, wqk_ref, wvg_ref, bw_ref, gb_ref, q_ref, k_ref, vt_ref, gate_ref, b_ref, m_ref, scr):
    i = pl.program_id(0)
    a = layer_norm(z_ref[0].astype(F32), gain_ref[...])
    qk = jnp.dot(a, wqk_ref[0], preferred_element_type=F32)
    q_ref[0] = (qk[:, :128] * (HEAD_DIM ** -0.5 * LOG2E)).astype(BF)
    k_ref[0] = qk[:, 128:].astype(BF)
    vg = jnp.dot(a, wvg_ref[...], preferred_element_type=F32)
    vt = jnp.transpose(vg[:, :128].astype(BF))
    tail = jnp.where(lax.broadcasted_iota(jnp.int32, (16, 1024), 0) == 0, 1.0, 0.0).astype(BF)
    for h in range(4):
        vt_ref[0, h, 0:32, :] = vt[32 * h:32 * h + 32, :]
        vt_ref[0, h, 32:48, :] = tail
    gate_ref[0] = jax.nn.sigmoid(vg[:, 128:] + gb_ref[...]).astype(BF)
    b = lax.dot_general(bw_ref[...], a, (((1,), (1,)), ((), ())), preferred_element_type=F32)
    b = b.astype(BF).astype(F32)
    m = jnp.max(b, axis=-1, keepdims=True)
    b = (b - m) * LOG2E
    for h in range(4):
        for kt in range(8):
            scr[h, kt, pl.ds(i, 1), :] = b[h:h + 1, kt * 128:(kt + 1) * 128]
    m_ref[0] = jnp.broadcast_to(m, (16, 128))

    @pl.when(i == 7)
    def _():
        b_ref[...] = scr[...].astype(BF)


def pre(z, gain, proj, bias_w, gate_bias):
    wq, wk, wv, wg = [proj[:, 128 * n:128 * n + 128] for n in range(4)]

    def slots(w, i):
        return jnp.concatenate([w[:, 32 * ((s - i) % 4):32 * ((s - i) % 4) + 32] for s in range(4)], axis=1)

    wqk = jnp.stack([jnp.concatenate([slots(wq, i), slots(wk, i)], axis=1) for i in range(4)])
    wvg = jnp.concatenate([wv, wg], axis=1)
    bwt = jnp.pad(jnp.transpose(bias_w), ((0, 12), (0, 0)))
    row = lambda i: (i, 0, 0)
    return pl.pallas_call(
        pre_kernel,
        grid=(8,),
        in_specs=[
            pl.BlockSpec((1, 1024, 128), row),
            pl.BlockSpec((1, 128), lambda i: (0, 0)),
            pl.BlockSpec((1, 128, 256), lambda i: (lax.rem(i, 4), 0, 0)),
            pl.BlockSpec((128, 256), lambda i: (0, 0)),
            pl.BlockSpec((16, 128), lambda i: (0, 0)),
            pl.BlockSpec((1, 128), lambda i: (0, 0)),
        ],
        out_specs=[
            pl.BlockSpec((1, 1024, 128), row),
            pl.BlockSpec((1, 1024, 128), row),
            pl.BlockSpec((1, 4, 48, 1024), lambda i: (i, 0, 0, 0)),
            pl.BlockSpec((1, 1024, 128), row),
            pl.BlockSpec((4, 8, 8, 128), lambda i: (0, 0, 0, 0)),
            pl.BlockSpec((1, 16, 128), row),
        ],
        out_shape=[
            jax.ShapeDtypeStruct((8, 1024, 128), BF),
            jax.ShapeDtypeStruct((8, 1024, 128), BF),
            jax.ShapeDtypeStruct((8, 4, 48, 1024), BF),
            jax.ShapeDtypeStruct((8, 1024, 128), BF),
            jax.ShapeDtypeStruct((4, 8, 8, 128), BF),
            jax.ShapeDtypeStruct((8, 16, 128), F32),
        ],
        scratch_shapes=[pltpu.VMEM((4, 8, 8, 128), F32)],
        compiler_params=pltpu.CompilerParams(vmem_limit_bytes=48 * 2**20),
        name="tri_pre",
    )(z, gain.reshape(1, 128), wqk, wvg, bwt, gate_bias.reshape(1, 128))


def post_kernel(o_ref, gate_ref, z_ref, w_ref, out_ref, scr):
    parts = []
    for i in range(8):
        o = jnp.transpose(o_ref[i])
        parts.append((o * gate_ref[i].astype(F32)).astype(BF))
    y = jnp.dot(jnp.concatenate(parts, axis=0), w_ref[...], preferred_element_type=F32)
    for i in range(8):
        scr[pl.ds(i, 128, stride=8), :] = z_ref[i].astype(F32) + y[128 * i:128 * i + 128]
    out_ref[...] = scr[...].astype(BF)


def post(o, gate, z, w):
    tile = lambda t: (0, t, 0)
    return pl.pallas_call(
        post_kernel,
        grid=(8,),
        in_specs=[
            pl.BlockSpec((8, 128, 128), lambda t: (0, 0, t)),
            pl.BlockSpec((8, 128, 128), tile),
            pl.BlockSpec((8, 128, 128), tile),
            pl.BlockSpec((128, 128), lambda t: (0, 0)),
        ],
        out_specs=pl.BlockSpec((1024, 128), lambda t: (t, 0)),
        out_shape=jax.ShapeDtypeStruct((8192, 128), BF),
        scratch_shapes=[pltpu.VMEM((1024, 128), F32)],
        compiler_params=pltpu.CompilerParams(vmem_limit_bytes=48 * 2**20),
        name="tri_post",
    )(o, gate, z, w)


def trans_kernel(z_ref, gain_ref, w1_ref, b1_ref, w2_ref, out_ref):
    z = z_ref[0].astype(F32)
    a = layer_norm(z, gain_ref[...])
    hid = jax.nn.relu(jnp.dot(a, w1_ref[...], preferred_element_type=F32) + b1_ref[...]).astype(BF)
    out_ref[0] = (z + jnp.dot(hid, w2_ref[...], preferred_element_type=F32)).astype(BF)


def trans(z, gain, w1, b1, w2):
    row = lambda i: (i, 0, 0)
    whole = lambda i: (0, 0)
    return pl.pallas_call(
        trans_kernel,
        grid=(8,),
        in_specs=[
            pl.BlockSpec((1, 1024, 128), row),
            pl.BlockSpec((1, 128), whole),
            pl.BlockSpec((128, 512), whole),
            pl.BlockSpec((1, 512), whole),
            pl.BlockSpec((512, 128), whole),
        ],
        out_specs=pl.BlockSpec((1, 1024, 128), row),
        out_shape=jax.ShapeDtypeStruct((8, 1024, 128), BF),
        compiler_params=pltpu.CompilerParams(vmem_limit_bytes=48 * 2**20),
        name="tri_trans",
    )(z, gain.reshape(1, 128), w1, b1.reshape(1, 512), w2)


def exact_attention(q, k, vt, b, maxima, mask):
    key_bias = (mask - 1.0) * big_negative
    heads = [jnp.array([(h + i) % 4 for h in range(4)]) for i in range(4)]

    def per_row(operands):
        i, q_row, k_row, vt_row = operands
        order = jnp.stack(heads)[lax.rem(i, 4)]
        qh = q_row.reshape(1024, 4, 32)[:, order]
        kh = k_row.reshape(1024, 4, 32)[:, order]

        def per_head(ops):
            qx, kx, vx, bx, mx = ops
            s = jnp.dot(qx, kx.T, preferred_element_type=F32)
            bias = jnp.swapaxes(bx, 0, 1).reshape(1024, 1024).astype(F32)
            s = (s + bias) * LN2 + mx[:, None] + key_bias
            w = jax.nn.softmax(s, axis=-1)
            return jnp.dot(vx[:32].astype(F32), w.T, preferred_element_type=F32)

        o = lax.map(per_head, (jnp.moveaxis(qh, 1, 0), jnp.moveaxis(kh, 1, 0), vt_row, b, maxima))
        return o.reshape(128, 1024)

    return lax.map(per_row, (jnp.arange(8), q, k, vt))


def gather_bias(piece, extra):
    block = jnp.concatenate([piece.reshape(256, 128), extra], axis=0)[None]
    full = lax.all_gather(lax.all_gather(block, "gy", axis=0, tiled=True), "gx", axis=0, tiled=True)
    b = full[:, :256].reshape(128, 4, 8, 8, 128)
    b = jnp.transpose(b, (1, 2, 0, 3, 4)).reshape(4, 8, 1024, 128)
    return b, full[:, 256:]


def swap(z):
    z = z.reshape(128, 8, 8, 128)
    z = lax.all_to_all(z, AX, split_axis=0, concat_axis=0, tiled=True)
    return jnp.swapaxes(z, 0, 1).reshape(8, 1024, 128)


def phase(z, mask_local, gain, proj, gate_bias, bias_w, out_w):
    q, k, vt, gate, piece, m = pre(z, gain, proj, bias_w, gate_bias)
    maxima = jnp.transpose(m[:, :4, 0]).reshape(1, 32)
    extra = jnp.zeros((8, 128), F32)
    extra = extra.at[0:1, 0:8].set(mask_local.astype(F32).reshape(1, 8)).at[1:2, 0:32].set(maxima).astype(BF)
    b, extras = gather_bias(piece, extra)
    mask = extras[:, 0, :8].reshape(1, 1024)
    o, den = attention(q, k, vt, b, jnp.broadcast_to(mask, (16, 1024)))
    fine = jnp.all((den > 2.0 ** -60) & (den < 2.0 ** 100))
    maxima = jnp.transpose(extras[:, 1, :32].reshape(128, 4, 8), (1, 0, 2)).reshape(4, 1024).astype(F32)
    o = lax.cond(
        fine,
        lambda: o,
        lambda: exact_attention(q, k, vt, b, maxima, mask.reshape(1024).astype(F32)),
    )
    return post(o, gate, z, out_w)


def local(
    pair_in,
    residue_mask,
    norm_start,
    proj_start,
    gate_bias_start,
    bias_w_start,
    out_w_start,
    norm_end,
    proj_end,
    gate_bias_end,
    bias_w_end,
    out_w_end,
    norm_trans,
    trans_in,
    trans_bias,
    trans_out,
):
    z = phase(pair_in, residue_mask, norm_start, proj_start, gate_bias_start, bias_w_start, out_w_start)
    z = swap(z)
    z = phase(z, residue_mask, norm_end, proj_end, gate_bias_end, bias_w_end, out_w_end)
    z = swap(z)
    return trans(z, norm_trans, trans_in, trans_bias, trans_out)


def solution(mesh):
    rows = P(AX, None, None)
    placed = (rows, P(AX)) + (P(),) * 14

    def whole(*args):
        with jax.sharding.use_abstract_mesh(mesh.abstract_mesh):
            return jax.shard_map(local, mesh=mesh, in_specs=placed, out_specs=rows, check_vma=False)(*args)

    return whole
```

time: 1330 us -> 462 us (0.35)
  waiting for transfers between devices: 545 us -> 137 us
  matrix products: 369 us -> 0 us
  other arithmetic: 171 us -> 3.78 us
  Pallas kernels: 0 us -> 130 us
  blocking collectives: 146 us -> 114 us
  local copies, waits for them, and re-layouts: 72.7 us -> 52.1 us
    all_gather x2, waiting for transfers between devices: 545 us -> 108 us  [gather_bias(): lax.all_gather(lax.all_gather(block, 'gy', axis=0, tiled=True), 'gx', axi...]
    dot_general x39 -> x0, matrix products: 369 us -> none  [the longest x16 208 us: attend_block(): jnp.einsum('jhd,khd->hjk', query, keys, preferred_element_type=jnp.float32)]
    reduce_sum x22 -> x0, other arithmetic: 146 us -> none  [the longest x16 128 us: attend_block(): attn_weights = jax.nn.softmax(scores, axis=-1)]
    pallas_call x0 -> x7, Pallas kernels: none -> 130 us  [the longest x2 86.6 us: attention(): pl.pallas_call(attn_kernel, grid=(2, 4), in_specs=[pl.BlockSpec((8, 1024,...]
    all_gather x0 -> x2, blocking collectives: none -> 72.8 us  [gather_bias(): lax.all_gather(block, 'gy', axis=0, tiled=True)]
    unnamed x1 -> x0, blocking collectives: 65.9 us -> none
    all_to_all x2 -> x1, blocking collectives: 80.5 us -> 40.8 us  [swap(): z = lax.all_to_all(z, AX, split_axis=0, concat_axis=0, tiled=True)]
    while x2 -> x0, local copies, waits for them, and re-layouts: 38.5 us -> none  [the longest x1 19.2 us: end_block(): lax.map(per_column, (query_part, key_cols, value_cols))]
  transfers between devices with their start and end apart: 2 -> 3, of which waited for: 2 -> 3; matrix products, arithmetic and copies ran while one was open for 2% -> 0% of each run, Pallas kernels for 0% -> 0%
where the time goes in v1:
time: 462 us; the launch traced here: 461 us
  waiting for transfers between devices  137 us (30%)
  Pallas kernels  130 us (28%)
  blocking collectives  114 us (25%)
  local copies, waits for them, and re-layouts  52.1 us (11%)
  between operations  15.1 us (3%)
  starting transfers between devices  9.45 us (2%)
    all_gather x2, waiting for transfers between devices, gather_bias(): lax.all_gather(lax.all_gather(block, 'gy', axis=0, tiled=True), 'gx', axi...  108 us
    pallas_call x2, Pallas kernels, attention(): pl.pallas_call(attn_kernel, grid=(2, 4), in_specs=[pl.BlockSpec((8, 1024,...  86.6 us
    all_gather x2, blocking collectives, gather_bias(): lax.all_gather(block, 'gy', axis=0, tiled=True)  72.8 us
    all_to_all x1, blocking collectives, swap(): z = lax.all_to_all(z, AX, split_axis=0, concat_axis=0, tiled=True)  40.8 us
    all_to_all x1, waiting for transfers between devices, swap(): z = lax.all_to_all(z, AX, split_axis=0, concat_axis=0, tiled=True)  28.5 us
    pallas_call x2, Pallas kernels, pre(): pl.pallas_call(pre_kernel, grid=(8,), in_specs=[pl.BlockSpec((1, 1024, 12...  18.8 us
    reshape x2, local copies, waits for them, and re-layouts, gather_bias(): b = full[:, :256].reshape(128, 4, 8, 8, 128)  17.7 us
    slice x2, local copies, waits for them, and re-layouts, gather_bias(): b = full[:, :256].reshape(128, 4, 8, 8, 128)  15.6 us
  transfers between devices with their start and end apart: 3, of which 3 were waited for; matrix products, arithmetic and copies ran while one was open for 0% of the time, Pallas kernels for 0%

profile of v1, /device:TPU:12, one launch (start us, length us, event | category | flops | bytes accessed | tf_op | source)
XLA Modules:
  0.0 460.8 jit_solution(701963857676269567)
XLA Ops:
  6.5 0.9 fusion.53
  7.5 0.9 fusion.54
  8.4 0.9 fusion.55
  9.4 0.9 fusion.52
  10.3 0.7 pad.23.bw_ref
  11.3 1.6 copy-done.1
  14.2 9.4 %tri_pre.2 = (bf16[8,1024,128]{2,1,0:T(8,128)(2,1)}, bf16[8,1024,128]{2,1,0:T(8,128)(2,1)}, bf16[8,4,48,1024]{3,2,1,0:T(8,128)(2,1)}, bf16[8,1024,128]{2,1,0:T(8...) custom-call(bf16[8,1024,128]{2,1,0:T(8,128)(2,1)S(1)} %copy-done.1, ...), custom_call_target="tpu_custom_call" | custom-call | tf_op jit(solution)/shard_map/tri_pre/pallas_call | solution.py:177
  24.5 36.1 %all-gather = bf16[2112,128]{1,0:T(8,128)(2,1)} all-gather(bf16[264,128]{1,0:T(8,128)(2,1)S(1)} %pad_maximum_fusion.2), channel_id=2, replica_groups=mesh['gx'=16,'gy'=8] {'gy'}, dimensions={0}, use_global_device_ids=true | all-gather | bytes 608256 | tf_op jit(solution)/shard_map/all_gather | solution.py:293
  60.6 55.8 %all-gather.5.cloned.1.call-done = bf16[128,264,128]{2,1,0:T(8,128)(2,1)} async-done(((bf16[8,264,128]{2,1,0:T(8,128)(2,1)}), bf16[128,264,128]{2,1,0:T(8,128)(2,1)}) %all-gather.5.cloned.1.call-update) | async-done | bytes 8650768 | tf_op jit(solution)/shard_map/all_gather | solution.py:293
  116.4 7.8 %slice.318 = bf16[128,256,128]{2,1,0:T(8,128)(2,1)} slice(bf16[128,264,128]{2,1,0:T(8,128)(2,1)} %all-gather.5.cloned.1.call-done), slice={[0:128], [0:256], [0:128]} | slice | bytes 16777216 | tf_op jit(solution)/shard_map/slice | solution.py:294
  124.2 8.9 %copy.116 = bf16[128,4,8,8,128]{4,3,0,2,1:T(8,128)(2,1)} copy(bf16[128,4,8,8,128]{4,3,2,1,0:T(8,128)(2,1)} %bitcast.245) | data formatting | bytes 16777216 | tf_op jit(solution)/shard_map/reshape | solution.py:294
  133.1 1.0 slice.320
  134.2 1.2 fusion.47
  136.1 43.3 %tri_attn.2 = (f32[8,128,1024]{2,1,0:T(8,128)}, f32[4,8,1024]{2,1,0:T(8,128)}) custom-call(bf16[8,1024,128]{2,1,0:T(8,128)(2,1)} %get-tuple-element.501.q_ref, bf16[8,1024,128]{2,1,0:T(8,128)(2,1)} %get-tuple-element.502.k_ref, bf16[8,4,48,1024]{3,2,1,0:T(8,128)(2,1)} %get-tuple-element.503.vt_ref, bf16[4,8,1024,128]{3,2,1,0:T(8,128)(2,1)} %bitcast.243, ...), custom_call_target="tpu_custom_call" | custom-call | tf_op jit(solution)/shard_map/tri_attn/pallas_call | solution.py:112
  179.4 1.6 and_reduce_fusion.1
  183.0 7.7 %tri_post.2 = bf16[8192,128]{1,0:T(8,128)(2,1)} custom-call(f32[8,128,1024]{2,1,0:T(8,128)} %get-tuple-element.1179.o_ref, bf16[8,1024,128]{2,1,0:T(8,128)(2,1)S(1)} %get-tuple-element.508.gate_ref, bf16[8,1024,128]{2,1,0:T(8,128)(2,1)} %z_ref.3, bf16[128,128]{1,0:T(8,128)(2,1)S(1)} %copy-done.4), custom_call_target="tpu_custom_call" | custom-call | tf_op jit(solution)/shard_map/tri_post/pallas_call | solution.py:223
  190.6 9.4 %all-to-all-start = ((bf16[128,8,8,128]{3,2,1,0:T(8,128)(2,1)}), bf16[128,8,8,128]{3,2,1,0:T(8,128)(2,1)S(1)}, u32[]{:S(2)}, u32[]{:S(2)}) async-start(bf16[128,8,8,128]{3,2,1,0:T(8,128)(2,1)} %bitcast.56), calls=%async_computation | async-start | bytes 4194304 | tf_op jit(solution)/shard_map/all_to_all | solution.py:301
  200.8 28.5 %all-to-all-done = bf16[128,8,8,128]{3,2,1,0:T(8,128)(2,1)S(1)} async-done(((bf16[128,8,8,128]{3,2,1,0:T(8,128)(2,1)}), bf16[128,8,8,128]{3,2,1,0:T(8,128)(2,1)S(1)}, u32[]{:S(2)}, u32[]{:S(2)}) %all-to-all-start) | async-done | bytes 2097184 | tf_op jit(solution)/shard_map/all_to_all | solution.py:301
  229.7 9.5 %tri_pre.3 = (bf16[8,1024,128]{2,1,0:T(8,128)(2,1)}, bf16[8,1024,128]{2,1,0:T(8,128)(2,1)}, bf16[8,4,48,1024]{3,2,1,0:T(8,128)(2,1)}, bf16[8,1024,128]{2,1,0:T(8...) custom-call(bf16[8,1024,128]{2,1,0:T(8,128)(2,1)S(1)} %copy_bitcast_fusion.3.z_ref, ...), custom_call_target="tpu_custom_call" | custom-call | tf_op jit(solution)/shard_map/tri_pre/pallas_call | solution.py:177
  239.1 1.4 copy-done
  240.9 36.7 %all-gather.1 = bf16[2112,128]{1,0:T(8,128)(2,1)} all-gather(bf16[264,128]{1,0:T(8,128)(2,1)S(1)} %pad_maximum_fusion.3), channel_id=3, replica_groups=mesh['gx'=16,'gy'=8] {'gy'}, dimensions={0}, use_global_device_ids=true | all-gather | bytes 608256 | tf_op jit(solution)/shard_map/all_gather | solution.py:293
  277.5 52.3 %all-gather.7.cloned.1.call-done = bf16[128,264,128]{2,1,0:T(8,128)(2,1)} async-done(((bf16[8,264,128]{2,1,0:T(8,128)(2,1)}), bf16[128,264,128]{2,1,0:T(8,128)(2,1)}) %all-gather.7.cloned.1.call-update) | async-done | bytes 8650768 | tf_op jit(solution)/shard_map/all_gather | solution.py:293
  329.8 7.8 %slice.321 = bf16[128,256,128]{2,1,0:T(8,128)(2,1)} slice(bf16[128,264,128]{2,1,0:T(8,128)(2,1)} %all-gather.7.cloned.1.call-done), slice={[0:128], [0:256], [0:128]} | slice | bytes 16777216 | tf_op jit(solution)/shard_map/slice | solution.py:294
  337.6 8.9 %copy.115 = bf16[128,4,8,8,128]{4,3,0,2,1:T(8,128)(2,1)} copy(bf16[128,4,8,8,128]{4,3,2,1,0:T(8,128)(2,1)} %bitcast.246) | data formatting | bytes 16777216 | tf_op jit(solution)/shard_map/reshape | solution.py:294
  346.5 1.0 slice.323
  347.6 1.2 fusion.46
  349.5 43.3 %tri_attn.3 = (f32[8,128,1024]{2,1,0:T(8,128)}, f32[4,8,1024]{2,1,0:T(8,128)}) custom-call(bf16[8,1024,128]{2,1,0:T(8,128)(2,1)} %get-tuple-element.509.q_ref, bf16[8,1024,128]{2,1,0:T(8,128)(2,1)} %get-tuple-element.510.k_ref, bf16[8,4,48,1024]{3,2,1,0:T(8,128)(2,1)} %get-tuple-element.511.vt_ref, bf16[4,8,1024,128]{3,2,1,0:T(8,128)(2,1)} %bitcast.241, ...), custom_call_target="tpu_custom_call" | custom-call | tf_op jit(solution)/shard_map/tri_attn/pallas_call | solution.py:112
  392.8 1.6 and_reduce_fusion
  395.2 0.7 copy-done.5
  395.9 6.5 %tri_post.3 = bf16[8192,128]{1,0:T(8,128)(2,1)S(1)} custom-call(f32[8,128,1024]{2,1,0:T(8,128)} %get-tuple-element.1180.o_ref, bf16[8,1024,128]{2,1,0:T(8,128)(2,1)S(1)} %get-tuple-element.516.gate_ref, bf16[8,1024,128]{2,1,0:T(8,128)(2,1)} %copy-done, bf16[128,128]{1,0:T(8,128)(2,1)S(1)} %copy-done.5), custom_call_target="tpu_custom_call" | custom-call | tf_op jit(solution)/shard_map/tri_post/pallas_call | solution.py:223
  402.5 40.8 %all_to_all.10 = bf16[128,8,8,128]{3,2,1,0:T(8,128)(2,1)S(1)} all-to-all(bf16[128,8,8,128]{3,2,1,0:T(8,128)(2,1)S(1)} %bitcast.228), channel_id=1, replica_groups=mesh['gx'=16,'gy'=8] {'gx','gy'}, dimensions={0} | all-to-all | bytes 4194304 | tf_op jit(solution)/shard_map/all_to_all | solution.py:301
  443.7 10.3 %tri_trans.1 = bf16[8,1024,128]{2,1,0:T(8,128)(2,1)} custom-call(bf16[8,1024,128]{2,1,0:T(8,128)(2,1)S(1)} %copy_bitcast_fusion.2.z_ref, f32[1,128]{1,0:T(1,128)S(1)} %bitcast.236, bf16[128,512]{1,0:T(8,128)(2,1)S(1)} %copy-done.2, f32[1,512]{1,0:T(1,128)S(1)} %bitcast.231, bf16[512,128]{1,0:T(8,128)(2,1)S(1)} %copy-done.3), custom_call_target="tpu_custom_call" | custom-call | tf_op jit(solution)/shard_map/tri_trans/pallas_call | solution.py:250
  (80 shorter events, 7.2 us)
Async XLA Ops:
  6.5 17.2 %copy-start.21 = (s32[8]{0:T(128)S(1)}, s32[8]{0:T(128)}, u32[]{:S(2)}) copy-start(s32[8]{0:T(128)} %param.45) | copy-start | bytes 100
  6.5 109.9 %all-gather.5.cloned.1.call-start = ((), (), s32[]{:S(2)}) async-start(), calls=%async_computation.2 | async-start | bytes 9191424 | tf_op jit(solution)/shard_map/all_gather | solution.py:293
  11.3 1.6 copy-start.1
  12.8 0.7 copy-start.7
  13.5 0.7 copy-start.8
  136.1 46.1 %copy-start.14 = (s32[4]{0:T(128)S(1)}, s32[4]{0:T(128)}, u32[]{:S(2)}) copy-start(s32[4]{0:T(128)} %constant.233.clone) | copy-start | bytes 52
  136.1 46.1 %copy-start.16 = (s32[4]{0:T(128)S(1)}, s32[4]{0:T(128)}, u32[]{:S(2)}) copy-start(s32[4]{0:T(128)} %constant.234.clone) | copy-start | bytes 52
  136.1 46.1 %copy-start.18 = (s32[4]{0:T(128)S(1)}, s32[4]{0:T(128)}, u32[]{:S(2)}) copy-start(s32[4]{0:T(128)} %constant.235.clone) | copy-start | bytes 52
  182.2 0.8 copy-start.4
  190.6 9.5 %copy-start.20 = (bf16[128,4]{0,1:T(4,128)(2,1)S(1)}, bf16[128,4]{0,1:T(4,128)(2,1)}, u32[]{:S(2)}) copy-start(bf16[128,4]{0,1:T(4,128)(2,1)} %param.54) | copy-start | bytes 3076
  190.6 9.5 %copy-start.12 = (bf16[128,512]{1,0:T(8,128)(2,1)S(1)}, bf16[128,512]{1,0:T(8,128)(2,1)}, u32[]{:S(2)}) copy-start(bf16[128,512]{1,0:T(8,128)(2,1)} %param.52) | copy-start | bytes 393220
  190.6 38.6 %all-to-all-start = ((bf16[128,8,8,128]{3,2,1,0:T(8,128)(2,1)}), bf16[128,8,8,128]{3,2,1,0:T(8,128)(2,1)S(1)}, u32[]{:S(2)}, u32[]{:S(2)}) async-start(bf16[128,8,8,128]{3,2,1,0:T(8,128)(2,1)} %bitcast.56), calls=%async_computation | async-start | bytes 4194304 | tf_op jit(solution)/shard_map/all_to_all | solution.py:301
  200.1 29.6 %copy-start.9 = (f32[128]{0:T(128)S(1)}, f32[128]{0:T(128)}, u32[]{:S(2)}) copy-start(f32[128]{0:T(128)} %param.51) | copy-start | bytes 1540
  200.1 29.6 %copy-start.10 = (f32[128]{0:T(128)S(1)}, f32[128]{0:T(128)}, u32[]{:S(2)}) copy-start(f32[128]{0:T(128)} %param.53) | copy-start | bytes 1540
  200.1 129.8 %all-gather.7.cloned.1.call-start = ((), (), s32[]{:S(2)}) async-start(), calls=%async_computation.3 | async-start | bytes 9191424 | tf_op jit(solution)/shard_map/all_gather | solution.py:293
  200.4 40.4 %copy-start.13 = (bf16[8,128]{1,0:T(8,128)(2,1)S(1)}, bf16[8,128]{1,0:T(8,128)(2,1)}, u32[]{:S(2)}) copy-start(bf16[8,128]{1,0:T(8,128)(2,1)} %copy.156) | copy-start | bytes 6148
  239.1 1.4 copy-start
  349.5 45.6 %copy-start.15 = (s32[4]{0:T(128)S(1)}, s32[4]{0:T(128)}, u32[]{:S(2)}) copy-start(s32[4]{0:T(128)} %constant.233.clone) | copy-start | bytes 52
  349.5 45.6 %copy-start.17 = (s32[4]{0:T(128)S(1)}, s32[4]{0:T(128)}, u32[]{:S(2)}) copy-start(s32[4]{0:T(128)} %constant.234.clone) | copy-start | bytes 52
  349.5 45.7 %copy-start.19 = (s32[4]{0:T(128)S(1)}, s32[4]{0:T(128)}, u32[]{:S(2)}) copy-start(s32[4]{0:T(128)} %constant.235.clone) | copy-start | bytes 52
  395.2 0.8 copy-start.5
  402.4 41.3 %copy-start.2 = (bf16[128,512]{1,0:T(8,128)(2,1)S(1)}, bf16[128,512]{1,0:T(8,128)(2,1)}, u32[]{:S(2)}) copy-start(bf16[128,512]{1,0:T(8,128)(2,1)} %w1_ref.1) | copy-start | bytes 393220
  402.4 41.3 %copy-start.3 = (bf16[512,128]{1,0:T(8,128)(2,1)S(1)}, bf16[512,128]{1,0:T(8,128)(2,1)}, u32[]{:S(2)}) copy-start(bf16[512,128]{1,0:T(8,128)(2,1)} %w2_ref.1) | copy-start | bytes 393220
  402.4 41.3 %copy-start.6 = (f32[512]{0:T(512)S(1)}, f32[512]{0:T(512)}, u32[]{:S(2)}) copy-start(f32[512]{0:T(512)} %param.58) | copy-start | bytes 6148
  402.5 41.3 %copy-start.11 = (f32[128]{0:T(128)S(1)}, f32[128]{0:T(128)}, u32[]{:S(2)}) copy-start(f32[128]{0:T(128)} %param.56) | copy-start | bytes 1540
Sparse Core Ops, SparseCore 0:
  60.7 55.6 all-gather.4
  277.7 52.1 all-gather.6

commit v2 on v1

--- a/solution.py
+++ b/solution.py
@@ -15,8 +15,15 @@
 big_negative = 1000000000.0
 
 
-def attn_body(q_ref, k_ref, vt_ref, b_ref, mask_ref, o_ref, den_ref, qs, eye, ps, *accs):
+def attn_body(q_ref, k_ref, vt_ref, b_ref, extra_ref, o_ref, den_ref, qs, eye, ps, mask_ref, *accs):
     h = pl.program_id(1)
+
+    @pl.when((pl.program_id(0) == 0) & (h == 0))
+    def _():
+        placed = jnp.sum(extra_ref[0].astype(F32).reshape(8, 16, 8, 128), axis=1)
+        for t in range(8):
+            mask_ref[:, t * 128:(t + 1) * 128] = jnp.broadcast_to(placed[t, 0:1, :], (16, 128)).astype(BF)
+
     NS = 6
     sacc = [accs[m * (NS + 4): m * (NS + 4) + NS] for m in range(2)]
     oacc = [accs[m * (NS + 4) + NS: (m + 1) * (NS + 4)] for m in range(2)]
@@ -47,14 +54,15 @@
             ps[m, r, (g * 4 + kt // 2) % 2, (kt % 2) * 128:(kt % 2) * 128 + 128, :] = p
     def push_qb(g, kt):
         for m in range(2):
-            rhs = jnp.concatenate([qs[g, m * 256:(m + 1) * 256, :], b_ref[0, kt, m * 256:(m + 1) * 256, :]], axis=1)
+            rhs = jnp.concatenate([qs[g, m * 256:(m + 1) * 256, :], b_ref[kt, m * 256:(m + 1) * 256, :]], axis=1)
             pltpu.matmul_push_rhs(rhs, 0, m, transpose=True)
     def push_p(g, kp, r):
         for m in range(2):
             pltpu.matmul_push_rhs(ps[m, r, (g * 4 + kp) % 2], 1, m)
     def pv(g, kp, r):
         i = 4 * g + r
-        lhs = vt_ref[i, 0, :, kp * 256:(kp + 1) * 256] * mask_ref[0:1, kp * 256:(kp + 1) * 256]
+        keep = mask_ref[:, kp * 256:(kp + 1) * 256]
+        lhs = vt_ref[i, 0, :, kp * 256:(kp + 1) * 256] * jnp.concatenate([keep] * 3, axis=0)
         for m in range(2):
             pltpu.matmul_acc_lhs(oacc[m][r], lhs, 1)
     def out(g, r):
@@ -102,13 +110,13 @@
         w = pvq.pop(0); push_p(*w); pv(*w)
         if w[1] == 3: out(w[0], w[2])
 
-def attn_kernel(q_ref, k_ref, vt_ref, b_ref, mask_ref, o_ref, den_ref, qs, eye, ps):
+def attn_kernel(q_ref, k_ref, vt_ref, b_ref, extra_ref, o_ref, den_ref, qs, eye, ps, mask_ref):
     specs = []
     for m in range(2):
         specs += [pltpu.ACC(m)((128, 256), F32)] * 6 + [pltpu.ACC(m)((48, 256), F32)] * 4
-    pl.run_scoped(lambda *accs: attn_body(q_ref, k_ref, vt_ref, b_ref, mask_ref, o_ref, den_ref, qs, eye, ps, *accs), *specs)
-
-def attention(q, k, vt, b, mask16):
+    pl.run_scoped(lambda *accs: attn_body(q_ref, k_ref, vt_ref, b_ref, extra_ref, o_ref, den_ref, qs, eye, ps, mask_ref, *accs), *specs)
+
+def attention(q, k, vt, b):
     return pl.pallas_call(
         attn_kernel,
         grid=(2, 4),
@@ -116,18 +124,156 @@
             pl.BlockSpec((8, 1024, 128), lambda a, h: (0, 0, 0)),
             pl.BlockSpec((8, 1024, 128), lambda a, h: (0, 0, 0)),
             pl.BlockSpec((8, 1, 48, 1024), lambda a, h: (0, h, 0, 0)),
-            pl.BlockSpec((1, 8, 512, 128), lambda a, h: (h, 0, a, 0)),
-            pl.BlockSpec((16, 1024), lambda a, h: (0, 0)),
+            pl.BlockSpec((8, 512, 128), lambda a, h: (h, a, 0)),
+            pl.BlockSpec((1, 1024, 128), lambda a, h: (32, 0, 0)),
         ],
         out_specs=[
             pl.BlockSpec((8, 32, 512), lambda a, h: (0, h, a)),
             pl.BlockSpec((1, 8, 512), lambda a, h: (h, 0, a)),
         ],
         out_shape=[jax.ShapeDtypeStruct((8, 128, 1024), F32), jax.ShapeDtypeStruct((4, 8, 1024), F32)],
-        scratch_shapes=[pltpu.VMEM((2, 512, 128), BF), pltpu.VMEM((128, 128), BF), pltpu.VMEM((2, 4, 2, 256, 256), BF)],
+        scratch_shapes=[pltpu.VMEM((2, 512, 128), BF), pltpu.VMEM((128, 128), BF), pltpu.VMEM((2, 4, 2, 256, 256), BF), pltpu.VMEM((16, 1024), BF)],
         compiler_params=pltpu.CompilerParams(vmem_limit_bytes=60 * 2**20),
         name="tri_attn",
-    )(q, k, vt, b, mask16)
+    )(q, k, vt, b, b)
+
+
+MESH_ID = pl.DeviceIdType.MESH
+ORDERS = ((0, 1, 2), (1, 2, 0), (2, 0, 1))
+
+
+def gather_kernel(piece_ref, out_ref, full, send_sem, recv_sem, out_sem):
+    gx, gy = lax.axis_index("gx"), lax.axis_index("gy")
+    core = lax.rem(gx, 2)
+    x = lax.rem(gx // 2, 4)
+    y = gy // 2
+    z = lax.rem(gy, 2) * 2 + gx // 8
+    here = (x, y, z)
+
+    def device(pos, c):
+        px, py, pz = pos
+        return ((lax.rem(pz, 2) * 4 + px) * 2 + c, py * 2 + pz // 2)
+
+    def moved(dim, step):
+        pos = list(here)
+        pos[dim] = lax.rem(pos[dim] + step + 4, 4)
+        return tuple(pos)
+
+    def region(lo, hi, pos, done):
+        px, py, pz = pos
+        zl = slice(None) if 2 in done else lax.rem(pz, 2)
+        zh = slice(None) if 2 in done else pz // 2
+        xi = slice(None) if 0 in done else px
+        yi = slice(None) if 1 in done else py
+        return full.at[lo:hi, zl, xi, core, yi, zh]
+
+    barrier = pltpu.get_barrier_semaphore()
+    partner = device(here, 1 - core)
+    peers = [device(moved(d, s), core) for d in range(3) for s in (1, 3)] + [partner]
+    for peer in peers:
+        pl.semaphore_signal(barrier, inc=1, device_id=peer, device_id_type=MESH_ID)
+    full[:, lax.rem(z, 2), x, core, y, z // 2] = piece_ref[...]
+    pl.semaphore_wait(barrier, 7)
+
+    slots = [0]
+    started = []
+
+    def copy(src, dst, dev):
+        n = slots[0]
+        slots[0] += 1
+        return pltpu.make_async_remote_copy(
+            src_ref=src, dst_ref=dst, send_sem=send_sem.at[n], recv_sem=recv_sem.at[n],
+            device_id=dev, device_id_type=MESH_ID)
+
+    def send(lo, hi, pos, done, dev, first=False):
+        spot = region(lo, hi, pos, done)
+        c = copy(piece_ref.at[lo:hi] if first else spot, spot, dev)
+        c.start()
+        started.append(c)
+        return c
+
+    def arrival(n, lo, hi, pos, done):
+        spot = region(lo, hi, pos, done)
+        pltpu.make_async_remote_copy(
+            src_ref=spot, dst_ref=spot, send_sem=send_sem.at[n], recv_sem=recv_sem.at[n],
+            device_id=partner, device_id_type=MESH_ID).wait_recv()
+
+    partner_waits = []
+
+    def share(lo, hi, pos, done, first=False):
+        n = slots[0]
+        send(lo, hi, pos, done, partner, first)
+        partner_waits.append((n, lo, hi, pos, done))
+
+    for stage in range(3):
+        tags = []
+        for part in range(3):
+            order = ORDERS[part]
+            dim, done = order[stage], order[:stage]
+            lo, hi = 11 * part, 11 * part + 11
+            right, left = device(moved(dim, 1), core), device(moved(dim, 3), core)
+            n = slots[0]
+            send(lo, hi, here, done, right, stage == 0)
+            send(lo, hi, here, done, left, stage == 0)
+            tags.append((n, lo, hi, dim, done, right, left))
+        if stage == 0:
+            share(0, 33, here, (), True)
+        halves = []
+        for n, lo, hi, dim, done, right, left in tags:
+            mid = lo + 6
+            h = slots[0]
+            arrival(n, lo, hi, moved(dim, 3), done)
+            send(lo, mid, moved(dim, 3), done, right)
+            arrival(n + 1, lo, hi, moved(dim, 1), done)
+            send(mid, hi, moved(dim, 1), done, left)
+            share(lo, hi, moved(dim, 3), done)
+            share(lo, hi, moved(dim, 1), done)
+            halves.append((h, lo, mid, hi, dim, done))
+        for h, lo, mid, hi, dim, done in halves:
+            arrival(h, lo, mid, moved(dim, 2), done)
+            arrival(h + 1, mid, hi, moved(dim, 2), done)
+            share(lo, hi, moved(dim, 2), done)
+
+    def partner_region(lo, hi, pos, done):
+        px, py, pz = pos
+        zl = slice(None) if 2 in done else lax.rem(pz, 2)
+        zh = slice(None) if 2 in done else pz // 2
+        xi = slice(None) if 0 in done else px
+        yi = slice(None) if 1 in done else py
+        return full.at[lo:hi, zl, xi, 1 - core, yi, zh]
+
+    for n, lo, hi, pos, done in partner_waits:
+        spot = partner_region(lo, hi, pos, done)
+        pltpu.make_async_remote_copy(
+            src_ref=spot, dst_ref=spot, send_sem=send_sem.at[n], recv_sem=recv_sem.at[n],
+            device_id=partner, device_id_type=MESH_ID).wait_recv()
+    outs = [pltpu.make_async_copy(full.at[11 * p:11 * p + 11], out_ref.at[11 * p:11 * p + 11], out_sem.at[p]) for p in range(3)]
+    for c in outs:
+        c.start()
+    for c in started:
+        c.wait_send()
+    for c in outs:
+        c.wait()
+
+
+def gather(piece, collective_id):
+    shape = (33, 2, 4, 2, 4, 2, 8, 128)
+    n = 64
+    out = pl.pallas_call(
+        gather_kernel,
+        in_specs=[pl.BlockSpec(memory_space=pltpu.VMEM)],
+        out_specs=pl.BlockSpec(memory_space=pl.ANY),
+        out_shape=jax.ShapeDtypeStruct(shape, BF),
+        scratch_shapes=[
+            pltpu.VMEM(shape, BF),
+            pltpu.SemaphoreType.DMA((n,)),
+            pltpu.SemaphoreType.DMA((n,)),
+            pltpu.SemaphoreType.DMA((3,)),
+        ],
+        compiler_params=pltpu.CompilerParams(collective_id=collective_id, has_side_effects=True, vmem_limit_bytes=24 * 2**20),
+        name="tri_gather",
+    )(piece)
+    return out.reshape(33, 1024, 128)
 
 
 def layer_norm(x, gain):
@@ -137,8 +283,13 @@
     return (c * lax.rsqrt(var + 1e-05) * gain).astype(BF)
 
 
-def pre_kernel(z_ref, gain_ref, wqk_ref, wvg_ref, bw_ref, gb_ref, q_ref, k_ref, vt_ref, gate_ref, b_ref, m_ref, scr):
+def pre_kernel(z_ref, gain_ref, wqk_ref, wvg_ref, bw_ref, gb_ref, mask_ref, q_ref, k_ref, vt_ref, gate_ref, b_ref, scr):
     i = pl.program_id(0)
+
+    @pl.when(i == 0)
+    def _():
+        scr[32] = mask_ref[...]
+
     a = layer_norm(z_ref[0].astype(F32), gain_ref[...])
     qk = jnp.dot(a, wqk_ref[0], preferred_element_type=F32)
     q_ref[0] = (qk[:, :128] * (HEAD_DIM ** -0.5 * LOG2E)).astype(BF)
@@ -156,15 +307,16 @@
     b = (b - m) * LOG2E
     for h in range(4):
         for kt in range(8):
-            scr[h, kt, pl.ds(i, 1), :] = b[h:h + 1, kt * 128:(kt + 1) * 128]
-    m_ref[0] = jnp.broadcast_to(m, (16, 128))
+            scr[8 * h + kt, pl.ds(i, 1), :] = b[h:h + 1, kt * 128:(kt + 1) * 128]
+    lane = lax.broadcasted_iota(jnp.int32, (4, 128), 1)
+    scr[32, 1:5, :] = jnp.where(lane == i, m[0:4], scr[32, 1:5, :])
 
     @pl.when(i == 7)
     def _():
         b_ref[...] = scr[...].astype(BF)
 
 
-def pre(z, gain, proj, bias_w, gate_bias):
+def pre(z, gain, proj, bias_w, gate_bias, mask_tile):
     wq, wk, wv, wg = [proj[:, 128 * n:128 * n + 128] for n in range(4)]
 
     def slots(w, i):
@@ -184,27 +336,26 @@
             pl.BlockSpec((128, 256), lambda i: (0, 0)),
             pl.BlockSpec((16, 128), lambda i: (0, 0)),
             pl.BlockSpec((1, 128), lambda i: (0, 0)),
+            pl.BlockSpec((8, 128), lambda i: (0, 0)),
         ],
         out_specs=[
             pl.BlockSpec((1, 1024, 128), row),
             pl.BlockSpec((1, 1024, 128), row),
             pl.BlockSpec((1, 4, 48, 1024), lambda i: (i, 0, 0, 0)),
             pl.BlockSpec((1, 1024, 128), row),
-            pl.BlockSpec((4, 8, 8, 128), lambda i: (0, 0, 0, 0)),
-            pl.BlockSpec((1, 16, 128), row),
+            pl.BlockSpec((33, 8, 128), lambda i: (0, 0, 0)),
         ],
         out_shape=[
             jax.ShapeDtypeStruct((8, 1024, 128), BF),
             jax.ShapeDtypeStruct((8, 1024, 128), BF),
             jax.ShapeDtypeStruct((8, 4, 48, 1024), BF),
             jax.ShapeDtypeStruct((8, 1024, 128), BF),
-            jax.ShapeDtypeStruct((4, 8, 8, 128), BF),
-            jax.ShapeDtypeStruct((8, 16, 128), F32),
-        ],
-        scratch_shapes=[pltpu.VMEM((4, 8, 8, 128), F32)],
+            jax.ShapeDtypeStruct((33, 8, 128), BF),
+        ],
+        scratch_shapes=[pltpu.VMEM((33, 8, 128), F32)],
         compiler_params=pltpu.CompilerParams(vmem_limit_bytes=48 * 2**20),
         name="tri_pre",
-    )(z, gain.reshape(1, 128), wqk, wvg, bwt, gate_bias.reshape(1, 128))
+    )(z, gain.reshape(1, 128), wqk, wvg, bwt, gate_bias.reshape(1, 128), mask_tile)
 
 
 def post_kernel(o_ref, gate_ref, z_ref, w_ref, out_ref, scr):
@@ -264,13 +415,17 @@
     )(z, gain.reshape(1, 128), w1, b1.reshape(1, 512), w2)
 
 
-def exact_attention(q, k, vt, b, maxima, mask):
+def exact_attention(q, k, vt, full):
+    extra = full[32].reshape(128, 8, 128)
+    mask = jnp.sum(extra[:, 0].reshape(8, 16, 128).astype(F32), axis=1).reshape(1024)
+    maxima = jnp.transpose(extra[:, 1:5, :8], (1, 0, 2)).reshape(4, 1024).astype(F32)
     key_bias = (mask - 1.0) * big_negative
-    heads = [jnp.array([(h + i) % 4 for h in range(4)]) for i in range(4)]
+    b = full[:32].reshape(4, 8, 1024, 128)
+    orders = jnp.array([[(h + i) % 4 for h in range(4)] for i in range(4)])
 
     def per_row(operands):
         i, q_row, k_row, vt_row = operands
-        order = jnp.stack(heads)[lax.rem(i, 4)]
+        order = orders[lax.rem(i, 4)]
         qh = q_row.reshape(1024, 4, 32)[:, order]
         kh = k_row.reshape(1024, 4, 32)[:, order]
 
@@ -288,35 +443,18 @@
     return lax.map(per_row, (jnp.arange(8), q, k, vt))
 
 
-def gather_bias(piece, extra):
-    block = jnp.concatenate([piece.reshape(256, 128), extra], axis=0)[None]
-    full = lax.all_gather(lax.all_gather(block, "gy", axis=0, tiled=True), "gx", axis=0, tiled=True)
-    b = full[:, :256].reshape(128, 4, 8, 8, 128)
-    b = jnp.transpose(b, (1, 2, 0, 3, 4)).reshape(4, 8, 1024, 128)
-    return b, full[:, 256:]
-
-
 def swap(z):
     z = z.reshape(128, 8, 8, 128)
     z = lax.all_to_all(z, AX, split_axis=0, concat_axis=0, tiled=True)
     return jnp.swapaxes(z, 0, 1).reshape(8, 1024, 128)
 
 
-def phase(z, mask_local, gain, proj, gate_bias, bias_w, out_w):
-    q, k, vt, gate, piece, m = pre(z, gain, proj, bias_w, gate_bias)
-    maxima = jnp.transpose(m[:, :4, 0]).reshape(1, 32)
-    extra = jnp.zeros((8, 128), F32)
-    extra = extra.at[0:1, 0:8].set(mask_local.astype(F32).reshape(1, 8)).at[1:2, 0:32].set(maxima).astype(BF)
-    b, extras = gather_bias(piece, extra)
-    mask = extras[:, 0, :8].reshape(1, 1024)
-    o, den = attention(q, k, vt, b, jnp.broadcast_to(mask, (16, 1024)))
+def phase(z, mask_tile, gain, proj, gate_bias, bias_w, out_w, collective_id):
+    q, k, vt, gate, piece = pre(z, gain, proj, bias_w, gate_bias, mask_tile)
+    full = gather(piece, collective_id)
+    o, den = attention(q, k, vt, full)
     fine = jnp.all((den > 2.0 ** -60) & (den < 2.0 ** 100))
-    maxima = jnp.transpose(extras[:, 1, :32].reshape(128, 4, 8), (1, 0, 2)).reshape(4, 1024).astype(F32)
-    o = lax.cond(
-        fine,
-        lambda: o,
-        lambda: exact_attention(q, k, vt, b, maxima, mask.reshape(1024).astype(F32)),
-    )
+    o = lax.cond(fine, lambda: o, lambda: exact_attention(q, k, vt, full))
     return post(o, gate, z, out_w)
 
 
@@ -338,9 +476,14 @@
     trans_bias,
     trans_out,
 ):
-    z = phase(pair_in, residue_mask, norm_start, proj_start, gate_bias_start, bias_w_start, out_w_start)
+    device = lax.axis_index("gx") * 8 + lax.axis_index("gy")
+    lane = lax.broadcasted_iota(jnp.int32, (8, 128), 1)
+    row = lax.broadcasted_iota(jnp.int32, (8, 128), 0)
+    spread = jnp.tile(residue_mask.astype(F32), 16).reshape(1, 128)
+    mask_tile = jnp.where((lane // 8 == lax.rem(device, 16)) & (row == 0), spread, 0.0)
+    z = phase(pair_in, mask_tile, norm_start, proj_start, gate_bias_start, bias_w_start, out_w_start, 0)
     z = swap(z)
-    z = phase(z, residue_mask, norm_end, proj_end, gate_bias_end, bias_w_end, out_w_end)
+    z = phase(z, mask_tile, norm_end, proj_end, gate_bias_end, bias_w_end, out_w_end, 1)
     z = swap(z)
     return trans(z, norm_trans, trans_in, trans_bias, trans_out)
 

time: 462 us -> 300 us (0.65)
  waiting for transfers between devices: 137 us -> 28.6 us
  Pallas kernels: 130 us -> 205 us
  blocking collectives: 114 us -> 40.8 us
  local copies, waits for them, and re-layouts: 52.1 us -> 9.7 us
  between operations: 15.1 us -> 1.47 us
    all_gather x2 -> x0, waiting for transfers between devices: 108 us -> none  [gather_bias(): lax.all_gather(lax.all_gather(block, 'gy', axis=0, tiled=True), 'gx', axi...]
    pallas_call x0 -> x2, Pallas kernels: none -> 74.9 us  [gather(): pl.pallas_call(gather_kernel, in_specs=[pl.BlockSpec(memory_space=pltpu.V...]
    all_gather x2 -> x0, blocking collectives: 72.8 us -> none  [gather_bias(): lax.all_gather(block, 'gy', axis=0, tiled=True)]
    slice x10 -> x0, local copies, waits for them, and re-layouts: 20.2 us -> none  [the longest x2 15.6 us: gather_bias(): b = full[:, :256].reshape(128, 4, 8, 8, 128)]
    reshape x2 -> x0, local copies, waits for them, and re-layouts: 17.7 us -> none  [gather_bias(): b = full[:, :256].reshape(128, 4, 8, 8, 128)]
  transfers between devices with their start and end apart: 3 -> 1, of which waited for: 3 -> 1; matrix products, arithmetic and copies ran while one was open for 0% -> 0% of each run, Pallas kernels for 0% -> 0%
where the time goes in v2:
time: 300 us; the launch traced here: 299 us
  Pallas kernels  205 us (68%)
  blocking collectives  40.8 us (14%)
  waiting for transfers between devices  28.6 us (10%)
  local copies, waits for them, and re-layouts  9.7 us (3%)
  starting transfers between devices  9.23 us (3%)
  other arithmetic  4.37 us (1%)
    pallas_call x2, Pallas kernels, attention(): pl.pallas_call(attn_kernel, grid=(2, 4), in_specs=[pl.BlockSpec((8, 1024,...  86.5 us
    pallas_call x2, Pallas kernels, gather(): pl.pallas_call(gather_kernel, in_specs=[pl.BlockSpec(memory_space=pltpu.V...  74.9 us
    all_to_all x1, blocking collectives, swap(): z = lax.all_to_all(z, AX, split_axis=0, concat_axis=0, tiled=True)  40.8 us
    all_to_all x1, waiting for transfers between devices, swap(): z = lax.all_to_all(z, AX, split_axis=0, concat_axis=0, tiled=True)  28.6 us
    pallas_call x2, Pallas kernels, pre(): pl.pallas_call(pre_kernel, grid=(8,), in_specs=[pl.BlockSpec((1, 1024, 12...  19 us
    pallas_call x2, Pallas kernels, post(): pl.pallas_call(post_kernel, grid=(8,), in_specs=[pl.BlockSpec((8, 128, 12...  14.2 us
    pallas_call x1, Pallas kernels, trans(): pl.pallas_call(trans_kernel, grid=(8,), in_specs=[pl.BlockSpec((1, 1024,...  10.3 us
    all_to_all x1, starting transfers between devices, swap(): z = lax.all_to_all(z, AX, split_axis=0, concat_axis=0, tiled=True)  9.23 us
  transfers between devices with their start and end apart: 1, of which 1 were waited for; matrix products, arithmetic and copies ran while one was open for 0% of the time, Pallas kernels for 0%

profile of v2, /device:TPU:12, one launch (start us, length us, event | category | flops | bytes accessed | tf_op | source)
XLA Modules:
  0.0 299.1 jit_solution(12001857126899151241)
XLA Ops:
  0.0 0.9 fusion.53
  0.9 0.9 fusion.54
  1.9 0.9 fusion.55
  2.8 0.9 fusion.52
  3.7 0.7 convert_element_type.76
  4.5 0.7 pad.7.bw_ref
  5.2 0.1 maximum_bitcast_fusion.1
  5.3 0.1 maximum_bitcast_fusion
  5.5 1.6 copy-done.1
  7.1 0.7 copy-done.9
  7.8 0.7 copy-done.10
  8.4 9.5 %tri_pre.2 = (bf16[8,1024,128]{2,1,0:T(8,128)(2,1)}, bf16[8,1024,128]{2,1,0:T(8,128)(2,1)}, bf16[8,4,48,1024]{3,2,1,0:T(8,128)(2,1)}, bf16[8,1024,128]{2,1,0:T(8,128)(2,1)S(1)}, bf16[33,8,128]{2,1,0:T(8,128)(2,1)S(1)}) custom-call(bf16[8,1024,128]{2,1,0:T(8,128)(2,1)S(1)} %copy-done.1, f32[1,128]{1,0:T(1,128)S(1)} %bitcast.210, ...), custom_call_target="tpu_custom_call" | custom-call | tf_op jit(solution)/shard_map/tri_pre/pallas_call | solution.py:329
  17.9 38.7 %tri_gather.2 = bf16[33,2,4,2,4,2,8,128]{7,6,5,4,3,2,1,0:T(8,128)(2,1)} custom-call(bf16[33,8,128]{2,1,0:T(8,128)(2,1)S(1)} %get-tuple-element.248.piece_ref), custom_call_target="tpu_custom_call" | custom-call | tf_op jit(solution)/shard_map/tri_gather/pallas_call | solution.py:262
  56.6 43.2 %tri_attn.2 = (f32[8,128,1024]{2,1,0:T(8,128)}, f32[4,8,1024]{2,1,0:T(8,128)}) custom-call(bf16[8,1024,128]{2,1,0:T(8,128)(2,1)} %get-tuple-element.245.q_ref, bf16[8,1024,128]{2,1,0:T(8,128)(2,1)} %get-tuple-element.246.k_ref, bf16[8,4,48,1024]{3,2,1,0:T(8,128)(2,1)} %get-tuple-element.247.vt_ref, bf16[33,1024,128]{2,1,0:T(8,128)(2,1)} %bitcast.224, ...), custom_call_target="tpu_custom_call" | custom-call | tf_op jit(solution)/shard_map/tri_attn/pallas_call | solution.py:120
  99.9 1.5 and_reduce_fusion.1
  102.0 0.7 copy-done.6
  102.7 7.7 %tri_post.2 = bf16[8192,128]{1,0:T(8,128)(2,1)} custom-call(f32[8,128,1024]{2,1,0:T(8,128)} %get-tuple-element.853.o_ref, bf16[8,1024,128]{2,1,0:T(8,128)(2,1)S(1)} %get-tuple-element.251.gate_ref, bf16[8,1024,128]{2,1,0:T(8,128)(2,1)} %z_ref.3, bf16[128,128]{1,0:T(8,128)(2,1)S(1)} %copy-done.6), custom_call_target="tpu_custom_call" | custom-call | tf_op jit(solution)/shard_map/tri_post/pallas_call | solution.py:374
  110.4 9.2 %all-to-all-start = ((bf16[128,8,8,128]{3,2,1,0:T(8,128)(2,1)}), bf16[128,8,8,128]{3,2,1,0:T(8,128)(2,1)S(1)}, u32[]{:S(2)}, u32[]{:S(2)}) async-start(bf16[128,8,8,128]{3,2,1,0:T(8,128)(2,1)} %bitcast.48), calls=%async_computation | async-start | bytes 4194304 | tf_op jit(solution)/shard_map/all_to_all | solution.py:448
  119.8 0.1 maximum_bitcast_fusion.4
  120.1 0.1 maximum_bitcast_fusion.3
  120.3 28.6 %all-to-all-done = bf16[128,8,8,128]{3,2,1,0:T(8,128)(2,1)S(1)} async-done(((bf16[128,8,8,128]{3,2,1,0:T(8,128)(2,1)}), bf16[128,8,8,128]{3,2,1,0:T(8,128)(2,1)S(1)}, u32[]{:S(2)}, u32[]{:S(2)}) %all-to-all-start) | async-done | bytes 2097184 | tf_op jit(solution)/shard_map/all_to_all | solution.py:448
  148.9 0.4 copy_bitcast_fusion.1.z_ref
  149.3 9.5 %tri_pre.3 = (bf16[8,1024,128]{2,1,0:T(8,128)(2,1)}, bf16[8,1024,128]{2,1,0:T(8,128)(2,1)}, bf16[8,4,48,1024]{3,2,1,0:T(8,128)(2,1)}, bf16[8,1024,128]{2,1,0:T(8,128)(2,1)S(1)}, bf16[33,8,128]{2,1,0:T(8,128)(2,1)S(1)}) custom-call(bf16[8,1024,128]{2,1,0:T(8,128)(2,1)S(1)} %copy_bitcast_fusion.1.z_ref, f32[1,128]{1,0:T(1,128)S(1)} %bitcast.212, ...), custom_call_target="tpu_custom_call" | custom-call | tf_op jit(solution)/shard_map/tri_pre/pallas_call | solution.py:329
  158.8 36.2 %tri_gather.3 = bf16[33,2,4,2,4,2,8,128]{7,6,5,4,3,2,1,0:T(8,128)(2,1)} custom-call(bf16[33,8,128]{2,1,0:T(8,128)(2,1)S(1)} %get-tuple-element.255.piece_ref), custom_call_target="tpu_custom_call" | custom-call | tf_op jit(solution)/shard_map/tri_gather/pallas_call | solution.py:262
  195.0 43.2 %tri_attn.3 = (f32[8,128,1024]{2,1,0:T(8,128)}, f32[4,8,1024]{2,1,0:T(8,128)}) custom-call(bf16[8,1024,128]{2,1,0:T(8,128)(2,1)} %get-tuple-element.252.q_ref, bf16[8,1024,128]{2,1,0:T(8,128)(2,1)} %get-tuple-element.253.k_ref, bf16[8,4,48,1024]{3,2,1,0:T(8,128)(2,1)} %get-tuple-element.254.vt_ref, bf16[33,1024,128]{2,1,0:T(8,128)(2,1)} %bitcast.221, ...), custom_call_target="tpu_custom_call" | custom-call | tf_op jit(solution)/shard_map/tri_attn/pallas_call | solution.py:120
  238.2 1.5 and_reduce_fusion
  240.3 0.2 conditional.3
  240.6 0.5 copy-done.7
  241.1 6.5 %tri_post.3 = bf16[8192,128]{1,0:T(8,128)(2,1)S(1)} custom-call(f32[8,128,1024]{2,1,0:T(8,128)} %get-tuple-element.854.o_ref, bf16[8,1024,128]{2,1,0:T(8,128)(2,1)S(1)} %get-tuple-element.258.gate_ref, bf16[8,1024,128]{2,1,0:T(8,128)(2,1)} %copy-done, bf16[128,128]{1,0:T(8,128)(2,1)S(1)} %copy-done.7), custom_call_target="tpu_custom_call" | custom-call | tf_op jit(solution)/shard_map/tri_post/pallas_call | solution.py:374
  247.6 40.8 %all_to_all.10 = bf16[128,8,8,128]{3,2,1,0:T(8,128)(2,1)S(1)} all-to-all(bf16[128,8,8,128]{3,2,1,0:T(8,128)(2,1)S(1)} %bitcast.208), channel_id=1, replica_groups=mesh['gx'=16,'gy'=8] {'gx','gy'}, dimensions={0} | all-to-all | bytes 4194304 | tf_op jit(solution)/shard_map/all_to_all | solution.py:448
  288.4 0.4 copy_bitcast_fusion.z_ref
  288.8 10.3 %tri_trans.1 = bf16[8,1024,128]{2,1,0:T(8,128)(2,1)} custom-call(bf16[8,1024,128]{2,1,0:T(8,128)(2,1)S(1)} %copy_bitcast_fusion.z_ref, f32[1,128]{1,0:T(1,128)S(1)} %bitcast.214, bf16[128,512]{1,0:T(8,128)(2,1)S(1)} %copy-done.2, f32[1,512]{1,0:T(1,128)S(1)} %bitcast.209, bf16[512,128]{1,0:T(8,128)(2,1)S(1)} %copy-done.3), custom_call_target="tpu_custom_call" | custom-call | tf_op jit(solution)/shard_map/tri_trans/pallas_call | solution.py:401
  (41 shorter events, 0.6 us)
Async XLA Ops:
  5.5 51.1 %copy-start.4 = (f32[8,128]{1,0:T(8,128)}, f32[8,128]{1,0:T(8,128)S(1)}, u32[]{:S(2)}) copy-start(f32[8,128]{1,0:T(8,128)S(1)} %fusion.45.mask_ref) | copy-start | bytes 12292
  5.5 1.6 copy-start.1
  7.1 0.7 copy-start.9
  7.8 0.7 copy-start.10
  101.9 0.8 copy-start.6
  110.4 9.3 %copy-start.15 = (bf16[128,4]{0,1:T(4,128)(2,1)S(1)}, bf16[128,4]{0,1:T(4,128)(2,1)}, u32[]{:S(2)}) copy-start(bf16[128,4]{0,1:T(4,128)(2,1)} %param.40) | copy-start | bytes 3076
  110.4 9.3 %copy-start.14 = (bf16[128,512]{1,0:T(8,128)(2,1)S(1)}, bf16[128,512]{1,0:T(8,128)(2,1)}, u32[]{:S(2)}) copy-start(bf16[128,512]{1,0:T(8,128)(2,1)} %param.38) | copy-start | bytes 393220
  110.4 38.5 %all-to-all-start = ((bf16[128,8,8,128]{3,2,1,0:T(8,128)(2,1)}), bf16[128,8,8,128]{3,2,1,0:T(8,128)(2,1)S(1)}, u32[]{:S(2)}, u32[]{:S(2)}) async-start(bf16[128,8,8,128]{3,2,1,0:T(8,128)(2,1)} %bitcast.48), calls=%async_computation | async-start | bytes 4194304 | tf_op jit(solution)/shard_map/all_to_all | solution.py:448
  119.6 29.6 %copy-start.5 = (f32[8,128]{1,0:T(8,128)S(1)}, f32[8,128]{1,0:T(8,128)}, u32[]{:S(2)}) copy-start(f32[8,128]{1,0:T(8,128)} %copy-done.4) | copy-start | bytes 12292
  119.6 29.6 %copy-start.11 = (f32[128]{0:T(128)S(1)}, f32[128]{0:T(128)}, u32[]{:S(2)}) copy-start(f32[128]{0:T(128)} %param.37) | copy-start | bytes 1540
  119.7 29.6 %copy-start.12 = (f32[128]{0:T(128)S(1)}, f32[128]{0:T(128)}, u32[]{:S(2)}) copy-start(f32[128]{0:T(128)} %param.39) | copy-start | bytes 1540
  149.2 45.8 %copy-start = (bf16[8,1024,128]{2,1,0:T(8,128)(2,1)}, bf16[8,1024,128]{2,1,0:T(8,128)(2,1)S(1)}, u32[]{:S(2)}) copy-start(bf16[8,1024,128]{2,1,0:T(8,128)(2,1)S(1)} %copy_bitcast_fusion.1.z_ref) | copy-start | bytes 6291460
  240.3 0.8 copy-start.7
  247.6 41.2 %copy-start.2 = (bf16[128,512]{1,0:T(8,128)(2,1)S(1)}, bf16[128,512]{1,0:T(8,128)(2,1)}, u32[]{:S(2)}) copy-start(bf16[128,512]{1,0:T(8,128)(2,1)} %w1_ref.1) | copy-start | bytes 393220
  247.6 41.2 %copy-start.3 = (bf16[512,128]{1,0:T(8,128)(2,1)S(1)}, bf16[512,128]{1,0:T(8,128)(2,1)}, u32[]{:S(2)}) copy-start(bf16[512,128]{1,0:T(8,128)(2,1)} %w2_ref.1) | copy-start | bytes 393220
  247.6 41.2 %copy-start.8 = (f32[512]{0:T(512)S(1)}, f32[512]{0:T(512)}, u32[]{:S(2)}) copy-start(f32[512]{0:T(512)} %param.44) | copy-start | bytes 6148
  247.6 41.2 %copy-start.13 = (f32[128]{0:T(128)S(1)}, f32[128]{0:T(128)}, u32[]{:S(2)}) copy-start(f32[128]{0:T(128)} %param.42) | copy-start | bytes 1540

commit v3 on v2

--- a/solution.py
+++ b/solution.py
@@ -358,34 +358,80 @@
     )(z, gain.reshape(1, 128), wqk, wvg, bwt, gate_bias.reshape(1, 128), mask_tile)
 
 
-def post_kernel(o_ref, gate_ref, z_ref, w_ref, out_ref, scr):
-    parts = []
-    for i in range(8):
-        o = jnp.transpose(o_ref[i])
-        parts.append((o * gate_ref[i].astype(F32)).astype(BF))
-    y = jnp.dot(jnp.concatenate(parts, axis=0), w_ref[...], preferred_element_type=F32)
-    for i in range(8):
-        scr[pl.ds(i, 128, stride=8), :] = z_ref[i].astype(F32) + y[128 * i:128 * i + 128]
-    out_ref[...] = scr[...].astype(BF)
-
-
-def post(o, gate, z, w):
-    tile = lambda t: (0, t, 0)
-    return pl.pallas_call(
+def post_kernel(o_ref, gate_ref, z_ref, w_ref, out_ref, scr, outgoing, landed, send_sem, recv_sem, out_sem):
+    gx, gy = lax.axis_index("gx"), lax.axis_index("gy")
+    me = gx * 8 + gy
+    barrier = pltpu.get_barrier_semaphore()
+
+    def greet(n, _):
+        peer = lax.rem(me + n, 128)
+        pl.semaphore_signal(barrier, inc=1, device_id=(peer // 8, lax.rem(peer, 8)), device_id_type=MESH_ID)
+        return 0
+
+    lax.fori_loop(1, 128, greet, 0)
+
+    def tile(s, _):
+        t = lax.rem(s + gx // 2, 8)
+        at = pl.ds(pl.multiple_of(t * 128, 128), 128)
+        parts = []
+        for i in range(8):
+            o = jnp.transpose(o_ref[i, :, at])
+            parts.append((o * gate_ref[i, at].astype(F32)).astype(BF))
+        y = jnp.dot(jnp.concatenate(parts, axis=0), w_ref[...], preferred_element_type=F32)
+        for i in range(8):
+            scr[pl.ds(i, 128, stride=8), :] = z_ref[i, at].astype(F32) + y[128 * i:128 * i + 128]
+        outgoing[pl.ds(pl.multiple_of(t * 16, 16), 16)] = scr[...].astype(BF).reshape(16, 8, 8, 128)
+
+        @pl.when(s == 0)
+        def _():
+            pl.semaphore_wait(barrier, 127)
+
+        def push(n, _):
+            dest = t * 16 + lax.rem(me + n, 16)
+
+            @pl.when(dest != me)
+            def _():
+                pltpu.make_async_remote_copy(
+                    src_ref=outgoing.at[dest], dst_ref=landed.at[:, me], send_sem=send_sem, recv_sem=recv_sem,
+                    device_id=(dest // 8, lax.rem(dest, 8)), device_id_type=MESH_ID).start()
+
+            return 0
+
+        lax.fori_loop(0, 16, push, 0)
+        return 0
+
+    lax.fori_loop(0, 8, tile, 0)
+    landed[:, me] = outgoing[me]
+    everything = landed.at[:, 0:127]
+    arrived = pltpu.make_async_remote_copy(
+        src_ref=outgoing.at[0:127], dst_ref=everything, send_sem=send_sem, recv_sem=recv_sem,
+        device_id=(lax.rem(gx + 1, 16), gy), device_id_type=MESH_ID)
+    arrived.wait_recv()
+    out = pltpu.make_async_copy(landed, out_ref, out_sem)
+    out.start()
+    arrived.wait_send()
+    out.wait()
+
+
+def post(o, gate, z, w, collective_id):
+    vmem = pl.BlockSpec(memory_space=pltpu.VMEM)
+    out = pl.pallas_call(
         post_kernel,
-        grid=(8,),
-        in_specs=[
-            pl.BlockSpec((8, 128, 128), lambda t: (0, 0, t)),
-            pl.BlockSpec((8, 128, 128), tile),
-            pl.BlockSpec((8, 128, 128), tile),
-            pl.BlockSpec((128, 128), lambda t: (0, 0)),
-        ],
-        out_specs=pl.BlockSpec((1024, 128), lambda t: (t, 0)),
-        out_shape=jax.ShapeDtypeStruct((8192, 128), BF),
-        scratch_shapes=[pltpu.VMEM((1024, 128), F32)],
-        compiler_params=pltpu.CompilerParams(vmem_limit_bytes=48 * 2**20),
+        in_specs=[vmem] * 4,
+        out_specs=pl.BlockSpec(memory_space=pl.ANY),
+        out_shape=jax.ShapeDtypeStruct((8, 128, 8, 128), BF),
+        scratch_shapes=[
+            pltpu.VMEM((1024, 128), F32),
+            pltpu.VMEM((128, 8, 8, 128), BF),
+            pltpu.VMEM((8, 128, 8, 128), BF),
+            pltpu.SemaphoreType.DMA,
+            pltpu.SemaphoreType.DMA,
+            pltpu.SemaphoreType.DMA,
+        ],
+        compiler_params=pltpu.CompilerParams(collective_id=collective_id, has_side_effects=True, vmem_limit_bytes=40 * 2**20),
         name="tri_post",
     )(o, gate, z, w)
+    return out.reshape(8, 1024, 128)
 
 
 def trans_kernel(z_ref, gain_ref, w1_ref, b1_ref, w2_ref, out_ref):
@@ -443,19 +489,13 @@
     return lax.map(per_row, (jnp.arange(8), q, k, vt))
 
 
-def swap(z):
-    z = z.reshape(128, 8, 8, 128)
-    z = lax.all_to_all(z, AX, split_axis=0, concat_axis=0, tiled=True)
-    return jnp.swapaxes(z, 0, 1).reshape(8, 1024, 128)
-
-
 def phase(z, mask_tile, gain, proj, gate_bias, bias_w, out_w, collective_id):
     q, k, vt, gate, piece = pre(z, gain, proj, bias_w, gate_bias, mask_tile)
     full = gather(piece, collective_id)
     o, den = attention(q, k, vt, full)
     fine = jnp.all((den > 2.0 ** -60) & (den < 2.0 ** 100))
     o = lax.cond(fine, lambda: o, lambda: exact_attention(q, k, vt, full))
-    return post(o, gate, z, out_w)
+    return post(o, gate, z, out_w, 2 + collective_id)
 
 
 def local(
@@ -482,9 +522,7 @@
     spread = jnp.tile(residue_mask.astype(F32), 16).reshape(1, 128)
     mask_tile = jnp.where((lane // 8 == lax.rem(device, 16)) & (row == 0), spread, 0.0)
     z = phase(pair_in, mask_tile, norm_start, proj_start, gate_bias_start, bias_w_start, out_w_start, 0)
-    z = swap(z)
     z = phase(z, mask_tile, norm_end, proj_end, gate_bias_end, bias_w_end, out_w_end, 1)
-    z = swap(z)
     return trans(z, norm_trans, trans_in, trans_bias, trans_out)
 
 

time: 300 us -> 291 us (0.970)
  Pallas kernels: 205 us -> 267 us
  blocking collectives: 40.8 us -> 0 us
  waiting for transfers between devices: 28.6 us -> 0 us
  starting transfers between devices: 9.23 us -> 0 us
  local copies, waits for them, and re-layouts: 9.7 us -> 13.9 us
    pallas_call x2, Pallas kernels: 14.2 us -> 75.3 us  [post(): pl.pallas_call(post_kernel, in_specs=[vmem] * 4, out_specs=pl.BlockSpec(m...]
    all_to_all x1 -> x0, blocking collectives: 40.8 us -> none  [swap(): z = lax.all_to_all(z, AX, split_axis=0, concat_axis=0, tiled=True)]
    all_to_all x1 -> x0, waiting for transfers between devices: 28.6 us -> none  [swap(): z = lax.all_to_all(z, AX, split_axis=0, concat_axis=0, tiled=True)]
    all_to_all x1 -> x0, starting transfers between devices: 9.23 us -> none  [swap(): z = lax.all_to_all(z, AX, split_axis=0, concat_axis=0, tiled=True)]
    unnamed x32 -> x48, local copies, waits for them, and re-layouts: 4.21 us -> 9.08 us
  transfers between devices with their start and end apart: 1 -> 0, of which waited for: 1 -> 0; matrix products, arithmetic and copies ran while one was open for 0% -> 0% of each run, Pallas kernels for 0% -> 0%
where the time goes in v3:
time: 291 us; the launch traced here: 287 us
  Pallas kernels  267 us (92%)
  local copies, waits for them, and re-layouts  13.9 us (5%)
  other arithmetic  4.41 us (2%)
    pallas_call x2, Pallas kernels, attention(): pl.pallas_call(attn_kernel, grid=(2, 4), in_specs=[pl.BlockSpec((8, 1024,...  86.8 us
    pallas_call x2, Pallas kernels, gather(): pl.pallas_call(gather_kernel, in_specs=[pl.BlockSpec(memory_space=pltpu.V...  76.1 us
    pallas_call x2, Pallas kernels, post(): pl.pallas_call(post_kernel, in_specs=[vmem] * 4, out_specs=pl.BlockSpec(m...  75.3 us
    pallas_call x2, Pallas kernels, pre(): pl.pallas_call(pre_kernel, grid=(8,), in_specs=[pl.BlockSpec((1, 1024, 12...  18.7 us
    pallas_call x1, Pallas kernels, trans(): pl.pallas_call(trans_kernel, grid=(8,), in_specs=[pl.BlockSpec((1, 1024,...  10.3 us
    unnamed x48, local copies, waits for them, and re-layouts  9.08 us

profile of v3, /device:TPU:12, one launch (start us, length us, event | category | flops | bytes accessed | tf_op | source)
XLA Modules:
  0.0 287.3 jit_solution(14493855209901184993)
XLA Ops:
  0.0 1.0 fusion.53
  1.0 1.0 fusion.54
  1.9 0.1 maximum_bitcast_fusion
  2.1 1.0 fusion.55
  3.0 0.1 maximum_bitcast_fusion.1
  3.1 0.9 fusion.52
  4.1 0.7 convert_element_type.76
  4.9 0.7 pad.7.bw_ref
  5.6 1.6 copy-done.2
  7.2 0.7 copy-done.15
  7.9 0.7 copy-done.16
  8.5 9.3 %tri_pre.2 = (bf16[8,1024,128]{2,1,0:T(8,128)(2,1)}, bf16[8,1024,128]{2,1,0:T(8,128)(2,1)}, bf16[8,4,48,1024]{3,2,1,0:T(8,128)(2,1)S(1)}, bf16[8,1024,128]{2,1,0:T(8,128)(2,1)S(1)}, bf16[33,8,128]{2,1,0:T(8,128)(2,1)S(1)}) custom-call(bf16[8,1024,128]{2,1,0:T(8,128)(2,1)S(1)} %copy-done.2, f32[1,128]{1,0:T(1,128)S(1)} %bitcast.202, ...), custom_call_target="tpu_custom_call" | custom-call | tf_op jit(solution)/shard_map/tri_pre/pallas_call | solution.py:329
  17.9 38.7 %tri_gather.2 = bf16[33,2,4,2,4,2,8,128]{7,6,5,4,3,2,1,0:T(8,128)(2,1)} custom-call(bf16[33,8,128]{2,1,0:T(8,128)(2,1)S(1)} %get-tuple-element.248.piece_ref), custom_call_target="tpu_custom_call" | custom-call | tf_op jit(solution)/shard_map/tri_gather/pallas_call | solution.py:262
  56.6 43.4 %tri_attn.2 = (f32[8,128,1024]{2,1,0:T(8,128)}, f32[4,8,1024]{2,1,0:T(8,128)}) custom-call(bf16[8,1024,128]{2,1,0:T(8,128)(2,1)} %get-tuple-element.245.q_ref, bf16[8,1024,128]{2,1,0:T(8,128)(2,1)} %get-tuple-element.246.k_ref, bf16[8,4,48,1024]{3,2,1,0:T(8,128)(2,1)S(1)} %get-tuple-element.247.vt_ref, bf16[33,1024,128]{2,1,0:T(8,128)(2,1)} %bitcast.216, ...), custom_call_target="tpu_custom_call" | custom-call | tf_op jit(solution)/shard_map/tri_attn/pallas_call | solution.py:120
  100.0 1.6 and_reduce_fusion.1
  102.2 0.2 conditional.2
  102.4 1.4 copy-done.3
  103.7 1.6 copy-done.7
  105.4 37.4 %tri_post.2 = bf16[8,128,8,128]{3,2,1,0:T(8,128)(2,1)S(1)} custom-call(f32[8,128,1024]{2,1,0:T(8,128)} %get-tuple-element.827.o_ref, bf16[8,1024,128]{2,1,0:T(8,128)(2,1)S(1)} %copy-done.7, bf16[8,1024,128]{2,1,0:T(8,128)(2,1)S(1)} %copy-done.3, bf16[128,128]{1,0:T(8,128)(2,1)S(1)} %copy-done.12), custom_call_target="tpu_custom_call" | custom-call | tf_op jit(solution)/shard_map/tri_post/pallas_call | solution.py:418
  142.8 0.1 fusion.49
  142.9 0.1 fusion.50
  143.0 0.1 maximum_bitcast_fusion.3
  143.1 0.1 fusion.51
  143.2 0.1 maximum_bitcast_fusion.4
  143.4 9.4 %tri_pre.3 = (bf16[8,1024,128]{2,1,0:T(8,128)(2,1)}, bf16[8,1024,128]{2,1,0:T(8,128)(2,1)}, bf16[8,4,48,1024]{3,2,1,0:T(8,128)(2,1)S(1)}, bf16[8,1024,128]{2,1,0:T(8,128)(2,1)S(1)}, bf16[33,8,128]{2,1,0:T(8,128)(2,1)S(1)}) custom-call(bf16[8,1024,128]{2,1,0:T(8,128)(2,1)S(1)} %bitcast.198, f32[1,128]{1,0:T(1,128)S(1)} %bitcast.204, ...), custom_call_target="tpu_custom_call" | custom-call | tf_op jit(solution)/shard_map/tri_pre/pallas_call | solution.py:329
  152.8 37.5 %tri_gather.3 = bf16[33,2,4,2,4,2,8,128]{7,6,5,4,3,2,1,0:T(8,128)(2,1)} custom-call(bf16[33,8,128]{2,1,0:T(8,128)(2,1)S(1)} %get-tuple-element.255.piece_ref), custom_call_target="tpu_custom_call" | custom-call | tf_op jit(solution)/shard_map/tri_gather/pallas_call | solution.py:262
  190.3 43.4 %tri_attn.3 = (f32[8,128,1024]{2,1,0:T(8,128)}, f32[4,8,1024]{2,1,0:T(8,128)}) custom-call(bf16[8,1024,128]{2,1,0:T(8,128)(2,1)} %get-tuple-element.252.q_ref, bf16[8,1024,128]{2,1,0:T(8,128)(2,1)} %get-tuple-element.253.k_ref, bf16[8,4,48,1024]{3,2,1,0:T(8,128)(2,1)S(1)} %get-tuple-element.254.vt_ref, bf16[33,1024,128]{2,1,0:T(8,128)(2,1)} %bitcast.213, ...), custom_call_target="tpu_custom_call" | custom-call | tf_op jit(solution)/shard_map/tri_attn/pallas_call | solution.py:120
  233.7 1.6 and_reduce_fusion
  235.9 1.5 copy-done.1
  237.4 1.6 copy-done.5
  239.0 37.9 %tri_post.3 = bf16[8,128,8,128]{3,2,1,0:T(8,128)(2,1)S(1)} custom-call(f32[8,128,1024]{2,1,0:T(8,128)} %get-tuple-element.828.o_ref, bf16[8,1024,128]{2,1,0:T(8,128)(2,1)S(1)} %copy-done.5, bf16[8,1024,128]{2,1,0:T(8,128)(2,1)S(1)} %bitcast.199, bf16[128,128]{1,0:T(8,128)(2,1)S(1)} %copy-done.13), custom_call_target="tpu_custom_call" | custom-call | tf_op jit(solution)/shard_map/tri_post/pallas_call | solution.py:418
  277.0 10.3 %tri_trans.1 = bf16[8,1024,128]{2,1,0:T(8,128)(2,1)} custom-call(bf16[8,1024,128]{2,1,0:T(8,128)(2,1)S(1)} %bitcast.200, f32[1,128]{1,0:T(1,128)S(1)} %bitcast.206, bf16[128,512]{1,0:T(8,128)(2,1)S(1)} %copy-done.8, f32[1,512]{1,0:T(1,128)S(1)} %bitcast.201, bf16[512,128]{1,0:T(8,128)(2,1)S(1)} %copy-done.9), custom_call_target="tpu_custom_call" | custom-call | tf_op jit(solution)/shard_map/tri_trans/pallas_call | solution.py:447
  (52 shorter events, 0.4 us)
Async XLA Ops:
  4.9 51.6 %copy-start.10 = (f32[8,128]{1,0:T(8,128)}, f32[8,128]{1,0:T(8,128)S(1)}, u32[]{:S(2)}) copy-start(f32[8,128]{1,0:T(8,128)S(1)} %fusion.45.mask_ref) | copy-start | bytes 12292
  5.6 1.6 copy-start.2
  7.2 0.7 copy-start.15
  7.9 0.7 copy-start.16
  17.9 38.7 %copy-start.6 = (bf16[8,1024,128]{2,1,0:T(8,128)(2,1)}, bf16[8,1024,128]{2,1,0:T(8,128)(2,1)S(1)}, u32[]{:S(2)}) copy-start(bf16[8,1024,128]{2,1,0:T(8,128)(2,1)S(1)} %get-tuple-element.251.gate_ref) | copy-start | bytes 6291460
  17.9 38.7 %copy-start.21 = (bf16[8,4,48,1024]{3,2,1,0:T(8,128)(2,1)}, bf16[8,4,48,1024]{3,2,1,0:T(8,128)(2,1)S(1)}, u32[]{:S(2)}) copy-start(bf16[8,4,48,1024]{3,2,1,0:T(8,128)(2,1)S(1)} %get-tuple-element.247.vt_ref) | copy-start | bytes 9437188
  102.1 1.6 copy-start.3
  102.2 1.6 copy-start.12
  103.7 1.6 copy-start.7
  105.3 37.4 %copy-start.22 = (bf16[128,512]{1,0:T(8,128)(2,1)S(1)}, bf16[128,512]{1,0:T(8,128)(2,1)}, u32[]{:S(2)}) copy-start(bf16[128,512]{1,0:T(8,128)(2,1)} %param.38) | copy-start | bytes 393220
  105.3 38.0 %copy-start.23 = (bf16[128,4]{0,1:T(4,128)(2,1)S(1)}, bf16[128,4]{0,1:T(4,128)(2,1)}, u32[]{:S(2)}) copy-start(bf16[128,4]{0,1:T(4,128)(2,1)} %param.40) | copy-start | bytes 3076
  105.3 38.1 %copy-start.11 = (f32[8,128]{1,0:T(8,128)S(1)}, f32[8,128]{1,0:T(8,128)}, u32[]{:S(2)}) copy-start(f32[8,128]{1,0:T(8,128)} %copy-done.10) | copy-start | bytes 12292
  105.3 38.1 %copy-start.17 = (f32[128]{0:T(128)S(1)}, f32[128]{0:T(128)}, u32[]{:S(2)}) copy-start(f32[128]{0:T(128)} %param.37) | copy-start | bytes 1540
  105.3 38.1 %copy-start.18 = (f32[128]{0:T(128)S(1)}, f32[128]{0:T(128)}, u32[]{:S(2)}) copy-start(f32[128]{0:T(128)} %param.39) | copy-start | bytes 1540
  142.8 47.5 %copy-start = (bf16[8,128,8,128]{3,2,1,0:T(8,128)(2,1)}, bf16[8,128,8,128]{3,2,1,0:T(8,128)(2,1)S(1)}, u32[]{:S(2)}) copy-start(bf16[8,128,8,128]{3,2,1,0:T(8,128)(2,1)S(1)} %tri_post.2) | copy-start | bytes 6291460
  152.8 37.5 %copy-start.4 = (bf16[8,1024,128]{2,1,0:T(8,128)(2,1)}, bf16[8,1024,128]{2,1,0:T(8,128)(2,1)S(1)}, u32[]{:S(2)}) copy-start(bf16[8,1024,128]{2,1,0:T(8,128)(2,1)S(1)} %get-tuple-element.258.gate_ref) | copy-start | bytes 6291460
  152.8 37.5 %copy-start.20 = (bf16[8,4,48,1024]{3,2,1,0:T(8,128)(2,1)}, bf16[8,4,48,1024]{3,2,1,0:T(8,128)(2,1)S(1)}, u32[]{:S(2)}) copy-start(bf16[8,4,48,1024]{3,2,1,0:T(8,128)(2,1)S(1)} %get-tuple-element.254.vt_ref) | copy-start | bytes 9437188
  235.8 1.6 copy-start.1
  235.8 1.6 copy-start.13
  237.4 1.6 copy-start.5
  239.0 37.9 %copy-start.8 = (bf16[128,512]{1,0:T(8,128)(2,1)S(1)}, bf16[128,512]{1,0:T(8,128)(2,1)}, u32[]{:S(2)}) copy-start(bf16[128,512]{1,0:T(8,128)(2,1)} %w1_ref.1) | copy-start | bytes 393220
  239.0 37.9 %copy-start.9 = (bf16[512,128]{1,0:T(8,128)(2,1)S(1)}, bf16[512,128]{1,0:T(8,128)(2,1)}, u32[]{:S(2)}) copy-start(bf16[512,128]{1,0:T(8,128)(2,1)} %w2_ref.1) | copy-start | bytes 393220
  239.0 38.0 %copy-start.14 = (f32[512]{0:T(512)S(1)}, f32[512]{0:T(512)}, u32[]{:S(2)}) copy-start(f32[512]{0:T(512)} %param.44) | copy-start | bytes 6148
  239.0 38.0 %copy-start.19 = (f32[128]{0:T(128)S(1)}, f32[128]{0:T(128)}, u32[]{:S(2)}) copy-start(f32[128]{0:T(128)} %param.42) | copy-start | bytes 1540

commit v4 on v3

--- a/solution.py
+++ b/solution.py
@@ -15,127 +15,154 @@
 big_negative = 1000000000.0
 
 
-def attn_body(q_ref, k_ref, vt_ref, b_ref, extra_ref, o_ref, den_ref, qs, eye, ps, mask_ref, *accs):
-    h = pl.program_id(1)
-
-    @pl.when((pl.program_id(0) == 0) & (h == 0))
-    def _():
-        placed = jnp.sum(extra_ref[0].astype(F32).reshape(8, 16, 8, 128), axis=1)
-        for t in range(8):
-            mask_ref[:, t * 128:(t + 1) * 128] = jnp.broadcast_to(placed[t, 0:1, :], (16, 128)).astype(BF)
-
-    NS = 6
-    sacc = [accs[m * (NS + 4): m * (NS + 4) + NS] for m in range(2)]
-    oacc = [accs[m * (NS + 4) + NS: (m + 1) * (NS + 4)] for m in range(2)]
-    qp = pl.program_id(0)
+def attn_setup(q_ref, qs, eye, slot):
     lane = lax.broadcasted_iota(jnp.int32, (16, 128), 1) // 32
-    masks = [jnp.where(lane == lax.rem(h + r, 4), 1.0, 0.0).astype(BF)[0:1] for r in range(4)]
+    for s in range(4):
+        slot[s] = jnp.where(lane == s, 1.0, 0.0).astype(BF)
     rowi = lax.broadcasted_iota(jnp.int32, (128, 128), 0)
     coli = lax.broadcasted_iota(jnp.int32, (128, 128), 1)
     eye[...] = jnp.where(rowi == coli, 1.0, 0.0).astype(BF)
-    qrow = pl.multiple_of(qp * 512, 512)
-    G = 2
-    for g in range(G):
+
+    def stack(n, _):
+        at = pl.ds(pl.multiple_of(n * 128, 128), 128)
+        for g in range(2):
+            rows = [q_ref[4 * g + r, at, :] for r in range(4)]
+            for h in range(4):
+                s = None
+                for r in range(4):
+                    t = rows[r] * jnp.concatenate([slot[(h + r) % 4]] * 8, axis=0)
+                    s = t if s is None else s + t
+                qs[2 * h + g, at, :] = s
+        return 0
+
+    lax.fori_loop(0, 8, stack, 0)
+
+
+def attn_mask(extra, mask_ref):
+    placed = jnp.sum(extra.astype(F32).reshape(8, 16, 8, 128), axis=1)
+    for t in range(8):
+        mask_ref[:, t * 128:(t + 1) * 128] = jnp.broadcast_to(placed[t, 0:1, :], (16, 128)).astype(BF)
+
+
+def attn_split(it):
+    group = it // 4
+    return lax.rem(group, 2), lax.rem(group // 2, 4), group // 8, lax.rem(it, 4)
+
+
+def attn_loop(first, last, k_ref, vt_ref, b_ref, o_ref, den_ref, qs, eye, slot, ps, mask_ref, sacc, oacc):
+    def push_qb(it, odd):
+        g, h, qp, kp = attn_split(it)
+        at = [pl.ds(pl.multiple_of(qp * 512 + m * 256, 256), 256) for m in range(2)]
         for m in range(2):
-            s = None
-            for r in range(4):
-                t = q_ref[4 * g + r, pl.ds(qrow + m * 256, 256), :] * masks[r]
-                s = t if s is None else s + t
-            qs[g, m * 256:(m + 1) * 256, :] = s
-
-    pend = []
-    LAG = 4
-    unit = [0]
-    def pop_one():
-        (g, kt, r, sl) = pend.pop(0)
+            rhs = jnp.concatenate([qs[2 * h + g, at[m], :], b_ref[8 * h + 2 * kp + odd, at[m], :]], axis=1)
+            pltpu.matmul_push_rhs(rhs, 0, m, transpose=True)
+
+    def pop_scores(par, odd, r, n):
         for m in range(2):
-            s = pltpu.matmul_pop(sacc[m][sl])
-            p = jnp.exp2(s.astype(BF))
-            ps[m, r, (g * 4 + kt // 2) % 2, (kt % 2) * 128:(kt % 2) * 128 + 128, :] = p
-    def push_qb(g, kt):
+            ps[2 * par + m][r, odd * 128:odd * 128 + 128, :] = jnp.exp2(pltpu.matmul_pop(sacc[m][n]).astype(BF))
+
+    def push_p(par, r):
         for m in range(2):
-            rhs = jnp.concatenate([qs[g, m * 256:(m + 1) * 256, :], b_ref[kt, m * 256:(m + 1) * 256, :]], axis=1)
-            pltpu.matmul_push_rhs(rhs, 0, m, transpose=True)
-    def push_p(g, kp, r):
-        for m in range(2):
-            pltpu.matmul_push_rhs(ps[m, r, (g * 4 + kp) % 2], 1, m)
-    def pv(g, kp, r):
-        i = 4 * g + r
-        keep = mask_ref[:, kp * 256:(kp + 1) * 256]
-        lhs = vt_ref[i, 0, :, kp * 256:(kp + 1) * 256] * jnp.concatenate([keep] * 3, axis=0)
+            pltpu.matmul_push_rhs(ps[2 * par + m][r], 1, m)
+
+    def pv(it, r):
+        g, h, _, kp = attn_split(it)
+        at = pl.ds(pl.multiple_of(kp * 256, 256), 256)
+        lhs = vt_ref[4 * g + r, h, :, at] * jnp.concatenate([mask_ref[:, at]] * 3, axis=0)
         for m in range(2):
             pltpu.matmul_acc_lhs(oacc[m][r], lhs, 1)
-    def out(g, r):
-        i = 4 * g + r
-        for m in range(2):
-            o = pltpu.matmul_pop(oacc[m][r])
-            d = o[32:33, :]
-            o_ref[i, :, m * 256:(m + 1) * 256] = o[0:32, :] * (1.0 / d)
-            den_ref[0, i:i + 1, m * 256:(m + 1) * 256] = d
-    pvq = []
-    push_qb(0, 0)
-    steps = [(g, kt) for g in range(G) for kt in range(8)]
-    staged = None
-    for n, (g, kt) in enumerate(steps):
+
+    def result(it):
+        g, h, qp, _ = attn_split(it)
         for r in range(4):
-            i = 4 * g + r
-            lhs = jnp.concatenate([k_ref[i, kt * 128:(kt + 1) * 128, :] * masks[r], eye[...]], axis=1)
-            sl = unit[0] % NS
-            unit[0] += 1
             for m in range(2):
-                pltpu.matmul_acc_lhs(sacc[m][sl], lhs, 0 if r == 0 else None)
-            if r == 0 and n + 1 < len(steps):
-                push_qb(*steps[n + 1])
-            pend.append((g, kt, r, sl))
-            if len(pend) > LAG:
-                pop_one()
-            if r == 1 and pvq and staged is None:
-                staged = pvq.pop(0)
-                push_p(*staged)
-        if staged is not None:
-            done = staged
-            pv(*staged); staged = None
-            if pvq:
-                staged = pvq.pop(0); push_p(*staged); pv(*staged); last = staged; staged = None
-            else:
-                last = done
-            for (gg, kp, r) in ([done] if last is done else [done, last]):
-                if kp == 3:
-                    out(gg, r)
-        if kt % 2 == 1:
-            pvq += [(g, kt // 2, r) for r in range(4)]
-    while pend:
-        pop_one()
-    while pvq:
-        w = pvq.pop(0); push_p(*w); pv(*w)
-        if w[1] == 3: out(w[0], w[2])
-
-def attn_kernel(q_ref, k_ref, vt_ref, b_ref, extra_ref, o_ref, den_ref, qs, eye, ps, mask_ref):
+                o = pltpu.matmul_pop(oacc[m][r])
+                d = o[32:33, :]
+                at = pl.ds(pl.multiple_of(qp * 512 + m * 256, 256), 256)
+                o_ref[4 * g + r, pl.ds(pl.multiple_of(h * 32, 32), 32), at] = o[0:32, :] * (1.0 / d)
+                den_ref[h, r, pl.ds(g, 1), at] = d
+
+    def step(it, par):
+        g, h, qp, kp = attn_split(it)
+        before = lax.max(it - 1, 0)
+        for odd in range(2):
+            for r in range(4):
+                at = pl.ds(pl.multiple_of((2 * kp + odd) * 128, 128), 128)
+                keep = jnp.concatenate([slot[lax.rem(h + r, 4)]] * 8, axis=0)
+                lhs = jnp.concatenate([k_ref[4 * g + r, at, :] * keep, eye[...]], axis=1)
+                if r >= 2:
+                    pop_scores(1 - par if odd == 0 else par, 1 - odd, r, r)
+                for m in range(2):
+                    pltpu.matmul_acc_lhs(sacc[m][r], lhs, 0 if r == 0 else None)
+                if r == 0:
+                    if odd == 0:
+                        push_qb(it, 1)
+                    else:
+                        push_qb(lax.min(it + 1, 63), 0)
+                    push_p(1 - par, 2 * odd)
+            pv(before, 2 * odd)
+            push_p(1 - par, 2 * odd + 1)
+            pv(before, 2 * odd + 1)
+            for r in range(2):
+                pop_scores(par, odd, r, r)
+
+    def body(pair, _):
+        step(2 * pair, 0)
+
+        @pl.when(lax.rem(pair, 2) == 0)
+        def _():
+            result(lax.max(2 * pair - 4, 0))
+
+        step(2 * pair + 1, 1)
+        return 0
+
+    if first == 0:
+        push_qb(0, 0)
+    lax.fori_loop(first // 2, last // 2, body, 0)
+    if last < 64:
+        return
+    par = (last - 1) % 2
+    zero = jnp.zeros((128, 256), BF)
+    for r in (2, 3):
+        pop_scores(par, 1, r, r)
+    for m in range(2):
+        pltpu.matmul_acc_lhs(sacc[m][0], zero, 0)
+        pltpu.matmul_pop(sacc[m][0])
+    for r in range(4):
+        push_p(par, r)
+        pv(last - 1, r)
+    result(last - 1)
+
+
+def attn_kernel(q_ref, k_ref, vt_ref, b_ref, o_ref, den_ref, qs, eye, slot, ps0, ps1, ps2, ps3, mask_ref):
+    ps = (ps0, ps1, ps2, ps3)
+    attn_setup(q_ref, qs, eye, slot)
+    attn_mask(b_ref[32], mask_ref)
     specs = []
     for m in range(2):
-        specs += [pltpu.ACC(m)((128, 256), F32)] * 6 + [pltpu.ACC(m)((48, 256), F32)] * 4
-    pl.run_scoped(lambda *accs: attn_body(q_ref, k_ref, vt_ref, b_ref, extra_ref, o_ref, den_ref, qs, eye, ps, mask_ref, *accs), *specs)
+        specs += [pltpu.ACC(m)((128, 256), F32)] * 4 + [pltpu.ACC(m)((48, 256), F32)] * 4
+
+    def run(*accs):
+        sacc = [accs[8 * m:8 * m + 4] for m in range(2)]
+        oacc = [accs[8 * m + 4:8 * m + 8] for m in range(2)]
+        attn_loop(0, 64, k_ref, vt_ref, b_ref, o_ref, den_ref, qs, eye, slot, ps, mask_ref, sacc, oacc)
+
+    pl.run_scoped(run, *specs)
+
 
 def attention(q, k, vt, b):
+    vmem = pl.BlockSpec(memory_space=pltpu.VMEM)
     return pl.pallas_call(
         attn_kernel,
-        grid=(2, 4),
-        in_specs=[
-            pl.BlockSpec((8, 1024, 128), lambda a, h: (0, 0, 0)),
-            pl.BlockSpec((8, 1024, 128), lambda a, h: (0, 0, 0)),
-            pl.BlockSpec((8, 1, 48, 1024), lambda a, h: (0, h, 0, 0)),
-            pl.BlockSpec((8, 512, 128), lambda a, h: (h, a, 0)),
-            pl.BlockSpec((1, 1024, 128), lambda a, h: (32, 0, 0)),
-        ],
-        out_specs=[
-            pl.BlockSpec((8, 32, 512), lambda a, h: (0, h, a)),
-            pl.BlockSpec((1, 8, 512), lambda a, h: (h, 0, a)),
-        ],
-        out_shape=[jax.ShapeDtypeStruct((8, 128, 1024), F32), jax.ShapeDtypeStruct((4, 8, 1024), F32)],
-        scratch_shapes=[pltpu.VMEM((2, 512, 128), BF), pltpu.VMEM((128, 128), BF), pltpu.VMEM((2, 4, 2, 256, 256), BF), pltpu.VMEM((16, 1024), BF)],
-        compiler_params=pltpu.CompilerParams(vmem_limit_bytes=60 * 2**20),
+        in_specs=[vmem] * 4,
+        out_specs=[vmem] * 2,
+        out_shape=[jax.ShapeDtypeStruct((8, 128, 1024), F32), jax.ShapeDtypeStruct((4, 4, 2, 1024), F32)],
+        scratch_shapes=[
+            pltpu.VMEM((8, 1024, 128), BF), pltpu.VMEM((128, 128), BF), pltpu.VMEM((4, 16, 128), BF),
+            *[pltpu.VMEM((4, 256, 256), BF)] * 4, pltpu.VMEM((16, 1024), BF)],
+        compiler_params=pltpu.CompilerParams(vmem_limit_bytes=40 * 2**20),
         name="tri_attn",
-    )(q, k, vt, b, b)
+    )(q, k, vt, b)
 
 
 MESH_ID = pl.DeviceIdType.MESH

time: 291 us -> 271 us (0.931)
  Pallas kernels: 267 us -> 248 us
    pallas_call x2, Pallas kernels: 86.8 us -> 72.3 us  [attention(): pl.pallas_call(attn_kernel, in_specs=[vmem] * 4, out_specs=[vmem] * 2, ou...]
    pallas_call x2, Pallas kernels: 76.1 us -> 73.1 us  [gather(): pl.pallas_call(gather_kernel, in_specs=[pl.BlockSpec(memory_space=pltpu.V...]
    unnamed x48 -> x60, local copies, waits for them, and re-layouts: 9.08 us -> 9.1 us
where the time goes in v4:
time: 271 us; the launch traced here: 267 us
  Pallas kernels  248 us (92%)
  local copies, waits for them, and re-layouts  13.9 us (5%)
  other arithmetic  2.98 us (1%)
    pallas_call x2, Pallas kernels, post(): pl.pallas_call(post_kernel, in_specs=[vmem] * 4, out_specs=pl.BlockSpec(m...  73.5 us
    pallas_call x2, Pallas kernels, gather(): pl.pallas_call(gather_kernel, in_specs=[pl.BlockSpec(memory_space=pltpu.V...  73.1 us
    pallas_call x2, Pallas kernels, attention(): pl.pallas_call(attn_kernel, in_specs=[vmem] * 4, out_specs=[vmem] * 2, ou...  72.3 us
    pallas_call x2, Pallas kernels, pre(): pl.pallas_call(pre_kernel, grid=(8,), in_specs=[pl.BlockSpec((1, 1024, 12...  18.6 us
    pallas_call x1, Pallas kernels, trans(): pl.pallas_call(trans_kernel, grid=(8,), in_specs=[pl.BlockSpec((1, 1024,...  10.3 us
    unnamed x60, local copies, waits for them, and re-layouts  9.1 us

profile of v4, /device:TPU:12, one launch (start us, length us, event | category | flops | bytes accessed | tf_op | source)
XLA Modules:
  0.0 266.7 jit_solution(4082975745658040146)
XLA Ops:
  0.0 1.0 fusion.53
  1.0 1.0 fusion.54
  1.9 0.1 maximum_bitcast_fusion
  2.1 1.0 fusion.55
  3.0 0.1 maximum_bitcast_fusion.1
  3.1 0.9 fusion.52
  4.1 0.7 convert_element_type.76
  4.9 0.7 pad.7.bw_ref
  5.6 1.6 copy-done.2
  7.2 0.7 copy-done.15
  7.9 0.7 copy-done.16
  8.5 9.2 %tri_pre.2 = (bf16[8,1024,128]{2,1,0:T(8,128)(2,1)S(1)}, bf16[8,1024,128]{2,1,0:T(8,128)(2,1)}, bf16[8,4,48,1024]{3,2,1,0:T(8,128)(2,1)S(1)}, bf16[8,1024,128]{2,1,0:T(8,128)(2,1)S(1)}, bf16[33,8,128]{2,1,0:T(8,128)(2,1)S(1)}) custom-call(bf16[8,1024,128]{2,1,0:T(8,128)(2,1)S(1)} %copy-done.2, f32[1,128]{1,0:T(1,128)S(1)} %bitcast.202, ...), custom_call_target="tpu_custom_call" | custom-call | tf_op jit(solution)/shard_map/tri_pre/pallas_call | solution.py:356
  17.7 36.7 %tri_gather.2 = bf16[33,2,4,2,4,2,8,128]{7,6,5,4,3,2,1,0:T(8,128)(2,1)S(1)} custom-call(bf16[33,8,128]{2,1,0:T(8,128)(2,1)S(1)} %get-tuple-element.248.piece_ref), custom_call_target="tpu_custom_call" | custom-call | tf_op jit(solution)/shard_map/tri_gather/pallas_call | solution.py:289
  54.6 36.2 %tri_attn.2 = (f32[8,128,1024]{2,1,0:T(8,128)}, f32[4,4,2,1024]{3,2,1,0:T(2,128)S(1)}) custom-call(bf16[8,1024,128]{2,1,0:T(8,128)(2,1)S(1)} %get-tuple-element.245.q_ref, bf16[8,1024,128]{2,1,0:T(8,128)(2,1)S(1)} %copy-done.27, bf16[8,4,48,1024]{3,2,1,0:T(8,128)(2,1)S(1)} %get-tuple-element.247.vt_ref, bf16[33,1024,128]{2,1,0:T(8,128)(2,1)S(1)} %bitcast.215), custom_call_target="tpu_custom_call" | custom-call | tf_op jit(solution)/shard_map/tri_attn/pallas_call | solution.py:155
  90.7 0.8 and_reduce_fusion.1
  92.3 0.2 conditional.2
  92.5 1.4 copy-done.3
  93.9 1.6 copy-done.7
  95.5 36.9 %tri_post.2 = bf16[8,128,8,128]{3,2,1,0:T(8,128)(2,1)S(1)} custom-call(f32[8,128,1024]{2,1,0:T(8,128)} %get-tuple-element.827.o_ref, bf16[8,1024,128]{2,1,0:T(8,128)(2,1)S(1)} %copy-done.7, bf16[8,1024,128]{2,1,0:T(8,128)(2,1)S(1)} %copy-done.3, bf16[128,128]{1,0:T(8,128)(2,1)S(1)} %copy-done.12), custom_call_target="tpu_custom_call" | custom-call | tf_op jit(solution)/shard_map/tri_post/pallas_call | solution.py:445
  132.4 0.1 fusion.49
  132.5 0.1 fusion.50
  132.6 0.1 maximum_bitcast_fusion.3
  132.7 0.1 fusion.51
  132.8 0.1 maximum_bitcast_fusion.4
  133.0 9.4 %tri_pre.3 = (bf16[8,1024,128]{2,1,0:T(8,128)(2,1)}, bf16[8,1024,128]{2,1,0:T(8,128)(2,1)}, bf16[8,4,48,1024]{3,2,1,0:T(8,128)(2,1)S(1)}, bf16[8,1024,128]{2,1,0:T(8,128)(2,1)S(1)}, bf16[33,8,128]{2,1,0:T(8,128)(2,1)S(1)}) custom-call(bf16[8,1024,128]{2,1,0:T(8,128)(2,1)S(1)} %bitcast.198, f32[1,128]{1,0:T(1,128)S(1)} %bitcast.204, ...), custom_call_target="tpu_custom_call" | custom-call | tf_op jit(solution)/shard_map/tri_pre/pallas_call | solution.py:356
  142.4 36.3 %tri_gather.3 = bf16[33,2,4,2,4,2,8,128]{7,6,5,4,3,2,1,0:T(8,128)(2,1)S(1)} custom-call(bf16[33,8,128]{2,1,0:T(8,128)(2,1)S(1)} %get-tuple-element.255.piece_ref), custom_call_target="tpu_custom_call" | custom-call | tf_op jit(solution)/shard_map/tri_gather/pallas_call | solution.py:289
  178.8 36.1 %tri_attn.3 = (f32[8,128,1024]{2,1,0:T(8,128)}, f32[4,4,2,1024]{3,2,1,0:T(2,128)S(1)}) custom-call(bf16[8,1024,128]{2,1,0:T(8,128)(2,1)S(1)} %copy-done.24, bf16[8,1024,128]{2,1,0:T(8,128)(2,1)S(1)} %copy-done.25, bf16[8,4,48,1024]{3,2,1,0:T(8,128)(2,1)S(1)} %get-tuple-element.254.vt_ref, bf16[33,1024,128]{2,1,0:T(8,128)(2,1)S(1)} %bitcast.213), custom_call_target="tpu_custom_call" | custom-call | tf_op jit(solution)/shard_map/tri_attn/pallas_call | solution.py:155
  214.9 0.8 and_reduce_fusion
  216.5 1.5 copy-done.1
  218.0 1.6 copy-done.5
  219.7 36.7 %tri_post.3 = bf16[8,128,8,128]{3,2,1,0:T(8,128)(2,1)S(1)} custom-call(f32[8,128,1024]{2,1,0:T(8,128)} %get-tuple-element.828.o_ref, bf16[8,1024,128]{2,1,0:T(8,128)(2,1)S(1)} %copy-done.5, bf16[8,1024,128]{2,1,0:T(8,128)(2,1)S(1)} %bitcast.199, bf16[128,128]{1,0:T(8,128)(2,1)S(1)} %copy-done.13), custom_call_target="tpu_custom_call" | custom-call | tf_op jit(solution)/shard_map/tri_post/pallas_call | solution.py:445
  256.4 10.3 %tri_trans.1 = bf16[8,1024,128]{2,1,0:T(8,128)(2,1)} custom-call(bf16[8,1024,128]{2,1,0:T(8,128)(2,1)S(1)} %bitcast.200, f32[1,128]{1,0:T(1,128)S(1)} %bitcast.206, bf16[128,512]{1,0:T(8,128)(2,1)S(1)} %copy-done.8, f32[1,512]{1,0:T(1,128)S(1)} %bitcast.201, bf16[512,128]{1,0:T(8,128)(2,1)S(1)} %copy-done.9), custom_call_target="tpu_custom_call" | custom-call | tf_op jit(solution)/shard_map/tri_trans/pallas_call | solution.py:474
  (64 shorter events, 0.4 us)
Async XLA Ops:
  4.9 49.6 %copy-start.10 = (f32[8,128]{1,0:T(8,128)}, f32[8,128]{1,0:T(8,128)S(1)}, u32[]{:S(2)}) copy-start(f32[8,128]{1,0:T(8,128)S(1)} %fusion.45.mask_ref) | copy-start | bytes 12292
  5.6 1.6 copy-start.2
  7.2 0.7 copy-start.15
  7.9 0.7 copy-start.16
  17.7 36.8 %copy-start.6 = (bf16[8,1024,128]{2,1,0:T(8,128)(2,1)}, bf16[8,1024,128]{2,1,0:T(8,128)(2,1)S(1)}, u32[]{:S(2)}) copy-start(bf16[8,1024,128]{2,1,0:T(8,128)(2,1)S(1)} %get-tuple-element.251.gate_ref) | copy-start | bytes 6291460
  17.7 36.8 %copy-start.23 = (bf16[8,4,48,1024]{3,2,1,0:T(8,128)(2,1)}, bf16[8,4,48,1024]{3,2,1,0:T(8,128)(2,1)S(1)}, u32[]{:S(2)}) copy-start(bf16[8,4,48,1024]{3,2,1,0:T(8,128)(2,1)S(1)} %get-tuple-element.247.vt_ref) | copy-start | bytes 9437188
  17.7 36.8 %copy-start.26 = (bf16[8,1024,128]{2,1,0:T(8,128)(2,1)}, bf16[8,1024,128]{2,1,0:T(8,128)(2,1)S(1)}, u32[]{:S(2)}) copy-start(bf16[8,1024,128]{2,1,0:T(8,128)(2,1)S(1)} %get-tuple-element.245.q_ref) | copy-start | bytes 6291460
  17.7 36.8 %copy-start.27 = (bf16[8,1024,128]{2,1,0:T(8,128)(2,1)S(1)}, bf16[8,1024,128]{2,1,0:T(8,128)(2,1)}, u32[]{:S(2)}) copy-start(bf16[8,1024,128]{2,1,0:T(8,128)(2,1)} %get-tuple-element.246.k_ref) | copy-start | bytes 6291460
  54.5 36.2 %copy-start.21 = (bf16[33,2,4,2,4,2,8,128]{7,6,5,4,3,2,1,0:T(8,128)(2,1)}, bf16[33,2,4,2,4,2,8,128]{7,6,5,4,3,2,1,0:T(8,128)(2,1)S(1)}, u32[]{:S(2)}) copy-start(bf16[33,2,4,2,4,2,8,128]{7,6,5,4,3,2,1,0:T(8,128)(2,1)S(1)} %tri_gather.2) | copy-start | bytes 25952260
  92.3 1.6 copy-start.3
  92.3 1.6 copy-start.12
  93.9 1.6 copy-start.7
  95.5 36.9 %copy-start.28 = (bf16[128,512]{1,0:T(8,128)(2,1)S(1)}, bf16[128,512]{1,0:T(8,128)(2,1)}, u32[]{:S(2)}) copy-start(bf16[128,512]{1,0:T(8,128)(2,1)} %param.38) | copy-start | bytes 393220
  95.5 37.5 %copy-start.29 = (bf16[128,4]{0,1:T(4,128)(2,1)S(1)}, bf16[128,4]{0,1:T(4,128)(2,1)}, u32[]{:S(2)}) copy-start(bf16[128,4]{0,1:T(4,128)(2,1)} %param.40) | copy-start | bytes 3076
  95.5 37.5 %copy-start.11 = (f32[8,128]{1,0:T(8,128)S(1)}, f32[8,128]{1,0:T(8,128)}, u32[]{:S(2)}) copy-start(f32[8,128]{1,0:T(8,128)} %copy-done.10) | copy-start | bytes 12292
  95.5 37.5 %copy-start.17 = (f32[128]{0:T(128)S(1)}, f32[128]{0:T(128)}, u32[]{:S(2)}) copy-start(f32[128]{0:T(128)} %param.37) | copy-start | bytes 1540
  95.5 37.5 %copy-start.18 = (f32[128]{0:T(128)S(1)}, f32[128]{0:T(128)}, u32[]{:S(2)}) copy-start(f32[128]{0:T(128)} %param.39) | copy-start | bytes 1540
  132.3 46.4 %copy-start = (bf16[8,128,8,128]{3,2,1,0:T(8,128)(2,1)}, bf16[8,128,8,128]{3,2,1,0:T(8,128)(2,1)S(1)}, u32[]{:S(2)}) copy-start(bf16[8,128,8,128]{3,2,1,0:T(8,128)(2,1)S(1)} %tri_post.2) | copy-start | bytes 6291460
  142.4 36.4 %copy-start.4 = (bf16[8,1024,128]{2,1,0:T(8,128)(2,1)}, bf16[8,1024,128]{2,1,0:T(8,128)(2,1)S(1)}, u32[]{:S(2)}) copy-start(bf16[8,1024,128]{2,1,0:T(8,128)(2,1)S(1)} %get-tuple-element.258.gate_ref) | copy-start | bytes 6291460
  142.4 36.4 %copy-start.22 = (bf16[8,4,48,1024]{3,2,1,0:T(8,128)(2,1)}, bf16[8,4,48,1024]{3,2,1,0:T(8,128)(2,1)S(1)}, u32[]{:S(2)}) copy-start(bf16[8,4,48,1024]{3,2,1,0:T(8,128)(2,1)S(1)} %get-tuple-element.254.vt_ref) | copy-start | bytes 9437188
  142.4 36.4 %copy-start.24 = (bf16[8,1024,128]{2,1,0:T(8,128)(2,1)S(1)}, bf16[8,1024,128]{2,1,0:T(8,128)(2,1)}, u32[]{:S(2)}) copy-start(bf16[8,1024,128]{2,1,0:T(8,128)(2,1)} %get-tuple-element.252.q_ref) | copy-start | bytes 6291460
  142.4 36.4 %copy-start.25 = (bf16[8,1024,128]{2,1,0:T(8,128)(2,1)S(1)}, bf16[8,1024,128]{2,1,0:T(8,128)(2,1)}, u32[]{:S(2)}) copy-start(bf16[8,1024,128]{2,1,0:T(8,128)(2,1)} %get-tuple-element.253.k_ref) | copy-start | bytes 6291460
  178.8 36.2 %copy-start.20 = (bf16[33,2,4,2,4,2,8,128]{7,6,5,4,3,2,1,0:T(8,128)(2,1)}, bf16[33,2,4,2,4,2,8,128]{7,6,5,4,3,2,1,0:T(8,128)(2,1)S(1)}, u32[]{:S(2)}) copy-start(bf16[33,2,4,2,4,2,8,128]{7,6,5,4,3,2,1,0:T(8,128)(2,1)S(1)} %tri_gather.3) | copy-start | bytes 25952260
  216.5 1.6 copy-start.1
  216.5 1.6 copy-start.13
  218.0 1.6 copy-start.5
  219.6 36.7 %copy-start.8 = (bf16[128,512]{1,0:T(8,128)(2,1)S(1)}, bf16[128,512]{1,0:T(8,128)(2,1)}, u32[]{:S(2)}) copy-start(bf16[128,512]{1,0:T(8,128)(2,1)} %w1_ref.1) | copy-start | bytes 393220
  219.6 36.7 %copy-start.9 = (bf16[512,128]{1,0:T(8,128)(2,1)S(1)}, bf16[512,128]{1,0:T(8,128)(2,1)}, u32[]{:S(2)}) copy-start(bf16[512,128]{1,0:T(8,128)(2,1)} %w2_ref.1) | copy-start | bytes 393220
  219.6 36.7 %copy-start.14 = (f32[512]{0:T(512)S(1)}, f32[512]{0:T(512)}, u32[]{:S(2)}) copy-start(f32[512]{0:T(512)} %param.44) | copy-start | bytes 6148
  219.6 36.7 %copy-start.19 = (f32[128]{0:T(128)S(1)}, f32[128]{0:T(128)}, u32[]{:S(2)}) copy-start(f32[128]{0:T(128)} %param.42) | copy-start | bytes 1540

commit v5 on v4

--- a/solution.py
+++ b/solution.py
@@ -13,6 +13,137 @@
 LOG2E = 1.4426950408889634
 LN2 = 0.6931471805599453
 big_negative = 1000000000.0
+
+
+MESH_ID = pl.DeviceIdType.MESH
+ORDERS = ((0, 1, 2), (1, 2, 0), (2, 0, 1))
+EXTRA = 26
+PLANES = 36
+EARLY = 43
+
+
+def plane(h, t):
+    if isinstance(t, int):
+        return 12 * (t // 3) + 3 * h + t % 3
+    return 12 * (t // 3) + 3 * h + lax.rem(t, 3)
+
+
+class Torus:
+    def __init__(self, piece_ref, full, send_sem, recv_sem):
+        gx, gy = lax.axis_index("gx"), lax.axis_index("gy")
+        self.core = lax.rem(gx, 2)
+        self.here = (lax.rem(gx // 2, 4), gy // 2, lax.rem(gy, 2) * 2 + gx // 8)
+        self.piece, self.full, self.send_sem, self.recv_sem = piece_ref, full, send_sem, recv_sem
+        self.partner = self.device(self.here, 1 - self.core)
+        self.sent = []
+
+    def device(self, pos, c):
+        px, py, pz = pos
+        return ((lax.rem(pz, 2) * 4 + px) * 2 + c, py * 2 + pz // 2)
+
+    def moved(self, dim, step):
+        pos = list(self.here)
+        pos[dim] = lax.rem(pos[dim] + step, 4)
+        return tuple(pos)
+
+    def region(self, lo, n, pos, done, other=False):
+        px, py, pz = pos
+        zl = slice(None) if 2 in done else lax.rem(pz, 2)
+        zh = slice(None) if 2 in done else pz // 2
+        xi = slice(None) if 0 in done else px
+        yi = slice(None) if 1 in done else py
+        return self.full.at[pl.ds(lo, n), zl, xi, 1 - self.core if other else self.core, yi, zh]
+
+    def send(self, slot, lo, n, pos, done, dev, first=False):
+        spot = self.region(lo, n, pos, done)
+        pltpu.make_async_remote_copy(
+            src_ref=self.piece.at[pl.ds(lo, n)] if first else spot, dst_ref=spot, send_sem=self.send_sem.at[slot],
+            recv_sem=self.recv_sem.at[slot], device_id=dev, device_id_type=MESH_ID).start()
+
+    def wait(self, slot, lo, n, pos, done, other=False, sent=False):
+        spot = self.region(lo, n, pos, done, other)
+        c = pltpu.make_async_remote_copy(
+            src_ref=spot, dst_ref=spot, send_sem=self.send_sem.at[slot], recv_sem=self.recv_sem.at[slot],
+            device_id=self.partner, device_id_type=MESH_ID)
+        c.wait_send() if sent else c.wait_recv()
+
+    def barrier(self):
+        barrier = pltpu.get_barrier_semaphore()
+        peers = [self.device(self.moved(d, s), self.core) for d in range(3) for s in (1, 3)] + [self.partner]
+        for peer in peers:
+            pl.semaphore_signal(barrier, inc=1, device_id=peer, device_id_type=MESH_ID)
+        px, py, pz = self.here
+        self.full[:, lax.rem(pz, 2), px, self.core, py, pz // 2] = self.piece[...]
+        pl.semaphore_wait(barrier, 7)
+
+    def outward(self, base, o, stage, lo, n):
+        dim, done = ORDERS[o][stage], ORDERS[o][:stage]
+        self.send(base, lo, n, self.here, done, self.device(self.moved(dim, 1), self.core), stage == 0)
+        self.send(base + 1, lo, n, self.here, done, self.device(self.moved(dim, 3), self.core), stage == 0)
+
+    def onward(self, base, o, stage, lo, n, n1):
+        dim, done = ORDERS[o][stage], ORDERS[o][:stage]
+        left, right = self.moved(dim, 3), self.moved(dim, 1)
+        self.wait(base, lo, n, left, done)
+        self.send(base + 2, lo, n1, left, done, self.device(right, self.core))
+        self.wait(base + 1, lo, n, right, done)
+        self.send(base + 3, lo + n1, n - n1, right, done, self.device(left, self.core))
+        self.send(base + 4, lo, n, left, done, self.partner)
+        self.send(base + 5, lo, n, right, done, self.partner)
+
+    def closing(self, base, o, stage, lo, n, n1):
+        dim, done = ORDERS[o][stage], ORDERS[o][:stage]
+        far = self.moved(dim, 2)
+        self.wait(base + 2, lo, n1, far, done)
+        self.wait(base + 3, lo + n1, n - n1, far, done)
+        self.send(base + 6, lo, n, far, done, self.partner)
+
+    def shared(self, base, o, stage, lo, n):
+        dim, done = ORDERS[o][stage], ORDERS[o][:stage]
+        for k, step in ((4, 3), (5, 1), (6, 2)):
+            self.wait(base + k, lo, n, self.moved(dim, step), done, True)
+
+    def settled(self, base, o, stage, lo, n, n1):
+        done = ORDERS[o][:stage]
+        for k, size in ((0, n), (1, n), (2, n1), (3, n - n1), (4, n), (5, n), (6, n)):
+            self.wait(base + k, lo, size, self.here, done, False, True)
+
+    def early(self):
+        for stage in range(2):
+            bases = [21 * stage + 7 * o for o in range(3)]
+            for o in range(3):
+                self.outward(bases[o], o, stage, 12 * o, 12)
+            if stage == 0:
+                self.send(42, 0, PLANES, self.here, (), self.partner, True)
+            for o in range(3):
+                self.onward(bases[o], o, stage, 12 * o, 12, 6)
+            for o in range(3):
+                self.closing(bases[o], o, stage, 12 * o, 12, 6)
+
+    def sizes(self, first):
+        return ((3, 2), (3, 1), (3, 1) if first else (2, 1))
+
+    def late(self, action, h, first=False):
+        for o, (n, n1) in enumerate(self.sizes(first)):
+            base, lo = EARLY + 21 * h + 7 * o, 12 * o + 3 * h
+            if action in ("outward", "shared"):
+                getattr(self, action)(base, o, 2, lo, n)
+            else:
+                getattr(self, action)(base, o, 2, lo, n, n1)
+
+    def early_shared(self):
+        self.wait(42, 0, PLANES, self.here, (), True)
+        for stage in range(2):
+            for o in range(3):
+                self.shared(21 * stage + 7 * o, o, stage, 12 * o, 12)
+
+    def finish(self):
+        self.wait(42, 0, PLANES, self.here, (), False, True)
+        for stage in range(2):
+            for o in range(3):
+                self.settled(21 * stage + 7 * o, o, stage, 12 * o, 12, 6)
+        for h in range(4):
+            self.late("settled", h, h == 0)
 
 
 def attn_setup(q_ref, qs, eye, slot):
@@ -49,12 +180,12 @@
     return lax.rem(group, 2), lax.rem(group // 2, 4), group // 8, lax.rem(it, 4)
 
 
-def attn_loop(first, last, k_ref, vt_ref, b_ref, o_ref, den_ref, qs, eye, slot, ps, mask_ref, sacc, oacc):
+def attn_loop(first, last, comm, k_ref, vt_ref, b_ref, o_ref, den_ref, qs, eye, slot, ps, mask_ref, sacc, oacc):
     def push_qb(it, odd):
         g, h, qp, kp = attn_split(it)
         at = [pl.ds(pl.multiple_of(qp * 512 + m * 256, 256), 256) for m in range(2)]
         for m in range(2):
-            rhs = jnp.concatenate([qs[2 * h + g, at[m], :], b_ref[8 * h + 2 * kp + odd, at[m], :]], axis=1)
+            rhs = jnp.concatenate([qs[2 * h + g, at[m], :], b_ref[plane(h, 2 * kp + odd), at[m], :]], axis=1)
             pltpu.matmul_push_rhs(rhs, 0, m, transpose=True)
 
     def pop_scores(par, odd, r, n):
@@ -108,6 +239,7 @@
 
     def body(pair, _):
         step(2 * pair, 0)
+        comm(pair + 1)
 
         @pl.when(lax.rem(pair, 2) == 0)
         def _():
@@ -134,10 +266,50 @@
     result(last - 1)
 
 
-def attn_kernel(q_ref, k_ref, vt_ref, b_ref, o_ref, den_ref, qs, eye, slot, ps0, ps1, ps2, ps3, mask_ref):
+def attn_kernel(piece_ref, q_hbm, k_hbm, vt_hbm, o_ref, den_ref, full_hbm, full, q_ref, k_ref, vt_ref, qs, eye, slot, ps0, ps1, ps2, ps3, mask_ref, send_sem, recv_sem, load_sem, out_sem):
     ps = (ps0, ps1, ps2, ps3)
+    loads = [pltpu.make_async_copy(a, b, load_sem.at[n]) for n, (a, b) in enumerate(((q_hbm, q_ref), (k_hbm, k_ref), (vt_hbm, vt_ref)))]
+    for c in loads:
+        c.start()
+    torus = Torus(piece_ref, full, send_sem, recv_sem)
+    torus.barrier()
+    torus.early()
+    torus.late("outward", 0, True)
+    torus.late("outward", 1)
+    for c in loads:
+        c.wait()
     attn_setup(q_ref, qs, eye, slot)
-    attn_mask(b_ref[32], mask_ref)
+    torus.late("onward", 0, True)
+    torus.late("outward", 2)
+    torus.late("onward", 1)
+    torus.late("outward", 3)
+    torus.late("closing", 0, True)
+    torus.early_shared()
+    torus.late("shared", 0, True)
+    b_ref = full.reshape(PLANES, 1024, 128)
+    attn_mask(b_ref[EXTRA], mask_ref)
+
+    out = pltpu.make_async_copy(full, full_hbm, out_sem)
+
+    def comm(pair):
+        @pl.when(pair == 16)
+        def _():
+            out.start()
+
+        @pl.when(pair < 13)
+        def _():
+            @pl.when((pair == 1) | (pair == 3))
+            def _():
+                torus.late("onward", (pair + 3) // 2)
+
+            @pl.when(lax.rem(pair, 4) == 2)
+            def _():
+                torus.late("closing", (pair + 2) // 4)
+
+            @pl.when((pair > 0) & (lax.rem(pair, 4) == 0))
+            def _():
+                torus.late("shared", pair // 4)
+
     specs = []
     for m in range(2):
         specs += [pltpu.ACC(m)((128, 256), F32)] * 4 + [pltpu.ACC(m)((48, 256), F32)] * 4
@@ -145,162 +317,45 @@
     def run(*accs):
         sacc = [accs[8 * m:8 * m + 4] for m in range(2)]
         oacc = [accs[8 * m + 4:8 * m + 8] for m in range(2)]
-        attn_loop(0, 64, k_ref, vt_ref, b_ref, o_ref, den_ref, qs, eye, slot, ps, mask_ref, sacc, oacc)
+        attn_loop(0, 64, comm, k_ref, vt_ref, b_ref, o_ref, den_ref, qs, eye, slot, ps, mask_ref, sacc, oacc)
 
     pl.run_scoped(run, *specs)
-
-
-def attention(q, k, vt, b):
+    torus.finish()
+    out.wait()
+
+
+def attention(piece, q, k, vt, collective_id):
     vmem = pl.BlockSpec(memory_space=pltpu.VMEM)
-    return pl.pallas_call(
+    hbm = pl.BlockSpec(memory_space=pl.ANY)
+    shape = (PLANES, 2, 4, 2, 4, 2, 8, 128)
+    o, den, full = pl.pallas_call(
         attn_kernel,
-        in_specs=[vmem] * 4,
-        out_specs=[vmem] * 2,
-        out_shape=[jax.ShapeDtypeStruct((8, 128, 1024), F32), jax.ShapeDtypeStruct((4, 4, 2, 1024), F32)],
-        scratch_shapes=[
-            pltpu.VMEM((8, 1024, 128), BF), pltpu.VMEM((128, 128), BF), pltpu.VMEM((4, 16, 128), BF),
-            *[pltpu.VMEM((4, 256, 256), BF)] * 4, pltpu.VMEM((16, 1024), BF)],
-        compiler_params=pltpu.CompilerParams(vmem_limit_bytes=40 * 2**20),
-        name="tri_attn",
-    )(q, k, vt, b)
-
-
-MESH_ID = pl.DeviceIdType.MESH
-ORDERS = ((0, 1, 2), (1, 2, 0), (2, 0, 1))
-
-
-def gather_kernel(piece_ref, out_ref, full, send_sem, recv_sem, out_sem):
-    gx, gy = lax.axis_index("gx"), lax.axis_index("gy")
-    core = lax.rem(gx, 2)
-    x = lax.rem(gx // 2, 4)
-    y = gy // 2
-    z = lax.rem(gy, 2) * 2 + gx // 8
-    here = (x, y, z)
-
-    def device(pos, c):
-        px, py, pz = pos
-        return ((lax.rem(pz, 2) * 4 + px) * 2 + c, py * 2 + pz // 2)
-
-    def moved(dim, step):
-        pos = list(here)
-        pos[dim] = lax.rem(pos[dim] + step + 4, 4)
-        return tuple(pos)
-
-    def region(lo, hi, pos, done):
-        px, py, pz = pos
-        zl = slice(None) if 2 in done else lax.rem(pz, 2)
-        zh = slice(None) if 2 in done else pz // 2
-        xi = slice(None) if 0 in done else px
-        yi = slice(None) if 1 in done else py
-        return full.at[lo:hi, zl, xi, core, yi, zh]
-
-    barrier = pltpu.get_barrier_semaphore()
-    partner = device(here, 1 - core)
-    peers = [device(moved(d, s), core) for d in range(3) for s in (1, 3)] + [partner]
-    for peer in peers:
-        pl.semaphore_signal(barrier, inc=1, device_id=peer, device_id_type=MESH_ID)
-    full[:, lax.rem(z, 2), x, core, y, z // 2] = piece_ref[...]
-    pl.semaphore_wait(barrier, 7)
-
-    slots = [0]
-    started = []
-
-    def copy(src, dst, dev):
-        n = slots[0]
-        slots[0] += 1
-        return pltpu.make_async_remote_copy(
-            src_ref=src, dst_ref=dst, send_sem=send_sem.at[n], recv_sem=recv_sem.at[n],
-            device_id=dev, device_id_type=MESH_ID)
-
-    def send(lo, hi, pos, done, dev, first=False):
-        spot = region(lo, hi, pos, done)
-        c = copy(piece_ref.at[lo:hi] if first else spot, spot, dev)
-        c.start()
-        started.append(c)
-        return c
-
-    def arrival(n, lo, hi, pos, done):
-        spot = region(lo, hi, pos, done)
-        pltpu.make_async_remote_copy(
-            src_ref=spot, dst_ref=spot, send_sem=send_sem.at[n], recv_sem=recv_sem.at[n],
-            device_id=partner, device_id_type=MESH_ID).wait_recv()
-
-    partner_waits = []
-
-    def share(lo, hi, pos, done, first=False):
-        n = slots[0]
-        send(lo, hi, pos, done, partner, first)
-        partner_waits.append((n, lo, hi, pos, done))
-
-    for stage in range(3):
-        tags = []
-        for part in range(3):
-            order = ORDERS[part]
-            dim, done = order[stage], order[:stage]
-            lo, hi = 11 * part, 11 * part + 11
-            right, left = device(moved(dim, 1), core), device(moved(dim, 3), core)
-            n = slots[0]
-            send(lo, hi, here, done, right, stage == 0)
-            send(lo, hi, here, done, left, stage == 0)
-            tags.append((n, lo, hi, dim, done, right, left))
-        if stage == 0:
-            share(0, 33, here, (), True)
-        halves = []
-        for n, lo, hi, dim, done, right, left in tags:
-            mid = lo + 6
-            h = slots[0]
-            arrival(n, lo, hi, moved(dim, 3), done)
-            send(lo, mid, moved(dim, 3), done, right)
-            arrival(n + 1, lo, hi, moved(dim, 1), done)
-            send(mid, hi, moved(dim, 1), done, left)
-            share(lo, hi, moved(dim, 3), done)
-            share(lo, hi, moved(dim, 1), done)
-            halves.append((h, lo, mid, hi, dim, done))
-        for h, lo, mid, hi, dim, done in halves:
-            arrival(h, lo, mid, moved(dim, 2), done)
-            arrival(h + 1, mid, hi, moved(dim, 2), done)
-            share(lo, hi, moved(dim, 2), done)
-
-    def partner_region(lo, hi, pos, done):
-        px, py, pz = pos
-        zl = slice(None) if 2 in done else lax.rem(pz, 2)
-        zh = slice(None) if 2 in done else pz // 2
-        xi = slice(None) if 0 in done else px
-        yi = slice(None) if 1 in done else py
-        return full.at[lo:hi, zl, xi, 1 - core, yi, zh]
-
-    for n, lo, hi, pos, done in partner_waits:
-        spot = partner_region(lo, hi, pos, done)
-        pltpu.make_async_remote_copy(
-            src_ref=spot, dst_ref=spot, send_sem=send_sem.at[n], recv_sem=recv_sem.at[n],
-            device_id=partner, device_id_type=MESH_ID).wait_recv()
-    outs = [pltpu.make_async_copy(full.at[11 * p:11 * p + 11], out_ref.at[11 * p:11 * p + 11], out_sem.at[p]) for p in range(3)]
-    for c in outs:
-        c.start()
-    for c in started:
-        c.wait_send()
-    for c in outs:
-        c.wait()
-
-
-def gather(piece, collective_id):
-    shape = (33, 2, 4, 2, 4, 2, 8, 128)
-    n = 64
-    out = pl.pallas_call(
-        gather_kernel,
-        in_specs=[pl.BlockSpec(memory_space=pltpu.VMEM)],
-        out_specs=pl.BlockSpec(memory_space=pl.ANY),
-        out_shape=jax.ShapeDtypeStruct(shape, BF),
+        in_specs=[vmem, hbm, hbm, hbm],
+        out_specs=[vmem, vmem, hbm],
+        out_shape=[
+            jax.ShapeDtypeStruct((8, 128, 1024), F32),
+            jax.ShapeDtypeStruct((4, 4, 2, 1024), F32),
+            jax.ShapeDtypeStruct(shape, BF),
+        ],
         scratch_shapes=[
             pltpu.VMEM(shape, BF),
-            pltpu.SemaphoreType.DMA((n,)),
-            pltpu.SemaphoreType.DMA((n,)),
+            pltpu.VMEM((8, 1024, 128), BF),
+            pltpu.VMEM((8, 1024, 128), BF),
+            pltpu.VMEM((8, 4, 48, 1024), BF),
+            pltpu.VMEM((8, 1024, 128), BF),
+            pltpu.VMEM((128, 128), BF),
+            pltpu.VMEM((4, 16, 128), BF),
+            *[pltpu.VMEM((4, 256, 256), BF)] * 4,
+            pltpu.VMEM((16, 1024), BF),
+            pltpu.SemaphoreType.DMA((EARLY + 84,)),
+            pltpu.SemaphoreType.DMA((EARLY + 84,)),
             pltpu.SemaphoreType.DMA((3,)),
+            pltpu.SemaphoreType.DMA,
         ],
-        compiler_params=pltpu.CompilerParams(collective_id=collective_id, has_side_effects=True, vmem_limit_bytes=24 * 2**20),
-        name="tri_gather",
-    )(piece)
-    return out.reshape(33, 1024, 128)
+        compiler_params=pltpu.CompilerParams(collective_id=collective_id, has_side_effects=True, vmem_limit_bytes=44 * 2**20),
+        name="tri_attn",
+    )(piece, q, k, vt)
+    return o, den, full.reshape(PLANES, 1024, 128)
 
 
 def layer_norm(x, gain):
@@ -315,7 +370,8 @@
 
     @pl.when(i == 0)
     def _():
-        scr[32] = mask_ref[...]
+        scr[...] = jnp.zeros((PLANES, 8, 128), F32)
+        scr[EXTRA] = mask_ref[...]
 
     a = layer_norm(z_ref[0].astype(F32), gain_ref[...])
     qk = jnp.dot(a, wqk_ref[0], preferred_element_type=F32)
@@ -334,9 +390,9 @@
     b = (b - m) * LOG2E
     for h in range(4):
         for kt in range(8):
-            scr[8 * h + kt, pl.ds(i, 1), :] = b[h:h + 1, kt * 128:(kt + 1) * 128]
+            scr[plane(h, kt), pl.ds(i, 1), :] = b[h:h + 1, kt * 128:(kt + 1) * 128]
     lane = lax.broadcasted_iota(jnp.int32, (4, 128), 1)
-    scr[32, 1:5, :] = jnp.where(lane == i, m[0:4], scr[32, 1:5, :])
+    scr[EXTRA, 1:5, :] = jnp.where(lane == i, m[0:4], scr[EXTRA, 1:5, :])
 
     @pl.when(i == 7)
     def _():
@@ -370,16 +426,16 @@
             pl.BlockSpec((1, 1024, 128), row),
             pl.BlockSpec((1, 4, 48, 1024), lambda i: (i, 0, 0, 0)),
             pl.BlockSpec((1, 1024, 128), row),
-            pl.BlockSpec((33, 8, 128), lambda i: (0, 0, 0)),
+            pl.BlockSpec((PLANES, 8, 128), lambda i: (0, 0, 0)),
         ],
         out_shape=[
             jax.ShapeDtypeStruct((8, 1024, 128), BF),
             jax.ShapeDtypeStruct((8, 1024, 128), BF),
             jax.ShapeDtypeStruct((8, 4, 48, 1024), BF),
             jax.ShapeDtypeStruct((8, 1024, 128), BF),
-            jax.ShapeDtypeStruct((33, 8, 128), BF),
+            jax.ShapeDtypeStruct((PLANES, 8, 128), BF),
         ],
-        scratch_shapes=[pltpu.VMEM((33, 8, 128), F32)],
+        scratch_shapes=[pltpu.VMEM((PLANES, 8, 128), F32)],
         compiler_params=pltpu.CompilerParams(vmem_limit_bytes=48 * 2**20),
         name="tri_pre",
     )(z, gain.reshape(1, 128), wqk, wvg, bwt, gate_bias.reshape(1, 128), mask_tile)
@@ -489,11 +545,11 @@
 
 
 def exact_attention(q, k, vt, full):
-    extra = full[32].reshape(128, 8, 128)
+    extra = full[EXTRA].reshape(128, 8, 128)
     mask = jnp.sum(extra[:, 0].reshape(8, 16, 128).astype(F32), axis=1).reshape(1024)
     maxima = jnp.transpose(extra[:, 1:5, :8], (1, 0, 2)).reshape(4, 1024).astype(F32)
     key_bias = (mask - 1.0) * big_negative
-    b = full[:32].reshape(4, 8, 1024, 128)
+    b = jnp.stack([jnp.stack([full[12 * (t // 3) + 3 * h + t % 3] for t in range(8)]) for h in range(4)])
     orders = jnp.array([[(h + i) % 4 for h in range(4)] for i in range(4)])
 
     def per_row(operands):
@@ -518,8 +574,7 @@
 
 def phase(z, mask_tile, gain, proj, gate_bias, bias_w, out_w, collective_id):
     q, k, vt, gate, piece = pre(z, gain, proj, bias_w, gate_bias, mask_tile)
-    full = gather(piece, collective_id)
-    o, den = attention(q, k, vt, full)
+    o, den, full = attention(piece, q, k, vt, collective_id)
     fine = jnp.all((den > 2.0 ** -60) & (den < 2.0 ** 100))
     o = lax.cond(fine, lambda: o, lambda: exact_attention(q, k, vt, full))
     return post(o, gate, z, out_w, 2 + collective_id)

time: 271 us -> 259 us (0.956)
  Pallas kernels: 248 us -> 236 us
    pallas_call x4 -> x2, Pallas kernels: 145 us -> 136 us  [attention(): pl.pallas_call(attn_kernel, in_specs=[vmem, hbm, hbm, hbm], out_specs=[vm...]
    unnamed x60 -> x56, local copies, waits for them, and re-layouts: 9.1 us -> 10.4 us
where the time goes in v5:
time: 259 us; the launch traced here: 256 us
  Pallas kernels  236 us (91%)
  local copies, waits for them, and re-layouts  15.2 us (6%)
  other arithmetic  2.76 us (1%)
    pallas_call x2, Pallas kernels, attention(): pl.pallas_call(attn_kernel, in_specs=[vmem, hbm, hbm, hbm], out_specs=[vm...  136 us
    pallas_call x2, Pallas kernels, post(): pl.pallas_call(post_kernel, in_specs=[vmem] * 4, out_specs=pl.BlockSpec(m...  73.4 us
    pallas_call x2, Pallas kernels, pre(): pl.pallas_call(pre_kernel, grid=(8,), in_specs=[pl.BlockSpec((1, 1024, 12...  16.8 us
    unnamed x56, local copies, waits for them, and re-layouts  10.4 us
    pallas_call x1, Pallas kernels, trans(): pl.pallas_call(trans_kernel, grid=(8,), in_specs=[pl.BlockSpec((1, 1024,...  10.3 us

profile of v5, /device:TPU:12, one launch (start us, length us, event | category | flops | bytes accessed | tf_op | source)
XLA Modules:
  0.0 255.8 jit_solution(7242118423301764450)
XLA Ops:
  0.0 1.0 fusion.57
  1.0 1.0 fusion.58
  1.9 0.1 maximum_bitcast_fusion.8
  2.1 1.0 fusion.59
  3.0 0.1 maximum_bitcast_fusion.9
  3.1 0.9 fusion.56
  4.1 0.7 convert_element_type.76
  4.7 0.1 broadcast_in_dim.40
  4.9 0.7 pad.7.bw_ref
  5.6 1.6 copy-done.2
  7.2 0.7 copy-done.15
  7.9 0.7 copy-done.16
  8.5 8.4 %tri_pre.2 = (bf16[8,1024,128]{2,1,0:T(8,128)(2,1)S(1)}, bf16[8,1024,128]{2,1,0:T(8,128)(2,1)S(1)}, bf16[8,4,48,1024]{3,2,1,0:T(8,128)(2,1)S(1)}, bf16[8,1024,12...) custom-call(bf16[8,1024,128]{2,1,0:T(8,128)(2,1)S(1)} %copy-done.2, f32[1,128]{1,0:T(1,128)S(1)} %bitcast.234, ...), custom_call_target="tpu_custom_call" | custom-call | tf_op jit(solution)/shard_map/tri_pre/pallas_call | solution.py:412
  16.9 1.3 copy-done.6
  18.3 67.6 %tri_attn.2 = (f32[8,128,1024]{2,1,0:T(8,128)}, f32[4,4,2,1024]{3,2,1,0:T(2,128)S(1)}, bf16[36,2,4,2,4,2,8,128]{7,6,5,4,3,2,1,0:T(8,128)(2,1)}) custom-call(bf16[36,8,128]{2,1,0:T(8,128)(2,1)S(1)} %get-tuple-element.249.piece_ref, bf16[8,1024,128]{2,1,0:T(8,128)(2,1)S(1)} %get-tuple-element.250.q_hbm, bf16[8,1024,128]{2,1,0:T(8,128)(2,1)S(1)} %get-tuple-element.251.k_hbm, ...), custom_call_target="tpu_custom_call" | custom-call | tf_op jit(solution)/shard_map/tri_attn/pallas_call | solution.py:331
  85.9 0.7 and_reduce_fusion.1
  87.2 0.2 conditional.2
  87.4 1.4 copy-done.3
  88.8 1.6 copy-done.7
  90.4 36.6 %tri_post.2 = bf16[8,128,8,128]{3,2,1,0:T(8,128)(2,1)S(1)} custom-call(f32[8,128,1024]{2,1,0:T(8,128)} %get-tuple-element.885.o_ref, bf16[8,1024,128]{2,1,0:T(8,128)(2,1)S(1)} %copy-done.7, bf16[8,1024,128]{2,1,0:T(8,128)(2,1)S(1)} %copy-done.3, bf16[128,128]{1,0:T(8,128)(2,1)S(1)} %copy-done.12), custom_call_target="tpu_custom_call" | custom-call | tf_op jit(solution)/shard_map/tri_post/pallas_call | solution.py:501
  127.0 0.1 fusion.53
  127.1 0.1 fusion.54
  127.2 0.1 maximum_bitcast_fusion.11
  127.3 0.1 fusion.55
  127.4 0.1 maximum_bitcast_fusion.12
  127.6 8.4 %tri_pre.3 = (bf16[8,1024,128]{2,1,0:T(8,128)(2,1)S(1)}, bf16[8,1024,128]{2,1,0:T(8,128)(2,1)S(1)}, bf16[8,4,48,1024]{3,2,1,0:T(8,128)(2,1)S(1)}, bf16[8,1024,12...) custom-call(bf16[8,1024,128]{2,1,0:T(8,128)(2,1)S(1)} %bitcast.230, f32[1,128]{1,0:T(1,128)S(1)} %bitcast.236, ...), custom_call_target="tpu_custom_call" | custom-call | tf_op jit(solution)/shard_map/tri_pre/pallas_call | solution.py:412
  136.1 67.9 %tri_attn.3 = (f32[8,128,1024]{2,1,0:T(8,128)}, f32[4,4,2,1024]{3,2,1,0:T(2,128)S(1)}, bf16[36,2,4,2,4,2,8,128]{7,6,5,4,3,2,1,0:T(8,128)(2,1)}) custom-call(bf16[36,8,128]{2,1,0:T(8,128)(2,1)S(1)} %get-tuple-element.257.piece_ref, bf16[8,1024,128]{2,1,0:T(8,128)(2,1)S(1)} %get-tuple-element.258.q_hbm, bf16[8,1024,128]{2,1,0:T(8,128)(2,1)S(1)} %get-tuple-element.259.k_hbm, ...), custom_call_target="tpu_custom_call" | custom-call | tf_op jit(solution)/shard_map/tri_attn/pallas_call | solution.py:331
  204.1 0.7 and_reduce_fusion
  205.4 1.5 copy-done.1
  207.0 1.6 copy-done.5
  208.6 36.9 %tri_post.3 = bf16[8,128,8,128]{3,2,1,0:T(8,128)(2,1)S(1)} custom-call(f32[8,128,1024]{2,1,0:T(8,128)} %get-tuple-element.886.o_ref, bf16[8,1024,128]{2,1,0:T(8,128)(2,1)S(1)} %copy-done.5, bf16[8,1024,128]{2,1,0:T(8,128)(2,1)S(1)} %bitcast.231, bf16[128,128]{1,0:T(8,128)(2,1)S(1)} %copy-done.13), custom_call_target="tpu_custom_call" | custom-call | tf_op jit(solution)/shard_map/tri_post/pallas_call | solution.py:501
  245.5 10.3 %tri_trans.1 = bf16[8,1024,128]{2,1,0:T(8,128)(2,1)} custom-call(bf16[8,1024,128]{2,1,0:T(8,128)(2,1)S(1)} %bitcast.232, f32[1,128]{1,0:T(1,128)S(1)} %bitcast.238, bf16[128,512]{1,0:T(8,128)(2,1)S(1)} %copy-done.8, f32[1,512]{1,0:T(1,128)S(1)} %bitcast.233, bf16[512,128]{1,0:T(8,128)(2,1)S(1)} %copy-done.9), custom_call_target="tpu_custom_call" | custom-call | tf_op jit(solution)/shard_map/tri_trans/pallas_call | solution.py:530
  (58 shorter events, 0.3 us)
Async XLA Ops:
  4.9 80.9 %copy-start.10 = (f32[8,128]{1,0:T(8,128)}, f32[8,128]{1,0:T(8,128)S(1)}, u32[]{:S(2)}) copy-start(f32[8,128]{1,0:T(8,128)S(1)} %fusion.45.mask_ref) | copy-start | bytes 12292
  5.6 1.6 copy-start.2
  7.2 0.7 copy-start.15
  7.9 0.7 copy-start.16
  16.9 1.3 copy-start.6
  18.3 67.6 %copy-start.21 = (bf16[8,4,48,1024]{3,2,1,0:T(8,128)(2,1)}, bf16[8,4,48,1024]{3,2,1,0:T(8,128)(2,1)S(1)}, u32[]{:S(2)}) copy-start(bf16[8,4,48,1024]{3,2,1,0:T(8,128)(2,1)S(1)} %get-tuple-element.252.vt_hbm) | copy-start | bytes 9437188
  18.3 67.6 %copy-start.24 = (bf16[8,1024,128]{2,1,0:T(8,128)(2,1)}, bf16[8,1024,128]{2,1,0:T(8,128)(2,1)S(1)}, u32[]{:S(2)}) copy-start(bf16[8,1024,128]{2,1,0:T(8,128)(2,1)S(1)} %get-tuple-element.250.q_hbm) | copy-start | bytes 6291460
  18.3 67.6 %copy-start.25 = (bf16[8,1024,128]{2,1,0:T(8,128)(2,1)}, bf16[8,1024,128]{2,1,0:T(8,128)(2,1)S(1)}, u32[]{:S(2)}) copy-start(bf16[8,1024,128]{2,1,0:T(8,128)(2,1)S(1)} %get-tuple-element.251.k_hbm) | copy-start | bytes 6291460
  87.2 1.6 copy-start.3
  87.2 1.6 copy-start.12
  88.8 1.6 copy-start.7
  90.4 36.6 %copy-start.26 = (bf16[128,512]{1,0:T(8,128)(2,1)S(1)}, bf16[128,512]{1,0:T(8,128)(2,1)}, u32[]{:S(2)}) copy-start(bf16[128,512]{1,0:T(8,128)(2,1)} %param.38) | copy-start | bytes 393220
  90.4 37.2 %copy-start.27 = (bf16[128,4]{0,1:T(4,128)(2,1)S(1)}, bf16[128,4]{0,1:T(4,128)(2,1)}, u32[]{:S(2)}) copy-start(bf16[128,4]{0,1:T(4,128)(2,1)} %param.40) | copy-start | bytes 3076
  90.4 37.2 %copy-start.11 = (f32[8,128]{1,0:T(8,128)S(1)}, f32[8,128]{1,0:T(8,128)}, u32[]{:S(2)}) copy-start(f32[8,128]{1,0:T(8,128)} %copy-done.10) | copy-start | bytes 12292
  90.4 37.2 %copy-start.17 = (f32[128]{0:T(128)S(1)}, f32[128]{0:T(128)}, u32[]{:S(2)}) copy-start(f32[128]{0:T(128)} %param.37) | copy-start | bytes 1540
  90.4 37.2 %copy-start.18 = (f32[128]{0:T(128)S(1)}, f32[128]{0:T(128)}, u32[]{:S(2)}) copy-start(f32[128]{0:T(128)} %param.39) | copy-start | bytes 1540
  127.0 77.1 %copy-start = (bf16[8,128,8,128]{3,2,1,0:T(8,128)(2,1)}, bf16[8,128,8,128]{3,2,1,0:T(8,128)(2,1)S(1)}, u32[]{:S(2)}) copy-start(bf16[8,128,8,128]{3,2,1,0:T(8,128)(2,1)S(1)} %tri_post.2) | copy-start | bytes 6291460
  136.1 68.0 %copy-start.4 = (bf16[8,1024,128]{2,1,0:T(8,128)(2,1)}, bf16[8,1024,128]{2,1,0:T(8,128)(2,1)S(1)}, u32[]{:S(2)}) copy-start(bf16[8,1024,128]{2,1,0:T(8,128)(2,1)S(1)} %get-tuple-element.264.gate_ref) | copy-start | bytes 6291460
  136.1 68.0 %copy-start.20 = (bf16[8,4,48,1024]{3,2,1,0:T(8,128)(2,1)}, bf16[8,4,48,1024]{3,2,1,0:T(8,128)(2,1)S(1)}, u32[]{:S(2)}) copy-start(bf16[8,4,48,1024]{3,2,1,0:T(8,128)(2,1)S(1)} %get-tuple-element.260.vt_hbm) | copy-start | bytes 9437188
  136.1 68.0 %copy-start.22 = (bf16[8,1024,128]{2,1,0:T(8,128)(2,1)}, bf16[8,1024,128]{2,1,0:T(8,128)(2,1)S(1)}, u32[]{:S(2)}) copy-start(bf16[8,1024,128]{2,1,0:T(8,128)(2,1)S(1)} %get-tuple-element.258.q_hbm) | copy-start | bytes 6291460
  136.1 68.0 %copy-start.23 = (bf16[8,1024,128]{2,1,0:T(8,128)(2,1)}, bf16[8,1024,128]{2,1,0:T(8,128)(2,1)S(1)}, u32[]{:S(2)}) copy-start(bf16[8,1024,128]{2,1,0:T(8,128)(2,1)S(1)} %get-tuple-element.259.k_hbm) | copy-start | bytes 6291460
  205.4 1.6 copy-start.1
  205.4 1.6 copy-start.13
  207.0 1.6 copy-start.5
  208.6 36.9 %copy-start.8 = (bf16[128,512]{1,0:T(8,128)(2,1)S(1)}, bf16[128,512]{1,0:T(8,128)(2,1)}, u32[]{:S(2)}) copy-start(bf16[128,512]{1,0:T(8,128)(2,1)} %w1_ref.1) | copy-start | bytes 393220
  208.6 36.9 %copy-start.9 = (bf16[512,128]{1,0:T(8,128)(2,1)S(1)}, bf16[512,128]{1,0:T(8,128)(2,1)}, u32[]{:S(2)}) copy-start(bf16[512,128]{1,0:T(8,128)(2,1)} %w2_ref.1) | copy-start | bytes 393220
  208.6 36.9 %copy-start.14 = (f32[512]{0:T(512)S(1)}, f32[512]{0:T(512)}, u32[]{:S(2)}) copy-start(f32[512]{0:T(512)} %param.44) | copy-start | bytes 6148
  208.6 36.9 %copy-start.19 = (f32[128]{0:T(128)S(1)}, f32[128]{0:T(128)}, u32[]{:S(2)}) copy-start(f32[128]{0:T(128)} %param.42) | copy-start | bytes 1540

commit v6 on v5

--- a/solution.py
+++ b/solution.py
@@ -180,7 +180,7 @@
     return lax.rem(group, 2), lax.rem(group // 2, 4), group // 8, lax.rem(it, 4)
 
 
-def attn_loop(first, last, comm, k_ref, vt_ref, b_ref, o_ref, den_ref, qs, eye, slot, ps, mask_ref, sacc, oacc):
+def attn_loop(first, last, comm, k_ref, vt_ref, b_ref, o_ref, qs, eye, slot, ps, mask_ref, sacc, oacc):
     def push_qb(it, odd):
         g, h, qp, kp = attn_split(it)
         at = [pl.ds(pl.multiple_of(qp * 512 + m * 256, 256), 256) for m in range(2)]
@@ -210,8 +210,8 @@
                 o = pltpu.matmul_pop(oacc[m][r])
                 d = o[32:33, :]
                 at = pl.ds(pl.multiple_of(qp * 512 + m * 256, 256), 256)
-                o_ref[4 * g + r, pl.ds(pl.multiple_of(h * 32, 32), 32), at] = o[0:32, :] * (1.0 / d)
-                den_ref[h, r, pl.ds(g, 1), at] = d
+                fine = (d > 2.0 ** -60) & (d < 2.0 ** 100)
+                o_ref[4 * g + r, pl.ds(pl.multiple_of(h * 32, 32), 32), at] = o[0:32, :] * jnp.where(fine, 1.0 / d, jnp.nan)
 
     def step(it, par):
         g, h, qp, kp = attn_split(it)
@@ -266,9 +266,12 @@
     result(last - 1)
 
 
-def attn_kernel(piece_ref, q_hbm, k_hbm, vt_hbm, o_ref, den_ref, full_hbm, full, q_ref, k_ref, vt_ref, qs, eye, slot, ps0, ps1, ps2, ps3, mask_ref, send_sem, recv_sem, load_sem, out_sem):
+def attn_kernel(piece_ref, w_ref, q_hbm, k_hbm, vt_hbm, gate_hbm, z_hbm, out_hbm, full, q_ref, k_ref, vt_ref, gate_ref, z_ref, qs, eye, slot, ps0, ps1, ps2, ps3, mask_ref, o_ref, wide, scr, outgoing, landed, note, notes, bad, send_sem, recv_sem, load_sem, push_sem, land_sem, note_send, note_recv, out_sem):
     ps = (ps0, ps1, ps2, ps3)
-    loads = [pltpu.make_async_copy(a, b, load_sem.at[n]) for n, (a, b) in enumerate(((q_hbm, q_ref), (k_hbm, k_ref), (vt_hbm, vt_ref)))]
+    gx, gy = lax.axis_index("gx"), lax.axis_index("gy")
+    me = gx * 8 + gy
+    pairs = ((q_hbm, q_ref), (k_hbm, k_ref), (vt_hbm, vt_ref), (gate_hbm, gate_ref), (z_hbm, z_ref))
+    loads = [pltpu.make_async_copy(a, b, load_sem.at[n]) for n, (a, b) in enumerate(pairs)]
     for c in loads:
         c.start()
     torus = Torus(piece_ref, full, send_sem, recv_sem)
@@ -279,6 +282,10 @@
     for c in loads:
         c.wait()
     attn_setup(q_ref, qs, eye, slot)
+    wide[...] = jnp.zeros((256, 256), BF)
+    wide[0:128, 0:128] = w_ref[...]
+    wide[128:256, 128:256] = w_ref[...]
+    bad[...] = jnp.zeros((8, 128), F32)
     torus.late("onward", 0, True)
     torus.late("outward", 2)
     torus.late("onward", 1)
@@ -289,26 +296,42 @@
     b_ref = full.reshape(PLANES, 1024, 128)
     attn_mask(b_ref[EXTRA], mask_ref)
 
-    out = pltpu.make_async_copy(full, full_hbm, out_sem)
-
-    def comm(pair):
-        @pl.when(pair == 16)
-        def _():
-            out.start()
-
-        @pl.when(pair < 13)
-        def _():
-            @pl.when((pair == 1) | (pair == 3))
+    def block(dest):
+        return pltpu.make_async_remote_copy(
+            src_ref=outgoing.at[dest], dst_ref=landed.at[:, me], send_sem=push_sem, recv_sem=land_sem,
+            device_id=(dest // 8, lax.rem(dest, 8)), device_id_type=MESH_ID)
+
+    def hand_over(t, sacc, final):
+        at = pl.ds(pl.multiple_of(t * 128, 128), 128)
+        for m in range(2):
+            pltpu.matmul_push_rhs(wide[...], 1, m)
+        for rp in range(4):
+            parts = []
+            for i in (2 * rp, 2 * rp + 1):
+                parts.append((jnp.transpose(o_ref[i, :, at]) * gate_ref[i, at].astype(F32)).astype(BF))
+            pltpu.matmul_acc_lhs(sacc[rp % 2][rp // 2], jnp.concatenate(parts, axis=1), 1 if rp < 2 else None)
+        worst = bad[...]
+        for rp in range(4):
+            y = pltpu.matmul_pop(sacc[rp % 2][rp // 2])
+            for u in range(2):
+                i = 2 * rp + u
+                v = z_ref[i, at].astype(F32) + y[:, 128 * u:128 * u + 128]
+                scr[pl.ds(i, 128, stride=8), :] = v
+                off = jnp.where(jnp.abs(v) < 1e30, 0.0, 1.0).reshape(16, 8, 128)
+                worst = jnp.maximum(worst, jnp.max(off, axis=0))
+        bad[...] = worst
+        outgoing[pl.ds(pl.multiple_of(t * 16, 16), 16)] = scr[...].astype(BF).reshape(16, 8, 8, 128)
+
+        def push(n, _):
+            dest = t * 16 + lax.rem(me + n, 16)
+
+            @pl.when(dest != me)
             def _():
-                torus.late("onward", (pair + 3) // 2)
-
-            @pl.when(lax.rem(pair, 4) == 2)
-            def _():
-                torus.late("closing", (pair + 2) // 4)
-
-            @pl.when((pair > 0) & (lax.rem(pair, 4) == 0))
-            def _():
-                torus.late("shared", pair // 4)
+                block(dest).start()
+
+            return 0
+
+        lax.fori_loop(0, 16, push, 0)
 
     specs = []
     for m in range(2):
@@ -317,45 +340,105 @@
     def run(*accs):
         sacc = [accs[8 * m:8 * m + 4] for m in range(2)]
         oacc = [accs[8 * m + 4:8 * m + 8] for m in range(2)]
-        attn_loop(0, 64, comm, k_ref, vt_ref, b_ref, o_ref, den_ref, qs, eye, slot, ps, mask_ref, sacc, oacc)
+
+        def comm(pair):
+            @pl.when(pair < 13)
+            def _():
+                @pl.when((pair == 1) | (pair == 3))
+                def _():
+                    torus.late("onward", (pair + 3) // 2)
+
+                @pl.when(lax.rem(pair, 4) == 2)
+                def _():
+                    torus.late("closing", (pair + 2) // 4)
+
+                @pl.when((pair > 0) & (lax.rem(pair, 4) == 0))
+                def _():
+                    torus.late("shared", pair // 4)
+
+            @pl.when((pair >= 18) & (pair < 22))
+            def _():
+                hand_over(lax.rem(pair - 18 + gx // 2, 4), sacc, False)
+
+        attn_loop(0, 64, comm, k_ref, vt_ref, b_ref, o_ref, qs, eye, slot, ps, mask_ref, sacc, oacc)
+
+        def tail(t, _):
+            hand_over(4 + lax.rem(t + gx // 2, 4), sacc, True)
+            return 0
+
+        lax.fori_loop(0, 4, tail, 0)
 
     pl.run_scoped(run, *specs)
+    seen = jnp.max(bad[...], axis=(0, 1), keepdims=True)
+    note[...] = jnp.broadcast_to(seen, (8, 128))
+    landed[:, me] = outgoing[me]
+    notes[me] = note[...]
+
+    def tell(dest):
+        return pltpu.make_async_remote_copy(
+            src_ref=note, dst_ref=notes.at[me], send_sem=note_send, recv_sem=note_recv,
+            device_id=(dest // 8, lax.rem(dest, 8)), device_id_type=MESH_ID)
+
+    def spread(n, _):
+        tell(lax.rem(me + n, 128)).start()
+        return 0
+
+    lax.fori_loop(1, 128, spread, 0)
     torus.finish()
+    neighbour = dict(device_id=(lax.rem(gx + 1, 16), gy), device_id_type=MESH_ID)
+    blocks = pltpu.make_async_remote_copy(
+        src_ref=outgoing.at[0:127], dst_ref=landed.at[:, 0:127], send_sem=push_sem, recv_sem=land_sem, **neighbour)
+    all_notes = pltpu.make_async_remote_copy(
+        src_ref=notes.at[0:127], dst_ref=notes.at[0:127], send_sem=note_send, recv_sem=note_recv, **neighbour)
+    blocks.wait_recv()
+    all_notes.wait_recv()
+    worst = jnp.max(notes[...], axis=0)
+    landed[0, 0, 0:8] = jnp.where(worst > 0.0, jnp.nan, landed[0, 0, 0:8].astype(F32)).astype(BF)
+    out = pltpu.make_async_copy(landed, out_hbm, out_sem)
+    out.start()
+    blocks.wait_send()
+    all_notes.wait_send()
     out.wait()
 
 
-def attention(piece, q, k, vt, collective_id):
+def attention(piece, w, q, k, vt, gate, z, collective_id):
     vmem = pl.BlockSpec(memory_space=pltpu.VMEM)
     hbm = pl.BlockSpec(memory_space=pl.ANY)
-    shape = (PLANES, 2, 4, 2, 4, 2, 8, 128)
-    o, den, full = pl.pallas_call(
+    rows = pltpu.VMEM((8, 1024, 128), BF)
+    out = pl.pallas_call(
         attn_kernel,
-        in_specs=[vmem, hbm, hbm, hbm],
-        out_specs=[vmem, vmem, hbm],
-        out_shape=[
-            jax.ShapeDtypeStruct((8, 128, 1024), F32),
-            jax.ShapeDtypeStruct((4, 4, 2, 1024), F32),
-            jax.ShapeDtypeStruct(shape, BF),
-        ],
+        in_specs=[vmem, vmem] + [hbm] * 5,
+        out_specs=hbm,
+        out_shape=jax.ShapeDtypeStruct((8, 128, 8, 128), BF),
         scratch_shapes=[
-            pltpu.VMEM(shape, BF),
-            pltpu.VMEM((8, 1024, 128), BF),
-            pltpu.VMEM((8, 1024, 128), BF),
+            pltpu.VMEM((PLANES, 2, 4, 2, 4, 2, 8, 128), BF),
+            rows,
+            rows,
             pltpu.VMEM((8, 4, 48, 1024), BF),
-            pltpu.VMEM((8, 1024, 128), BF),
+            rows,
+            rows,
+            rows,
             pltpu.VMEM((128, 128), BF),
             pltpu.VMEM((4, 16, 128), BF),
             *[pltpu.VMEM((4, 256, 256), BF)] * 4,
             pltpu.VMEM((16, 1024), BF),
+            pltpu.VMEM((8, 128, 1024), F32),
+            pltpu.VMEM((256, 256), BF),
+            pltpu.VMEM((1024, 128), F32),
+            pltpu.VMEM((128, 8, 8, 128), BF),
+            pltpu.VMEM((8, 128, 8, 128), BF),
+            pltpu.VMEM((8, 128), F32),
+            pltpu.VMEM((128, 8, 128), F32),
+            pltpu.VMEM((8, 128), F32),
             pltpu.SemaphoreType.DMA((EARLY + 84,)),
             pltpu.SemaphoreType.DMA((EARLY + 84,)),
-            pltpu.SemaphoreType.DMA((3,)),
-            pltpu.SemaphoreType.DMA,
+            pltpu.SemaphoreType.DMA((5,)),
+            *[pltpu.SemaphoreType.DMA] * 5,
         ],
-        compiler_params=pltpu.CompilerParams(collective_id=collective_id, has_side_effects=True, vmem_limit_bytes=44 * 2**20),
+        compiler_params=pltpu.CompilerParams(collective_id=collective_id, has_side_effects=True, vmem_limit_bytes=48 * 2**20),
         name="tri_attn",
-    )(piece, q, k, vt)
-    return o, den, full.reshape(PLANES, 1024, 128)
+    )(piece, w, q, k, vt, gate, z)
+    return out.reshape(8, 1024, 128)
 
 
 def layer_norm(x, gain):
@@ -365,7 +448,7 @@
     return (c * lax.rsqrt(var + 1e-05) * gain).astype(BF)
 
 
-def pre_kernel(z_ref, gain_ref, wqk_ref, wvg_ref, bw_ref, gb_ref, mask_ref, q_ref, k_ref, vt_ref, gate_ref, b_ref, scr):
+def pre_kernel(z_ref, gain_ref, proj_ref, bw_ref, gb_ref, mask_ref, q_ref, k_ref, vt_ref, gate_ref, b_ref, scr):
     i = pl.program_id(0)
 
     @pl.when(i == 0)
@@ -374,10 +457,12 @@
         scr[EXTRA] = mask_ref[...]
 
     a = layer_norm(z_ref[0].astype(F32), gain_ref[...])
-    qk = jnp.dot(a, wqk_ref[0], preferred_element_type=F32)
+    shift = 32 * lax.rem(i, 4)
+    rolled = [pltpu.roll(proj_ref[:, 128 * n:128 * n + 128].astype(F32), shift, 1) for n in range(2)]
+    qk = jnp.dot(a, jnp.concatenate(rolled, axis=1).astype(BF), preferred_element_type=F32)
     q_ref[0] = (qk[:, :128] * (HEAD_DIM ** -0.5 * LOG2E)).astype(BF)
     k_ref[0] = qk[:, 128:].astype(BF)
-    vg = jnp.dot(a, wvg_ref[...], preferred_element_type=F32)
+    vg = jnp.dot(a, proj_ref[:, 256:512], preferred_element_type=F32)
     vt = jnp.transpose(vg[:, :128].astype(BF))
     tail = jnp.where(lax.broadcasted_iota(jnp.int32, (16, 1024), 0) == 0, 1.0, 0.0).astype(BF)
     for h in range(4):
@@ -400,13 +485,6 @@
 
 
 def pre(z, gain, proj, bias_w, gate_bias, mask_tile):
-    wq, wk, wv, wg = [proj[:, 128 * n:128 * n + 128] for n in range(4)]
-
-    def slots(w, i):
-        return jnp.concatenate([w[:, 32 * ((s - i) % 4):32 * ((s - i) % 4) + 32] for s in range(4)], axis=1)
-
-    wqk = jnp.stack([jnp.concatenate([slots(wq, i), slots(wk, i)], axis=1) for i in range(4)])
-    wvg = jnp.concatenate([wv, wg], axis=1)
     bwt = jnp.pad(jnp.transpose(bias_w), ((0, 12), (0, 0)))
     row = lambda i: (i, 0, 0)
     return pl.pallas_call(
@@ -415,8 +493,7 @@
         in_specs=[
             pl.BlockSpec((1, 1024, 128), row),
             pl.BlockSpec((1, 128), lambda i: (0, 0)),
-            pl.BlockSpec((1, 128, 256), lambda i: (lax.rem(i, 4), 0, 0)),
-            pl.BlockSpec((128, 256), lambda i: (0, 0)),
+            pl.BlockSpec((128, 512), lambda i: (0, 0)),
             pl.BlockSpec((16, 128), lambda i: (0, 0)),
             pl.BlockSpec((1, 128), lambda i: (0, 0)),
             pl.BlockSpec((8, 128), lambda i: (0, 0)),
@@ -438,87 +515,18 @@
         scratch_shapes=[pltpu.VMEM((PLANES, 8, 128), F32)],
         compiler_params=pltpu.CompilerParams(vmem_limit_bytes=48 * 2**20),
         name="tri_pre",
-    )(z, gain.reshape(1, 128), wqk, wvg, bwt, gate_bias.reshape(1, 128), mask_tile)
-
-
-def post_kernel(o_ref, gate_ref, z_ref, w_ref, out_ref, scr, outgoing, landed, send_sem, recv_sem, out_sem):
-    gx, gy = lax.axis_index("gx"), lax.axis_index("gy")
-    me = gx * 8 + gy
-    barrier = pltpu.get_barrier_semaphore()
-
-    def greet(n, _):
-        peer = lax.rem(me + n, 128)
-        pl.semaphore_signal(barrier, inc=1, device_id=(peer // 8, lax.rem(peer, 8)), device_id_type=MESH_ID)
-        return 0
-
-    lax.fori_loop(1, 128, greet, 0)
-
-    def tile(s, _):
-        t = lax.rem(s + gx // 2, 8)
-        at = pl.ds(pl.multiple_of(t * 128, 128), 128)
-        parts = []
-        for i in range(8):
-            o = jnp.transpose(o_ref[i, :, at])
-            parts.append((o * gate_ref[i, at].astype(F32)).astype(BF))
-        y = jnp.dot(jnp.concatenate(parts, axis=0), w_ref[...], preferred_element_type=F32)
-        for i in range(8):
-            scr[pl.ds(i, 128, stride=8), :] = z_ref[i, at].astype(F32) + y[128 * i:128 * i + 128]
-        outgoing[pl.ds(pl.multiple_of(t * 16, 16), 16)] = scr[...].astype(BF).reshape(16, 8, 8, 128)
-
-        @pl.when(s == 0)
-        def _():
-            pl.semaphore_wait(barrier, 127)
-
-        def push(n, _):
-            dest = t * 16 + lax.rem(me + n, 16)
-
-            @pl.when(dest != me)
-            def _():
-                pltpu.make_async_remote_copy(
-                    src_ref=outgoing.at[dest], dst_ref=landed.at[:, me], send_sem=send_sem, recv_sem=recv_sem,
-                    device_id=(dest // 8, lax.rem(dest, 8)), device_id_type=MESH_ID).start()
-
-            return 0
-
-        lax.fori_loop(0, 16, push, 0)
-        return 0
-
-    lax.fori_loop(0, 8, tile, 0)
-    landed[:, me] = outgoing[me]
-    everything = landed.at[:, 0:127]
-    arrived = pltpu.make_async_remote_copy(
-        src_ref=outgoing.at[0:127], dst_ref=everything, send_sem=send_sem, recv_sem=recv_sem,
-        device_id=(lax.rem(gx + 1, 16), gy), device_id_type=MESH_ID)
-    arrived.wait_recv()
-    out = pltpu.make_async_copy(landed, out_ref, out_sem)
-    out.start()
-    arrived.wait_send()
-    out.wait()
-
-
-def post(o, gate, z, w, collective_id):
-    vmem = pl.BlockSpec(memory_space=pltpu.VMEM)
-    out = pl.pallas_call(
-        post_kernel,
-        in_specs=[vmem] * 4,
-        out_specs=pl.BlockSpec(memory_space=pl.ANY),
-        out_shape=jax.ShapeDtypeStruct((8, 128, 8, 128), BF),
-        scratch_shapes=[
-            pltpu.VMEM((1024, 128), F32),
-            pltpu.VMEM((128, 8, 8, 128), BF),
-            pltpu.VMEM((8, 128, 8, 128), BF),
-            pltpu.SemaphoreType.DMA,
-            pltpu.SemaphoreType.DMA,
-            pltpu.SemaphoreType.DMA,
-        ],
-        compiler_params=pltpu.CompilerParams(collective_id=collective_id, has_side_effects=True, vmem_limit_bytes=40 * 2**20),
-        name="tri_post",
-    )(o, gate, z, w)
-    return out.reshape(8, 1024, 128)
-
-
-def trans_kernel(z_ref, gain_ref, w1_ref, b1_ref, w2_ref, out_ref):
+    )(z, gain.reshape(1, 128), proj, bwt, gate_bias.reshape(1, 128), mask_tile)
+
+
+def trans_kernel(z_ref, gain_ref, w1_ref, b1_ref, w2_ref, out_ref, flag_ref):
     z = z_ref[0].astype(F32)
+
+    @pl.when(pl.program_id(0) == 0)
+    def _():
+        flag_ref[...] = jnp.zeros((8, 128), F32)
+
+    off = jnp.where(jnp.abs(z[0:16]) < 1e30, 0.0, 1.0)
+    flag_ref[...] = jnp.maximum(flag_ref[...], jnp.maximum(off[0:8], off[8:16]))
     a = layer_norm(z, gain_ref[...])
     hid = jax.nn.relu(jnp.dot(a, w1_ref[...], preferred_element_type=F32) + b1_ref[...]).astype(BF)
     out_ref[0] = (z + jnp.dot(hid, w2_ref[...], preferred_element_type=F32)).astype(BF)
@@ -537,47 +545,52 @@
             pl.BlockSpec((1, 512), whole),
             pl.BlockSpec((512, 128), whole),
         ],
-        out_specs=pl.BlockSpec((1, 1024, 128), row),
-        out_shape=jax.ShapeDtypeStruct((8, 1024, 128), BF),
+        out_specs=[pl.BlockSpec((1, 1024, 128), row), pl.BlockSpec((8, 128), whole)],
+        out_shape=[jax.ShapeDtypeStruct((8, 1024, 128), BF), jax.ShapeDtypeStruct((8, 128), F32)],
         compiler_params=pltpu.CompilerParams(vmem_limit_bytes=48 * 2**20),
         name="tri_trans",
     )(z, gain.reshape(1, 128), w1, b1.reshape(1, 512), w2)
 
 
-def exact_attention(q, k, vt, full):
-    extra = full[EXTRA].reshape(128, 8, 128)
-    mask = jnp.sum(extra[:, 0].reshape(8, 16, 128).astype(F32), axis=1).reshape(1024)
-    maxima = jnp.transpose(extra[:, 1:5, :8], (1, 0, 2)).reshape(4, 1024).astype(F32)
+def exact_phase(z, mask, gain, proj, gate_bias, bias_w, out_w):
     key_bias = (mask - 1.0) * big_negative
-    b = jnp.stack([jnp.stack([full[12 * (t // 3) + 3 * h + t % 3] for t in range(8)]) for h in range(4)])
-    orders = jnp.array([[(h + i) % 4 for h in range(4)] for i in range(4)])
-
-    def per_row(operands):
-        i, q_row, k_row, vt_row = operands
-        order = orders[lax.rem(i, 4)]
-        qh = q_row.reshape(1024, 4, 32)[:, order]
-        kh = k_row.reshape(1024, 4, 32)[:, order]
-
-        def per_head(ops):
-            qx, kx, vx, bx, mx = ops
-            s = jnp.dot(qx, kx.T, preferred_element_type=F32)
-            bias = jnp.swapaxes(bx, 0, 1).reshape(1024, 1024).astype(F32)
-            s = (s + bias) * LN2 + mx[:, None] + key_bias
-            w = jax.nn.softmax(s, axis=-1)
-            return jnp.dot(vx[:32].astype(F32), w.T, preferred_element_type=F32)
-
-        o = lax.map(per_head, (jnp.moveaxis(qh, 1, 0), jnp.moveaxis(kh, 1, 0), vt_row, b, maxima))
-        return o.reshape(128, 1024)
-
-    return lax.map(per_row, (jnp.arange(8), q, k, vt))
-
-
-def phase(z, mask_tile, gain, proj, gate_bias, bias_w, out_w, collective_id):
+    a = layer_norm(z.astype(F32), gain)
+    p = jnp.dot(a.reshape(8192, 128), proj, preferred_element_type=F32).reshape(8, 1024, 512)
+    q, k, v = [jnp.moveaxis(p[..., 128 * n:128 * n + 128].astype(BF).reshape(8, 1024, 4, 32), 2, 0) for n in range(3)]
+    b = jnp.dot(a.reshape(8192, 128), bias_w, preferred_element_type=F32).astype(BF).reshape(8, 1024, 4)
+    b = lax.all_gather(jnp.transpose(b, (2, 0, 1)), AX, axis=1, tiled=True)
+
+    def per_head(ops):
+        qh, kh, vh, bh = ops
+
+        def per_row(rows):
+            qr, kr, vr = rows
+            s = jnp.dot(qr, kr.T, preferred_element_type=F32) * HEAD_DIM ** -0.5 + bh.astype(F32) + key_bias
+            return jnp.dot(jax.nn.softmax(s, axis=-1), vr.astype(F32), preferred_element_type=F32)
+
+        return lax.map(per_row, (qh, kh, vh))
+
+    o = jnp.moveaxis(lax.map(per_head, (q, k, v, b)), 0, 2).reshape(8, 1024, 128)
+    gated = (o * jax.nn.sigmoid(p[..., 384:] + gate_bias)).astype(BF)
+    y = jnp.dot(gated.reshape(8192, 128), out_w, preferred_element_type=F32).reshape(8, 1024, 128)
+    z = (z.astype(F32) + y).astype(BF)
+    z = lax.all_to_all(z, AX, split_axis=1, concat_axis=0, tiled=True)
+    return jnp.swapaxes(z, 0, 1)
+
+
+def exact(z, mask_local, phases, last):
+    mask = lax.all_gather(mask_local.astype(F32), AX, axis=0, tiled=True)
+    stacked = [jnp.stack(pair) for pair in zip(*phases)]
+    z, _ = lax.scan(lambda z, ws: (exact_phase(z, mask, *ws), None), z, stacked)
+    gain, w1, b1, w2 = last
+    a = layer_norm(z.astype(F32), gain).reshape(8192, 128)
+    hid = jax.nn.relu(jnp.dot(a, w1, preferred_element_type=F32) + b1).astype(BF)
+    return (z.astype(F32) + jnp.dot(hid, w2, preferred_element_type=F32).reshape(8, 1024, 128)).astype(BF)
+
+
+def phase(z, mask_tile, collective_id, gain, proj, gate_bias, bias_w, out_w):
     q, k, vt, gate, piece = pre(z, gain, proj, bias_w, gate_bias, mask_tile)
-    o, den, full = attention(piece, q, k, vt, collective_id)
-    fine = jnp.all((den > 2.0 ** -60) & (den < 2.0 ** 100))
-    o = lax.cond(fine, lambda: o, lambda: exact_attention(q, k, vt, full))
-    return post(o, gate, z, out_w, 2 + collective_id)
+    return attention(piece, out_w, q, k, vt, gate, z, collective_id)
 
 
 def local(
@@ -603,9 +616,13 @@
     row = lax.broadcasted_iota(jnp.int32, (8, 128), 0)
     spread = jnp.tile(residue_mask.astype(F32), 16).reshape(1, 128)
     mask_tile = jnp.where((lane // 8 == lax.rem(device, 16)) & (row == 0), spread, 0.0)
-    z = phase(pair_in, mask_tile, norm_start, proj_start, gate_bias_start, bias_w_start, out_w_start, 0)
-    z = phase(z, mask_tile, norm_end, proj_end, gate_bias_end, bias_w_end, out_w_end, 1)
-    return trans(z, norm_trans, trans_in, trans_bias, trans_out)
+    start = (norm_start, proj_start, gate_bias_start, bias_w_start, out_w_start)
+    end = (norm_end, proj_end, gate_bias_end, bias_w_end, out_w_end)
+    z = phase(pair_in, mask_tile, 0, *start)
+    z = phase(z, mask_tile, 1, *end)
+    last = (norm_trans, trans_in, trans_bias, trans_out)
+    out, flag = trans(z, *last)
+    return lax.cond(jnp.max(flag) == 0.0, lambda: out, lambda: exact(pair_in, residue_mask, (start, end), last))
 
 
 def solution(mesh):

time: 259 us -> 242 us (0.934)
  Pallas kernels: 236 us -> 217 us
  between operations: 1.54 us -> 14.3 us
  local copies, waits for them, and re-layouts: 15.2 us -> 4.84 us
    pallas_call x4 -> x2, Pallas kernels: 209 us -> 185 us  [attention(): pl.pallas_call(attn_kernel, in_specs=[vmem, vmem] + [hbm] * 5, out_specs=...]
    unnamed x56 -> x36, local copies, waits for them, and re-layouts: 10.4 us -> 4.06 us
    pallas_call x2, Pallas kernels: 16.8 us -> 21.9 us  [pre(): pl.pallas_call(pre_kernel, grid=(8,), in_specs=[pl.BlockSpec((1, 1024, 12...]
    slice x6 -> x0, local copies, waits for them, and re-layouts: 3.14 us -> none  [slots(): w[:, 32 * ((s - i) % 4):32 * ((s - i) % 4) + 32]]
where the time goes in v6:
time: 242 us; the launch traced here: 238 us
  Pallas kernels  217 us (90%)
  between operations  14.3 us (6%)
  local copies, waits for them, and re-layouts  4.84 us (2%)
    pallas_call x2, Pallas kernels, attention(): pl.pallas_call(attn_kernel, in_specs=[vmem, vmem] + [hbm] * 5, out_specs=...  185 us
    pallas_call x2, Pallas kernels, pre(): pl.pallas_call(pre_kernel, grid=(8,), in_specs=[pl.BlockSpec((1, 1024, 12...  21.9 us
    pallas_call x1, Pallas kernels, trans(): pl.pallas_call(trans_kernel, grid=(8,), in_specs=[pl.BlockSpec((1, 1024,...  10.6 us

profile of v6, /device:TPU:12, one launch (start us, length us, event | category | flops | bytes accessed | tf_op | source)
XLA Modules:
  0.0 237.7 jit_solution(5066463009876346691)
XLA Ops:
  6.5 0.7 convert_element_type.72
  7.2 0.1 broadcast_in_dim.29
  7.3 0.1 fusion.51.mask_ref
  7.4 0.7 pad.7.bw_ref
  8.1 10.9 %tri_pre.2 = (bf16[8,1024,128]{2,1,0:T(8,128)(2,1)S(1)}, bf16[8,1024,128]{2,1,0:T(8,128)(2,1)S(1)}, bf16[8,4,48,1024]{3,2,1,0:T(8,128)(2,1)}, bf16[8,1024,128]{2,1,0:T(8,128)(2,1)}, bf16[36,8,128]{2,1,0:T(8,128)(2,1)S(1)}) custom-call(bf16[8,1024,128]{2,1,0:T(8,128)(2,1)} %z_hbm.1, f32[1,128]{1,0:T(1,128)} %bitcast.176, bf16[128,512]{1,0:T(8,128)(2,1)} %proj_ref.2, ...), custom_call_target="tpu_custom_call" | custom-call | tf_op jit(solution)/shard_map/tri_pre/pallas_call | solution.py:490
  19.0 1.3 copy-done.2
  20.4 0.0 copy-start.15
  20.4 92.9 %tri_attn.2 = bf16[8,128,8,128]{3,2,1,0:T(8,128)(2,1)S(1)} custom-call(bf16[36,8,128]{2,1,0:T(8,128)(2,1)S(1)} %get-tuple-element.244.piece_ref, bf16[128,128]{1,0:T(8,128)(2,1)} %w_ref.2, bf16[8,1024,128]{2,1,0:T(8,128)(2,1)S(1)} %get-tuple-element.245.q_hbm, bf16[8,1024,128]{2,1,0:T(8,128)(2,1)} %copy-done.2, ...), custom_call_target="tpu_custom_call" | custom-call | tf_op jit(solution)/shard_map/tri_attn/pallas_call | solution.py:408
  113.2 0.0 copy-start
  113.2 1.3 copy-done
  114.5 0.0 copy-done.24
  114.6 0.0 copy-done.11
  114.6 0.0 copy-done.31
  114.6 0.0 copy-done.32
  114.6 10.9 %tri_pre.3 = (bf16[8,1024,128]{2,1,0:T(8,128)(2,1)S(1)}, bf16[8,1024,128]{2,1,0:T(8,128)(2,1)S(1)}, bf16[8,4,48,1024]{3,2,1,0:T(8,128)(2,1)}, bf16[8,1024,128]{2,1,0:T(8,128)(2,1)}, bf16[36,8,128]{2,1,0:T(8,128)(2,1)S(1)}) custom-call(bf16[8,1024,128]{2,1,0:T(8,128)(2,1)} %bitcast.150, f32[1,128]{1,0:T(1,128)S(1)} %bitcast.180, ...), custom_call_target="tpu_custom_call" | custom-call | tf_op jit(solution)/shard_map/tri_pre/pallas_call | solution.py:490
  125.5 1.3 copy-done.1
  126.8 0.0 copy-done.15
  126.9 0.0 copy-start.27
  126.9 0.0 copy-start.10
  126.9 0.0 copy-start.14
  126.9 0.0 copy-start.23
  126.9 0.0 copy-start.29
  126.9 0.0 copy-start.30
  126.9 0.0 copy-start.37
  126.9 91.7 %tri_attn.3 = bf16[8,128,8,128]{3,2,1,0:T(8,128)(2,1)S(1)} custom-call(bf16[36,8,128]{2,1,0:T(8,128)(2,1)S(1)} %get-tuple-element.249.piece_ref, bf16[128,128]{1,0:T(8,128)(2,1)S(1)} %copy-done.15, bf16[8,1024,128]{2,1,0:T(8,128)(2,1)S(1)} %get-tuple-element.250.q_hbm, bf16[8,1024,128]{2,1,0:T(8,128)(2,1)} %copy-done.1, ...), custom_call_target="tpu_custom_call" | custom-call | tf_op jit(solution)/shard_map/tri_attn/pallas_call | solution.py:408
  218.6 0.0 copy-done.16
  218.6 0.0 copy-done.18
  218.6 0.0 copy-done.25
  218.6 0.0 copy-done.27
  218.7 10.6 %tri_trans.1 = (bf16[8,1024,128]{2,1,0:T(8,128)(2,1)}, f32[8,128]{1,0:T(8,128)S(1)}) custom-call(bf16[8,1024,128]{2,1,0:T(8,128)(2,1)S(1)} %bitcast.152, f32[1,128]{1,0:T(1,128)S(1)} %bitcast.174, bf16[128,512]{1,0:T(8,128)(2,1)S(1)} %copy-done.16, f32[1,512]{1,0:T(1,128)S(1)} %bitcast.175, bf16[512,128]{1,0:T(8,128)(2,1)S(1)} %copy-done.18), custom_call_target="tpu_custom_call" | custom-call | tf_op jit(solution)/shard_map/tri_trans/pallas_call | solution.py:538
  229.2 0.7 reduce_max.18
  230.6 0.2 conditional.1
  (20 shorter events, 0.1 us)
Async XLA Ops:
  19.0 1.3 copy-start.2
  20.3 94.2 %copy-start.24 = (bf16[128,4]{0,1:T(4,128)(2,1)S(1)}, bf16[128,4]{0,1:T(4,128)(2,1)}, u32[]{:S(2)}) copy-start(bf16[128,4]{0,1:T(4,128)(2,1)} %param.34) | copy-start | bytes 3076
  20.3 94.2 %copy-start.11 = (bf16[128,512]{1,0:T(8,128)(2,1)S(1)}, bf16[128,512]{1,0:T(8,128)(2,1)}, u32[]{:S(2)}) copy-start(bf16[128,512]{1,0:T(8,128)(2,1)} %proj_ref.3) | copy-start | bytes 393220
  20.4 94.2 %copy-start.31 = (f32[128]{0:T(128)S(1)}, f32[128]{0:T(128)}, u32[]{:S(2)}) copy-start(f32[128]{0:T(128)} %param.31) | copy-start | bytes 1540
  20.4 94.2 %copy-start.32 = (f32[128]{0:T(128)S(1)}, f32[128]{0:T(128)}, u32[]{:S(2)}) copy-start(f32[128]{0:T(128)} %param.33) | copy-start | bytes 1540
  20.4 106.5 %copy-start.15 = (bf16[128,128]{1,0:T(8,128)(2,1)S(1)}, bf16[128,128]{1,0:T(8,128)(2,1)}, u32[]{:S(2)}) copy-start(bf16[128,128]{1,0:T(8,128)(2,1)} %w_ref.3) | copy-start | bytes 98308
  113.2 1.3 copy-start
  125.5 1.3 copy-start.1
  126.8 91.8 %copy-start.16 = (bf16[128,512]{1,0:T(8,128)(2,1)S(1)}, bf16[128,512]{1,0:T(8,128)(2,1)}, u32[]{:S(2)}) copy-start(bf16[128,512]{1,0:T(8,128)(2,1)} %w1_ref.1) | copy-start | bytes 393220
  126.8 91.8 %copy-start.18 = (bf16[512,128]{1,0:T(8,128)(2,1)S(1)}, bf16[512,128]{1,0:T(8,128)(2,1)}, u32[]{:S(2)}) copy-start(bf16[512,128]{1,0:T(8,128)(2,1)} %w2_ref.1) | copy-start | bytes 393220
  126.8 91.8 %copy-start.25 = (f32[128]{0:T(128)S(1)}, f32[128]{0:T(128)}, u32[]{:S(2)}) copy-start(f32[128]{0:T(128)} %param.36) | copy-start | bytes 1540
  126.9 91.8 %copy-start.27 = (f32[512]{0:T(512)S(1)}, f32[512]{0:T(512)}, u32[]{:S(2)}) copy-start(f32[512]{0:T(512)} %param.38) | copy-start | bytes 6148
  126.9 103.7 %copy-start.10 = (bf16[128,512]{1,0:T(8,128)(2,1)S(1)}, bf16[128,512]{1,0:T(8,128)(2,1)}, u32[]{:S(2)}) copy-start(bf16[128,512]{1,0:T(8,128)(2,1)} %proj_ref.2) | copy-start | bytes 393220
  126.9 103.7 %copy-start.14 = (bf16[128,128]{1,0:T(8,128)(2,1)S(1)}, bf16[128,128]{1,0:T(8,128)(2,1)}, u32[]{:S(2)}) copy-start(bf16[128,128]{1,0:T(8,128)(2,1)} %w_ref.2) | copy-start | bytes 98308
  126.9 103.7 %copy-start.23 = (bf16[128,4]{0,1:T(4,128)(2,1)S(1)}, bf16[128,4]{0,1:T(4,128)(2,1)}, u32[]{:S(2)}) copy-start(bf16[128,4]{0,1:T(4,128)(2,1)} %param.29) | copy-start | bytes 3076
  126.9 103.7 %copy-start.29 = (f32[128]{0:T(128)S(1)}, f32[128]{0:T(128)}, u32[]{:S(2)}) copy-start(f32[128]{0:T(128)} %param.26) | copy-start | bytes 1540
  126.9 103.7 %copy-start.30 = (f32[128]{0:T(128)S(1)}, f32[128]{0:T(128)}, u32[]{:S(2)}) copy-start(f32[128]{0:T(128)} %param.28) | copy-start | bytes 1540
  126.9 103.7 %copy-start.37 = (s32[8]{0:T(128)S(1)}, s32[8]{0:T(128)}, u32[]{:S(2)}) copy-start(s32[8]{0:T(128)} %param.25) | copy-start | bytes 100

commit v7 on v6

--- a/solution.py
+++ b/solution.py
@@ -177,15 +177,18 @@
 
 def attn_split(it):
     group = it // 4
-    return lax.rem(group, 2), lax.rem(group // 2, 4), group // 8, lax.rem(it, 4)
+    late = group >= 8
+    head = jnp.where(late, lax.rem(group, 4), group // 2)
+    quarter = jnp.where(late, group // 4, lax.rem(group, 2))
+    return head, quarter, lax.rem(it, 4)
 
 
 def attn_loop(first, last, comm, k_ref, vt_ref, b_ref, o_ref, qs, eye, slot, ps, mask_ref, sacc, oacc):
     def push_qb(it, odd):
-        g, h, qp, kp = attn_split(it)
-        at = [pl.ds(pl.multiple_of(qp * 512 + m * 256, 256), 256) for m in range(2)]
+        h, qp, kp = attn_split(it)
+        at = pl.ds(pl.multiple_of(qp * 256, 256), 256)
         for m in range(2):
-            rhs = jnp.concatenate([qs[2 * h + g, at[m], :], b_ref[plane(h, 2 * kp + odd), at[m], :]], axis=1)
+            rhs = jnp.concatenate([qs[2 * h + m, at, :], b_ref[plane(h, 2 * kp + odd), at, :]], axis=1)
             pltpu.matmul_push_rhs(rhs, 0, m, transpose=True)
 
     def pop_scores(par, odd, r, n):
@@ -197,33 +200,33 @@
             pltpu.matmul_push_rhs(ps[2 * par + m][r], 1, m)
 
     def pv(it, r):
-        g, h, _, kp = attn_split(it)
+        h, _, kp = attn_split(it)
         at = pl.ds(pl.multiple_of(kp * 256, 256), 256)
-        lhs = vt_ref[4 * g + r, h, :, at] * jnp.concatenate([mask_ref[:, at]] * 3, axis=0)
+        keep = jnp.concatenate([mask_ref[:, at]] * 3, axis=0)
         for m in range(2):
-            pltpu.matmul_acc_lhs(oacc[m][r], lhs, 1)
+            pltpu.matmul_acc_lhs(oacc[m][r], vt_ref[4 * m + r, h, :, at] * keep, 1)
 
     def result(it):
-        g, h, qp, _ = attn_split(it)
+        h, qp, _ = attn_split(it)
+        at = pl.ds(pl.multiple_of(qp * 256, 256), 256)
         for r in range(4):
             for m in range(2):
                 o = pltpu.matmul_pop(oacc[m][r])
                 d = o[32:33, :]
-                at = pl.ds(pl.multiple_of(qp * 512 + m * 256, 256), 256)
                 fine = (d > 2.0 ** -60) & (d < 2.0 ** 100)
-                o_ref[4 * g + r, pl.ds(pl.multiple_of(h * 32, 32), 32), at] = o[0:32, :] * jnp.where(fine, 1.0 / d, jnp.nan)
+                o_ref[4 * m + r, pl.ds(pl.multiple_of(h * 32, 32), 32), at] = o[0:32, :] * jnp.where(fine, 1.0 / d, jnp.nan)
 
     def step(it, par):
-        g, h, qp, kp = attn_split(it)
+        h, _, kp = attn_split(it)
         before = lax.max(it - 1, 0)
         for odd in range(2):
             for r in range(4):
                 at = pl.ds(pl.multiple_of((2 * kp + odd) * 128, 128), 128)
                 keep = jnp.concatenate([slot[lax.rem(h + r, 4)]] * 8, axis=0)
-                lhs = jnp.concatenate([k_ref[4 * g + r, at, :] * keep, eye[...]], axis=1)
                 if r >= 2:
                     pop_scores(1 - par if odd == 0 else par, 1 - odd, r, r)
                 for m in range(2):
+                    lhs = jnp.concatenate([k_ref[4 * m + r, at, :] * keep, eye[...]], axis=1)
                     pltpu.matmul_acc_lhs(sacc[m][r], lhs, 0 if r == 0 else None)
                 if r == 0:
                     if odd == 0:
@@ -301,7 +304,7 @@
             src_ref=outgoing.at[dest], dst_ref=landed.at[:, me], send_sem=push_sem, recv_sem=land_sem,
             device_id=(dest // 8, lax.rem(dest, 8)), device_id_type=MESH_ID)
 
-    def hand_over(t, sacc, final):
+    def hand_over(t, sacc):
         at = pl.ds(pl.multiple_of(t * 128, 128), 128)
         for m in range(2):
             pltpu.matmul_push_rhs(wide[...], 1, m)
@@ -358,15 +361,19 @@
 
             @pl.when((pair >= 18) & (pair < 22))
             def _():
-                hand_over(lax.rem(pair - 18 + gx // 2, 4), sacc, False)
+                hand_over(lax.rem(pair - 18 + gx // 2, 4), sacc)
+
+            @pl.when((pair >= 26) & (pair < 28))
+            def _():
+                hand_over(4 + lax.rem(pair + gx // 2, 2), sacc)
 
         attn_loop(0, 64, comm, k_ref, vt_ref, b_ref, o_ref, qs, eye, slot, ps, mask_ref, sacc, oacc)
 
         def tail(t, _):
-            hand_over(4 + lax.rem(t + gx // 2, 4), sacc, True)
+            hand_over(6 + lax.rem(t + gx // 2, 2), sacc)
             return 0
 
-        lax.fori_loop(0, 4, tail, 0)
+        lax.fori_loop(0, 2, tail, 0)
 
     pl.run_scoped(run, *specs)
     seen = jnp.max(bad[...], axis=(0, 1), keepdims=True)
@@ -448,18 +455,20 @@
     return (c * lax.rsqrt(var + 1e-05) * gain).astype(BF)
 
 
-def pre_kernel(z_ref, gain_ref, proj_ref, bw_ref, gb_ref, mask_ref, q_ref, k_ref, vt_ref, gate_ref, b_ref, scr):
+def pre_kernel(z_ref, gain_ref, proj_ref, bw_ref, gb_ref, mask_ref, q_ref, k_ref, vt_ref, gate_ref, b_ref, scr, wqk):
     i = pl.program_id(0)
 
     @pl.when(i == 0)
     def _():
+        for s in range(4):
+            for n in range(2):
+                w = proj_ref[:, 128 * n:128 * n + 128].astype(F32)
+                wqk[s, :, 128 * n:128 * n + 128] = (pltpu.roll(w, 32 * s, 1) if s else w).astype(BF)
         scr[...] = jnp.zeros((PLANES, 8, 128), F32)
         scr[EXTRA] = mask_ref[...]
 
     a = layer_norm(z_ref[0].astype(F32), gain_ref[...])
-    shift = 32 * lax.rem(i, 4)
-    rolled = [pltpu.roll(proj_ref[:, 128 * n:128 * n + 128].astype(F32), shift, 1) for n in range(2)]
-    qk = jnp.dot(a, jnp.concatenate(rolled, axis=1).astype(BF), preferred_element_type=F32)
+    qk = jnp.dot(a, wqk[lax.rem(i, 4)], preferred_element_type=F32)
     q_ref[0] = (qk[:, :128] * (HEAD_DIM ** -0.5 * LOG2E)).astype(BF)
     k_ref[0] = qk[:, 128:].astype(BF)
     vg = jnp.dot(a, proj_ref[:, 256:512], preferred_element_type=F32)
@@ -512,7 +521,7 @@
             jax.ShapeDtypeStruct((8, 1024, 128), BF),
             jax.ShapeDtypeStruct((PLANES, 8, 128), BF),
         ],
-        scratch_shapes=[pltpu.VMEM((PLANES, 8, 128), F32)],
+        scratch_shapes=[pltpu.VMEM((PLANES, 8, 128), F32), pltpu.VMEM((4, 128, 256), BF)],
         compiler_params=pltpu.CompilerParams(vmem_limit_bytes=48 * 2**20),
         name="tri_pre",
     )(z, gain.reshape(1, 128), proj, bwt, gate_bias.reshape(1, 128), mask_tile)
@@ -554,26 +563,36 @@
 
 def exact_phase(z, mask, gain, proj, gate_bias, bias_w, out_w):
     key_bias = (mask - 1.0) * big_negative
-    a = layer_norm(z.astype(F32), gain)
-    p = jnp.dot(a.reshape(8192, 128), proj, preferred_element_type=F32).reshape(8, 1024, 512)
+
+    def before(row):
+        a = layer_norm(row.astype(F32), gain)
+        b = jnp.dot(a, bias_w, preferred_element_type=F32).astype(BF)
+        return jnp.dot(a, proj, preferred_element_type=F32), jnp.transpose(b)
+
+    p, b = lax.map(before, z)
     q, k, v = [jnp.moveaxis(p[..., 128 * n:128 * n + 128].astype(BF).reshape(8, 1024, 4, 32), 2, 0) for n in range(3)]
-    b = jnp.dot(a.reshape(8192, 128), bias_w, preferred_element_type=F32).astype(BF).reshape(8, 1024, 4)
-    b = lax.all_gather(jnp.transpose(b, (2, 0, 1)), AX, axis=1, tiled=True)
 
     def per_head(ops):
         qh, kh, vh, bh = ops
+        eighths = jnp.swapaxes(bh.reshape(8, 8, 128), 0, 1)
+        bias = lax.map(lambda c: lax.all_gather(c, AX, axis=0, tiled=True), eighths)
+        bias = jnp.swapaxes(bias, 0, 1).reshape(1024, 1024).astype(F32)
 
         def per_row(rows):
             qr, kr, vr = rows
-            s = jnp.dot(qr, kr.T, preferred_element_type=F32) * HEAD_DIM ** -0.5 + bh.astype(F32) + key_bias
+            s = jnp.dot(qr, kr.T, preferred_element_type=F32) * HEAD_DIM ** -0.5 + bias + key_bias
             return jnp.dot(jax.nn.softmax(s, axis=-1), vr.astype(F32), preferred_element_type=F32)
 
         return lax.map(per_row, (qh, kh, vh))
 
-    o = jnp.moveaxis(lax.map(per_head, (q, k, v, b)), 0, 2).reshape(8, 1024, 128)
-    gated = (o * jax.nn.sigmoid(p[..., 384:] + gate_bias)).astype(BF)
-    y = jnp.dot(gated.reshape(8192, 128), out_w, preferred_element_type=F32).reshape(8, 1024, 128)
-    z = (z.astype(F32) + y).astype(BF)
+    o = jnp.moveaxis(lax.map(per_head, (q, k, v, jnp.swapaxes(b, 0, 1))), 0, 2).reshape(8, 1024, 128)
+
+    def after(ops):
+        row, mixed, logit = ops
+        gated = (mixed * jax.nn.sigmoid(logit + gate_bias)).astype(BF)
+        return (row.astype(F32) + jnp.dot(gated, out_w, preferred_element_type=F32)).astype(BF)
+
+    z = lax.map(after, (z, o, p[..., 384:]))
     z = lax.all_to_all(z, AX, split_axis=1, concat_axis=0, tiled=True)
     return jnp.swapaxes(z, 0, 1)
 
@@ -582,10 +601,7 @@
     mask = lax.all_gather(mask_local.astype(F32), AX, axis=0, tiled=True)
     stacked = [jnp.stack(pair) for pair in zip(*phases)]
     z, _ = lax.scan(lambda z, ws: (exact_phase(z, mask, *ws), None), z, stacked)
-    gain, w1, b1, w2 = last
-    a = layer_norm(z.astype(F32), gain).reshape(8192, 128)
-    hid = jax.nn.relu(jnp.dot(a, w1, preferred_element_type=F32) + b1).astype(BF)
-    return (z.astype(F32) + jnp.dot(hid, w2, preferred_element_type=F32).reshape(8, 1024, 128)).astype(BF)
+    return trans(z, *last)[0]
 
 
 def phase(z, mask_tile, collective_id, gain, proj, gate_bias, bias_w, out_w):

time: 242 us -> 228 us (0.942)
  between operations: 14.3 us -> 1.02 us
where the time goes in v7:
time: 228 us; the launch traced here: 224 us
  Pallas kernels  216 us (95%)
  local copies, waits for them, and re-layouts  5.51 us (2%)
    pallas_call x2, Pallas kernels, attention(): pl.pallas_call(attn_kernel, in_specs=[vmem, vmem] + [hbm] * 5, out_specs=...  184 us
    pallas_call x2, Pallas kernels, pre(): pl.pallas_call(pre_kernel, grid=(8,), in_specs=[pl.BlockSpec((1, 1024, 12...  21.6 us
    pallas_call x1, Pallas kernels, trans(): pl.pallas_call(trans_kernel, grid=(8,), in_specs=[pl.BlockSpec((1, 1024,...  10.6 us

profile of v7, /device:TPU:12, one launch (start us, length us, event | category | flops | bytes accessed | tf_op | source)
XLA Modules:
  0.0 224.3 jit_solution(10771740765641951848)
XLA Ops:
  0.0 0.8 convert_element_type.62
  0.8 0.7 pad.8.bw_ref
  1.5 0.7 pad.7.bw_ref
  2.2 0.1 broadcast_in_dim.44
  2.3 0.1 fusion.47.mask_ref
  2.4 10.8 %tri_pre.2 = (bf16[8,1024,128]{2,1,0:T(8,128)(2,1)S(1)}, bf16[8,1024,128]{2,1,0:T(8,128)(2,1)S(1)}, bf16[8,4,48,1024]{3,2,1,0:T(8,128)(2,1)}, bf16[8,1024,128]{2,1,0:T(8,128)(2,1)}, bf16[36,8,128]{2,1,0:T(8,128)(2,1)S(1)}) custom-call(bf16[8,1024,128]{2,1,0:T(8,128)(2,1)} %z_hbm.1, f32[1,128]{1,0:T(1,128)} %bitcast.232, bf16[128,512]{1,0:T(8,128)(2,1)} %proj_ref.2, ...), custom_call_target="tpu_custom_call" | custom-call | tf_op jit(solution)/shard_map/tri_pre/pallas_call | solution.py:499
  13.2 1.3 copy-done.2
  14.5 0.0 copy-done.7
  14.5 0.0 copy-done.21
  14.5 0.0 copy-start.37
  14.5 93.7 %tri_attn.2 = bf16[8,128,8,128]{3,2,1,0:T(8,128)(2,1)S(1)} custom-call(bf16[36,8,128]{2,1,0:T(8,128)(2,1)S(1)} %get-tuple-element.337.piece_ref, bf16[128,128]{1,0:T(8,128)(2,1)S(1)} %copy-done.21, bf16[8,1024,128]{2,1,0:T(8,128)(2,1)S(1)} %get-tuple-element.338.q_hbm, bf16[8,1024,128]{2,1,0:T(8,128)(2,1)} %copy-done.2, ...), custom_call_target="tpu_custom_call" | custom-call | tf_op jit(solution)/shard_map/tri_attn/pallas_call | solution.py:415
  108.2 0.0 copy-start
  108.2 1.3 copy-done
  109.5 0.0 copy-done.18
  109.5 0.0 copy-done.36
  109.5 0.0 copy-done.37
  109.5 10.8 %tri_pre.3 = (bf16[8,1024,128]{2,1,0:T(8,128)(2,1)S(1)}, bf16[8,1024,128]{2,1,0:T(8,128)(2,1)S(1)}, bf16[8,4,48,1024]{3,2,1,0:T(8,128)(2,1)}, bf16[8,1024,128]{2,1,0:T(8,128)(2,1)}, bf16[36,8,128]{2,1,0:T(8,128)(2,1)S(1)}) custom-call(bf16[8,1024,128]{2,1,0:T(8,128)(2,1)} %bitcast.206, f32[1,128]{1,0:T(1,128)S(1)} %bitcast.236, ...), custom_call_target="tpu_custom_call" | custom-call | tf_op jit(solution)/shard_map/tri_pre/pallas_call | solution.py:499
  120.3 1.3 copy-done.1
  121.6 0.0 copy-done.22
  121.6 0.0 copy-start.32
  121.7 90.3 %tri_attn.3 = bf16[8,128,8,128]{3,2,1,0:T(8,128)(2,1)S(1)} custom-call(bf16[36,8,128]{2,1,0:T(8,128)(2,1)S(1)} %get-tuple-element.342.piece_ref, bf16[128,128]{1,0:T(8,128)(2,1)S(1)} %copy-done.22, bf16[8,1024,128]{2,1,0:T(8,128)(2,1)S(1)} %get-tuple-element.343.q_hbm, bf16[8,1024,128]{2,1,0:T(8,128)(2,1)} %copy-done.1, ...), custom_call_target="tpu_custom_call" | custom-call | tf_op jit(solution)/shard_map/tri_attn/pallas_call | solution.py:415
  211.9 0.0 copy-start.17
  211.9 0.0 copy-start.30
  212.0 0.0 copy-start.31
  212.0 0.0 copy-start.34
  212.0 0.0 copy-start.35
  212.0 0.0 copy-start.38
  212.0 0.0 copy-done.13
  212.0 0.0 copy-done.15
  212.0 10.6 %tri_trans.3 = (bf16[8,1024,128]{2,1,0:T(8,128)(2,1)}, f32[8,128]{1,0:T(8,128)S(1)}) custom-call(bf16[8,1024,128]{2,1,0:T(8,128)(2,1)S(1)} %bitcast.208, f32[1,128]{1,0:T(1,128)S(1)} %bitcast.230, bf16[128,512]{1,0:T(8,128)(2,1)S(1)} %copy-done.13, f32[1,512]{1,0:T(1,128)S(1)} %bitcast.224, bf16[512,128]{1,0:T(8,128)(2,1)S(1)} %copy-done.15), custom_call_target="tpu_custom_call" | custom-call | tf_op jit(solution)/shard_map/tri_trans/pallas_call | solution.py:547
  222.6 0.6 reduce_max.18
  223.9 0.2 conditional.1
  (22 shorter events, 0.1 us)
Async XLA Ops:
  0.0 14.5 %copy-start.7 = (bf16[8,1024,128]{2,1,0:T(8,128)(2,1)S(1)}, bf16[8,1024,128]{2,1,0:T(8,128)(2,1)}, u32[]{:S(2)}) copy-start(bf16[8,1024,128]{2,1,0:T(8,128)(2,1)} %z_hbm.1) | copy-start | bytes 6291460
  0.0 14.5 %copy-start.21 = (bf16[128,128]{1,0:T(8,128)(2,1)S(1)}, bf16[128,128]{1,0:T(8,128)(2,1)}, u32[]{:S(2)}) copy-start(bf16[128,128]{1,0:T(8,128)(2,1)} %w_ref.2) | copy-start | bytes 98308
  13.2 1.3 copy-start.2
  14.5 95.0 %copy-start.18 = (bf16[128,512]{1,0:T(8,128)(2,1)S(1)}, bf16[128,512]{1,0:T(8,128)(2,1)}, u32[]{:S(2)}) copy-start(bf16[128,512]{1,0:T(8,128)(2,1)} %proj_ref.3) | copy-start | bytes 393220
  14.5 95.0 %copy-start.36 = (f32[128]{0:T(128)S(1)}, f32[128]{0:T(128)}, u32[]{:S(2)}) copy-start(f32[128]{0:T(128)} %param.37) | copy-start | bytes 1540
  14.5 95.0 %copy-start.37 = (f32[128]{0:T(128)S(1)}, f32[128]{0:T(128)}, u32[]{:S(2)}) copy-start(f32[128]{0:T(128)} %param.39) | copy-start | bytes 1540
  108.2 1.3 copy-start
  109.5 12.1 %copy-start.22 = (bf16[128,128]{1,0:T(8,128)(2,1)S(1)}, bf16[128,128]{1,0:T(8,128)(2,1)}, u32[]{:S(2)}) copy-start(bf16[128,128]{1,0:T(8,128)(2,1)} %w_ref.3) | copy-start | bytes 98308
  120.3 1.3 copy-start.1
  121.6 90.4 %copy-start.13 = (bf16[128,512]{1,0:T(8,128)(2,1)S(1)}, bf16[128,512]{1,0:T(8,128)(2,1)}, u32[]{:S(2)}) copy-start(bf16[128,512]{1,0:T(8,128)(2,1)} %w1_ref.1) | copy-start | bytes 393220
  121.6 90.4 %copy-start.15 = (bf16[512,128]{1,0:T(8,128)(2,1)S(1)}, bf16[512,128]{1,0:T(8,128)(2,1)}, u32[]{:S(2)}) copy-start(bf16[512,128]{1,0:T(8,128)(2,1)} %w2_ref.1) | copy-start | bytes 393220
  121.6 90.4 %copy-start.28 = (f32[512]{0:T(512)S(1)}, f32[512]{0:T(512)}, u32[]{:S(2)}) copy-start(f32[512]{0:T(512)} %param.44) | copy-start | bytes 6148
  121.6 90.4 %copy-start.32 = (f32[128]{0:T(128)S(1)}, f32[128]{0:T(128)}, u32[]{:S(2)}) copy-start(f32[128]{0:T(128)} %param.42) | copy-start | bytes 1540
  211.9 11.9 %copy-start.17 = (bf16[128,512]{1,0:T(8,128)(2,1)S(1)}, bf16[128,512]{1,0:T(8,128)(2,1)}, u32[]{:S(2)}) copy-start(bf16[128,512]{1,0:T(8,128)(2,1)} %proj_ref.2) | copy-start | bytes 393220
  211.9 11.9 %copy-start.30 = (bf16[128,4]{0,1:T(4,128)(2,1)S(1)}, bf16[128,4]{0,1:T(4,128)(2,1)}, u32[]{:S(2)}) copy-start(bf16[128,4]{0,1:T(4,128)(2,1)} %param.35) | copy-start | bytes 3076
  212.0 11.9 %copy-start.31 = (bf16[128,4]{0,1:T(4,128)(2,1)S(1)}, bf16[128,4]{0,1:T(4,128)(2,1)}, u32[]{:S(2)}) copy-start(bf16[128,4]{0,1:T(4,128)(2,1)} %param.40) | copy-start | bytes 3076
  212.0 11.9 %copy-start.34 = (f32[128]{0:T(128)S(1)}, f32[128]{0:T(128)}, u32[]{:S(2)}) copy-start(f32[128]{0:T(128)} %param.32) | copy-start | bytes 1540
  212.0 11.9 %copy-start.35 = (f32[128]{0:T(128)S(1)}, f32[128]{0:T(128)}, u32[]{:S(2)}) copy-start(f32[128]{0:T(128)} %param.34) | copy-start | bytes 1540
  212.0 11.9 %copy-start.38 = (s32[8]{0:T(128)S(1)}, s32[8]{0:T(128)}, u32[]{:S(2)}) copy-start(s32[8]{0:T(128)} %param.31) | copy-start | bytes 100

commit v8 on v7

--- a/solution.py
+++ b/solution.py
@@ -186,9 +186,10 @@
 def attn_loop(first, last, comm, k_ref, vt_ref, b_ref, o_ref, qs, eye, slot, ps, mask_ref, sacc, oacc):
     def push_qb(it, odd):
         h, qp, kp = attn_split(it)
-        at = pl.ds(pl.multiple_of(qp * 256, 256), 256)
+        core, zl = qp // 2, lax.rem(qp, 2)
+        bias = b_ref[plane(h, 2 * kp + odd), zl, :, core].reshape(256, 128)
         for m in range(2):
-            rhs = jnp.concatenate([qs[2 * h + m, at, :], b_ref[plane(h, 2 * kp + odd), at, :]], axis=1)
+            rhs = jnp.concatenate([qs[2 * h + m, zl, :, core].reshape(256, 128), bias], axis=1)
             pltpu.matmul_push_rhs(rhs, 0, m, transpose=True)
 
     def pop_scores(par, odd, r, n):
@@ -296,29 +297,40 @@
     torus.late("closing", 0, True)
     torus.early_shared()
     torus.late("shared", 0, True)
-    b_ref = full.reshape(PLANES, 1024, 128)
-    attn_mask(b_ref[EXTRA], mask_ref)
-
-    def block(dest):
+    attn_mask(full.reshape(PLANES, 1024, 128)[EXTRA], mask_ref)
+    b_ref = full.reshape(PLANES, 2, 4, 2, 64, 128)
+    qs_by = qs.reshape(8, 2, 4, 2, 64, 128)
+    gate_by = gate_ref.reshape(8, 2, 4, 2, 64, 128)
+    z_by = z_ref.reshape(8, 2, 4, 2, 64, 128)
+
+    def owner(n):
+        quarter, x, low = n // 32, lax.rem(n // 8, 4), lax.rem(n, 8)
+        return (lax.rem(quarter, 2) * 8 + x * 2 + quarter // 2) * 8 + low
+
+    my_block = (lax.rem(gx, 2) * 2 + gx // 8) * 32 + lax.rem(gx // 2, 4) * 8 + gy
+
+    def block(n):
+        dest = owner(n)
         return pltpu.make_async_remote_copy(
-            src_ref=outgoing.at[dest], dst_ref=landed.at[:, me], send_sem=push_sem, recv_sem=land_sem,
+            src_ref=outgoing.at[n], dst_ref=landed.at[:, me], send_sem=push_sem, recv_sem=land_sem,
             device_id=(dest // 8, lax.rem(dest, 8)), device_id_type=MESH_ID)
 
     def hand_over(t, sacc):
         at = pl.ds(pl.multiple_of(t * 128, 128), 128)
+        core, zl, half = t // 4, lax.rem(t // 2, 2), pl.ds(2 * lax.rem(t, 2), 2)
         for m in range(2):
             pltpu.matmul_push_rhs(wide[...], 1, m)
         for rp in range(4):
             parts = []
             for i in (2 * rp, 2 * rp + 1):
-                parts.append((jnp.transpose(o_ref[i, :, at]) * gate_ref[i, at].astype(F32)).astype(BF))
+                parts.append((jnp.transpose(o_ref[i, :, at]) * gate_by[i, zl, half, core].reshape(128, 128).astype(F32)).astype(BF))
             pltpu.matmul_acc_lhs(sacc[rp % 2][rp // 2], jnp.concatenate(parts, axis=1), 1 if rp < 2 else None)
         worst = bad[...]
         for rp in range(4):
             y = pltpu.matmul_pop(sacc[rp % 2][rp // 2])
             for u in range(2):
                 i = 2 * rp + u
-                v = z_ref[i, at].astype(F32) + y[:, 128 * u:128 * u + 128]
+                v = z_by[i, zl, half, core].reshape(128, 128).astype(F32) + y[:, 128 * u:128 * u + 128]
                 scr[pl.ds(i, 128, stride=8), :] = v
                 off = jnp.where(jnp.abs(v) < 1e30, 0.0, 1.0).reshape(16, 8, 128)
                 worst = jnp.maximum(worst, jnp.max(off, axis=0))
@@ -326,11 +338,11 @@
         outgoing[pl.ds(pl.multiple_of(t * 16, 16), 16)] = scr[...].astype(BF).reshape(16, 8, 8, 128)
 
         def push(n, _):
-            dest = t * 16 + lax.rem(me + n, 16)
-
-            @pl.when(dest != me)
+            spot = t * 16 + lax.rem(me + n, 16)
+
+            @pl.when(spot != my_block)
             def _():
-                block(dest).start()
+                block(spot).start()
 
             return 0
 
@@ -367,7 +379,7 @@
             def _():
                 hand_over(4 + lax.rem(pair + gx // 2, 2), sacc)
 
-        attn_loop(0, 64, comm, k_ref, vt_ref, b_ref, o_ref, qs, eye, slot, ps, mask_ref, sacc, oacc)
+        attn_loop(0, 64, comm, k_ref, vt_ref, b_ref, o_ref, qs_by, eye, slot, ps, mask_ref, sacc, oacc)
 
         def tail(t, _):
             hand_over(6 + lax.rem(t + gx // 2, 2), sacc)
@@ -378,7 +390,7 @@
     pl.run_scoped(run, *specs)
     seen = jnp.max(bad[...], axis=(0, 1), keepdims=True)
     note[...] = jnp.broadcast_to(seen, (8, 128))
-    landed[:, me] = outgoing[me]
+    landed[:, me] = outgoing[my_block]
     notes[me] = note[...]
 
     def tell(dest):

time: 228 us -> 222 us (0.974)
  Pallas kernels: 216 us -> 210 us
    pallas_call x2, Pallas kernels: 184 us -> 178 us  [attention(): pl.pallas_call(attn_kernel, in_specs=[vmem, vmem] + [hbm] * 5, out_specs=...]
where the time goes in v8:
time: 222 us; the launch traced here: 218 us
  Pallas kernels  210 us (95%)
  local copies, waits for them, and re-layouts  5.51 us (2%)
    pallas_call x2, Pallas kernels, attention(): pl.pallas_call(attn_kernel, in_specs=[vmem, vmem] + [hbm] * 5, out_specs=...  178 us
    pallas_call x2, Pallas kernels, pre(): pl.pallas_call(pre_kernel, grid=(8,), in_specs=[pl.BlockSpec((1, 1024, 12...  21.6 us
    pallas_call x1, Pallas kernels, trans(): pl.pallas_call(trans_kernel, grid=(8,), in_specs=[pl.BlockSpec((1, 1024,...  10.6 us

profile of v8, /device:TPU:12, one launch (start us, length us, event | category | flops | bytes accessed | tf_op | source)
XLA Modules:
  0.0 218.2 jit_solution(11124035804322480030)
XLA Ops:
  0.0 0.8 convert_element_type.62
  0.8 0.7 pad.8.bw_ref
  1.5 0.7 pad.7.bw_ref
  2.2 0.1 broadcast_in_dim.44
  2.3 0.1 fusion.47.mask_ref
  2.4 10.8 %tri_pre.2 = (bf16[8,1024,128]{2,1,0:T(8,128)(2,1)S(1)}, bf16[8,1024,128]{2,1,0:T(8,128)(2,1)S(1)}, bf16[8,4,48,1024]{3,2,1,0:T(8,128)(2,1)}, bf16[8,1024,128]{2,1,0:T(8,128)(2,1)}, bf16[36,8,128]{2,1,0:T(8,128)(2,1)S(1)}) custom-call(bf16[8,1024,128]{2,1,0:T(8,128)(2,1)} %z_hbm.1, f32[1,128]{1,0:T(1,128)} %bitcast.232, bf16[128,512]{1,0:T(8,128)(2,1)} %proj_ref.2, ...), custom_call_target="tpu_custom_call" | custom-call | tf_op jit(solution)/shard_map/tri_pre/pallas_call | solution.py:511
  13.2 1.3 copy-done.2
  14.5 0.0 copy-done.7
  14.5 0.0 copy-done.21
  14.5 0.0 copy-start.37
  14.5 90.0 %tri_attn.2 = bf16[8,128,8,128]{3,2,1,0:T(8,128)(2,1)S(1)} custom-call(bf16[36,8,128]{2,1,0:T(8,128)(2,1)S(1)} %get-tuple-element.337.piece_ref, bf16[128,128]{1,0:T(8,128)(2,1)S(1)} %copy-done.21, bf16[8,1024,128]{2,1,0:T(8,128)(2,1)S(1)} %get-tuple-element.338.q_hbm, bf16[8,1024,128]{2,1,0:T(8,128)(2,1)} %copy-done.2, ...), custom_call_target="tpu_custom_call" | custom-call | tf_op jit(solution)/shard_map/tri_attn/pallas_call | solution.py:427
  104.5 0.0 copy-start
  104.5 1.3 copy-done
  105.8 0.0 copy-done.18
  105.8 0.0 copy-done.37
  105.8 10.8 %tri_pre.3 = (bf16[8,1024,128]{2,1,0:T(8,128)(2,1)S(1)}, bf16[8,1024,128]{2,1,0:T(8,128)(2,1)S(1)}, bf16[8,4,48,1024]{3,2,1,0:T(8,128)(2,1)}, bf16[8,1024,128]{2,1,0:T(8,128)(2,1)}, bf16[36,8,128]{2,1,0:T(8,128)(2,1)S(1)}) custom-call(bf16[8,1024,128]{2,1,0:T(8,128)(2,1)} %bitcast.206, f32[1,128]{1,0:T(1,128)S(1)} %bitcast.236, ...), custom_call_target="tpu_custom_call" | custom-call | tf_op jit(solution)/shard_map/tri_pre/pallas_call | solution.py:511
  116.6 1.3 copy-done.1
  117.9 0.0 copy-start.32
  117.9 87.8 %tri_attn.3 = bf16[8,128,8,128]{3,2,1,0:T(8,128)(2,1)S(1)} custom-call(bf16[36,8,128]{2,1,0:T(8,128)(2,1)S(1)} %get-tuple-element.342.piece_ref, bf16[128,128]{1,0:T(8,128)(2,1)S(1)} %copy-done.22, bf16[8,1024,128]{2,1,0:T(8,128)(2,1)S(1)} %get-tuple-element.343.q_hbm, bf16[8,1024,128]{2,1,0:T(8,128)(2,1)} %copy-done.1, ...), custom_call_target="tpu_custom_call" | custom-call | tf_op jit(solution)/shard_map/tri_attn/pallas_call | solution.py:427
  205.8 0.0 copy-start.17
  205.8 0.0 copy-start.30
  205.8 0.0 copy-start.31
  205.8 0.0 copy-start.34
  205.9 0.0 copy-start.35
  205.9 0.0 copy-start.38
  205.9 0.0 copy-done.13
  205.9 0.0 copy-done.15
  205.9 0.0 copy-done.28
  205.9 0.0 copy-done.32
  205.9 10.6 %tri_trans.3 = (bf16[8,1024,128]{2,1,0:T(8,128)(2,1)}, f32[8,128]{1,0:T(8,128)S(1)}) custom-call(bf16[8,1024,128]{2,1,0:T(8,128)(2,1)S(1)} %bitcast.208, f32[1,128]{1,0:T(1,128)S(1)} %bitcast.230, bf16[128,512]{1,0:T(8,128)(2,1)S(1)} %copy-done.13, f32[1,512]{1,0:T(1,128)S(1)} %bitcast.224, bf16[512,128]{1,0:T(8,128)(2,1)S(1)} %copy-done.15), custom_call_target="tpu_custom_call" | custom-call | tf_op jit(solution)/shard_map/tri_trans/pallas_call | solution.py:559
  216.5 0.6 reduce_max.18
  217.8 0.2 conditional.1
  (22 shorter events, 0.1 us)
Async XLA Ops:
  0.0 14.5 %copy-start.7 = (bf16[8,1024,128]{2,1,0:T(8,128)(2,1)S(1)}, bf16[8,1024,128]{2,1,0:T(8,128)(2,1)}, u32[]{:S(2)}) copy-start(bf16[8,1024,128]{2,1,0:T(8,128)(2,1)} %z_hbm.1) | copy-start | bytes 6291460
  0.0 14.5 %copy-start.21 = (bf16[128,128]{1,0:T(8,128)(2,1)S(1)}, bf16[128,128]{1,0:T(8,128)(2,1)}, u32[]{:S(2)}) copy-start(bf16[128,128]{1,0:T(8,128)(2,1)} %w_ref.2) | copy-start | bytes 98308
  13.2 1.3 copy-start.2
  14.5 91.3 %copy-start.18 = (bf16[128,512]{1,0:T(8,128)(2,1)S(1)}, bf16[128,512]{1,0:T(8,128)(2,1)}, u32[]{:S(2)}) copy-start(bf16[128,512]{1,0:T(8,128)(2,1)} %proj_ref.3) | copy-start | bytes 393220
  14.5 91.3 %copy-start.36 = (f32[128]{0:T(128)S(1)}, f32[128]{0:T(128)}, u32[]{:S(2)}) copy-start(f32[128]{0:T(128)} %param.37) | copy-start | bytes 1540
  14.5 91.3 %copy-start.37 = (f32[128]{0:T(128)S(1)}, f32[128]{0:T(128)}, u32[]{:S(2)}) copy-start(f32[128]{0:T(128)} %param.39) | copy-start | bytes 1540
  104.5 1.3 copy-start
  105.8 12.1 %copy-start.22 = (bf16[128,128]{1,0:T(8,128)(2,1)S(1)}, bf16[128,128]{1,0:T(8,128)(2,1)}, u32[]{:S(2)}) copy-start(bf16[128,128]{1,0:T(8,128)(2,1)} %w_ref.3) | copy-start | bytes 98308
  116.6 1.3 copy-start.1
  117.9 88.0 %copy-start.13 = (bf16[128,512]{1,0:T(8,128)(2,1)S(1)}, bf16[128,512]{1,0:T(8,128)(2,1)}, u32[]{:S(2)}) copy-start(bf16[128,512]{1,0:T(8,128)(2,1)} %w1_ref.1) | copy-start | bytes 393220
  117.9 88.0 %copy-start.15 = (bf16[512,128]{1,0:T(8,128)(2,1)S(1)}, bf16[512,128]{1,0:T(8,128)(2,1)}, u32[]{:S(2)}) copy-start(bf16[512,128]{1,0:T(8,128)(2,1)} %w2_ref.1) | copy-start | bytes 393220
  117.9 88.0 %copy-start.28 = (f32[512]{0:T(512)S(1)}, f32[512]{0:T(512)}, u32[]{:S(2)}) copy-start(f32[512]{0:T(512)} %param.44) | copy-start | bytes 6148
  117.9 88.0 %copy-start.32 = (f32[128]{0:T(128)S(1)}, f32[128]{0:T(128)}, u32[]{:S(2)}) copy-start(f32[128]{0:T(128)} %param.42) | copy-start | bytes 1540
  205.8 11.9 %copy-start.17 = (bf16[128,512]{1,0:T(8,128)(2,1)S(1)}, bf16[128,512]{1,0:T(8,128)(2,1)}, u32[]{:S(2)}) copy-start(bf16[128,512]{1,0:T(8,128)(2,1)} %proj_ref.2) | copy-start | bytes 393220
  205.8 11.9 %copy-start.30 = (bf16[128,4]{0,1:T(4,128)(2,1)S(1)}, bf16[128,4]{0,1:T(4,128)(2,1)}, u32[]{:S(2)}) copy-start(bf16[128,4]{0,1:T(4,128)(2,1)} %param.35) | copy-start | bytes 3076
  205.8 11.9 %copy-start.31 = (bf16[128,4]{0,1:T(4,128)(2,1)S(1)}, bf16[128,4]{0,1:T(4,128)(2,1)}, u32[]{:S(2)}) copy-start(bf16[128,4]{0,1:T(4,128)(2,1)} %param.40) | copy-start | bytes 3076
  205.8 11.9 %copy-start.34 = (f32[128]{0:T(128)S(1)}, f32[128]{0:T(128)}, u32[]{:S(2)}) copy-start(f32[128]{0:T(128)} %param.32) | copy-start | bytes 1540
  205.9 11.9 %copy-start.35 = (f32[128]{0:T(128)S(1)}, f32[128]{0:T(128)}, u32[]{:S(2)}) copy-start(f32[128]{0:T(128)} %param.34) | copy-start | bytes 1540
  205.9 11.9 %copy-start.38 = (s32[8]{0:T(128)S(1)}, s32[8]{0:T(128)}, u32[]{:S(2)}) copy-start(s32[8]{0:T(128)} %param.31) | copy-start | bytes 100

commit v9 on v8

--- a/solution.py
+++ b/solution.py
@@ -454,7 +454,7 @@
             pltpu.SemaphoreType.DMA((5,)),
             *[pltpu.SemaphoreType.DMA] * 5,
         ],
-        compiler_params=pltpu.CompilerParams(collective_id=collective_id, has_side_effects=True, vmem_limit_bytes=48 * 2**20),
+        compiler_params=pltpu.CompilerParams(collective_id=collective_id, has_side_effects=True, vmem_limit_bytes=60 * 2**20),
         name="tri_attn",
     )(piece, w, q, k, vt, gate, z)
     return out.reshape(8, 1024, 128)

time: 222 us -> 230 us (1.036)
  local copies, waits for them, and re-layouts: 5.51 us -> 9.77 us
  Pallas kernels: 210 us -> 214 us
    unnamed x38 -> x46, local copies, waits for them, and re-layouts: 4.05 us -> 8.31 us
    pallas_call x2, Pallas kernels: 178 us -> 182 us  [attention(): pl.pallas_call(attn_kernel, in_specs=[vmem, vmem] + [hbm] * 5, out_specs=...]
where the time goes in v9:
time: 230 us; the launch traced here: 227 us
  Pallas kernels  214 us (93%)
  local copies, waits for them, and re-layouts  9.77 us (4%)
    pallas_call x2, Pallas kernels, attention(): pl.pallas_call(attn_kernel, in_specs=[vmem, vmem] + [hbm] * 5, out_specs=...  182 us
    pallas_call x2, Pallas kernels, pre(): pl.pallas_call(pre_kernel, grid=(8,), in_specs=[pl.BlockSpec((1, 1024, 12...  21.5 us
    pallas_call x1, Pallas kernels, trans(): pl.pallas_call(trans_kernel, grid=(8,), in_specs=[pl.BlockSpec((1, 1024,...  10.6 us
    unnamed x46, local copies, waits for them, and re-layouts  8.31 us

profile of v9, /device:TPU:12, one launch (start us, length us, event | category | flops | bytes accessed | tf_op | source)
XLA Modules:
  0.0 226.5 jit_solution(13002644124958253956)
XLA Ops:
  0.0 0.8 convert_element_type.62
  0.8 0.7 pad.8.bw_ref
  1.5 0.7 pad.7.bw_ref
  2.2 0.1 broadcast_in_dim.44
  2.3 0.1 fusion.47.mask_ref
  2.4 10.8 %tri_pre.2 = (bf16[8,1024,128]{2,1,0:T(8,128)(2,1)S(1)}, bf16[8,1024,128]{2,1,0:T(8,128)(2,1)S(1)}, bf16[8,4,48,1024]{3,2,1,0:T(8,128)(2,1)}, bf16[8,1024,128]{2,1,0:T(8,128)(2,1)}, bf16[36,8,128]{2,1,0:T(8,128)(2,1)S(1)}) custom-call(bf16[8,1024,128]{2,1,0:T(8,128)(2,1)} %z_hbm.1, f32[1,128]{1,0:T(1,128)} %bitcast.232, bf16[128,512]{1,0:T(8,128)(2,1)} %proj_ref.2, ...), custom_call_target="tpu_custom_call" | custom-call | tf_op jit(solution)/shard_map/tri_pre/pallas_call | solution.py:511
  13.2 1.3 copy-done.3
  14.5 1.4 copy-done.4
  15.9 0.6 copy-done.6
  16.5 0.0 copy-done.11
  16.5 0.0 copy-done.25
  16.5 0.0 copy-start.41
  16.5 91.3 %tri_attn.2 = bf16[8,128,8,128]{3,2,1,0:T(8,128)(2,1)} custom-call(bf16[36,8,128]{2,1,0:T(8,128)(2,1)} %copy-done.6, bf16[128,128]{1,0:T(8,128)(2,1)S(1)} %copy-done.25, bf16[8,1024,128]{2,1,0:T(8,128)(2,1)} %copy-done.3, bf16[8,1024,128]{2,1,0:T(8,128)(2,1)} %copy-done.4, bf16[8,4,48,1024]{3,2,1,0:T(8,128)(2,1)} %get-tuple-element.340.vt_hbm, ...), custom_call_target="tpu_custom_call" | custom-call | tf_op jit(solution)/shard_map/tri_attn/pallas_call | solution.py:427
  107.8 0.0 copy-start.26
  107.9 0.0 copy-done.22
  107.9 0.0 copy-done.40
  107.9 0.0 copy-done.41
  107.9 10.7 %tri_pre.3 = (bf16[8,1024,128]{2,1,0:T(8,128)(2,1)S(1)}, bf16[8,1024,128]{2,1,0:T(8,128)(2,1)S(1)}, bf16[8,4,48,1024]{3,2,1,0:T(8,128)(2,1)}, bf16[8,1024,128]{2,1,0:T(8,128)(2,1)}, bf16[36,8,128]{2,1,0:T(8,128)(2,1)S(1)}) custom-call(bf16[8,1024,128]{2,1,0:T(8,128)(2,1)} %bitcast.217, f32[1,128]{1,0:T(1,128)S(1)} %bitcast.236, ...), custom_call_target="tpu_custom_call" | custom-call | tf_op jit(solution)/shard_map/tri_pre/pallas_call | solution.py:511
  118.6 1.3 copy-done.1
  120.0 1.4 copy-done.2
  121.3 0.6 copy-done.5
  122.0 0.0 copy-done.26
  122.0 0.0 copy-start.36
  122.0 90.5 %tri_attn.3 = bf16[8,128,8,128]{3,2,1,0:T(8,128)(2,1)} custom-call(bf16[36,8,128]{2,1,0:T(8,128)(2,1)} %copy-done.5, bf16[128,128]{1,0:T(8,128)(2,1)S(1)} %copy-done.26, bf16[8,1024,128]{2,1,0:T(8,128)(2,1)} %copy-done.1, bf16[8,1024,128]{2,1,0:T(8,128)(2,1)} %copy-done.2, bf16[8,4,48,1024]{3,2,1,0:T(8,128)(2,1)} %get-tuple-element.345.vt_hbm, ...), custom_call_target="tpu_custom_call" | custom-call | tf_op jit(solution)/shard_map/tri_attn/pallas_call | solution.py:427
  212.5 0.0 copy-start.34
  212.5 0.0 copy-start.38
  212.5 0.0 copy-done.17
  212.5 0.0 copy-done.19
  212.5 1.6 copy-done
  214.1 10.6 %tri_trans.3 = (bf16[8,1024,128]{2,1,0:T(8,128)(2,1)}, f32[8,128]{1,0:T(8,128)S(1)}) custom-call(bf16[8,1024,128]{2,1,0:T(8,128)(2,1)S(1)} %bitcast.206, f32[1,128]{1,0:T(1,128)S(1)} %bitcast.230, bf16[128,512]{1,0:T(8,128)(2,1)S(1)} %copy-done.17, f32[1,512]{1,0:T(1,128)S(1)} %bitcast.224, bf16[512,128]{1,0:T(8,128)(2,1)S(1)} %copy-done.19), custom_call_target="tpu_custom_call" | custom-call | tf_op jit(solution)/shard_map/tri_trans/pallas_call | solution.py:559
  224.7 0.7 reduce_max.18
  226.1 0.2 conditional.1
  (30 shorter events, 0.1 us)
Async XLA Ops:
  0.0 16.5 %copy-start.11 = (bf16[8,1024,128]{2,1,0:T(8,128)(2,1)S(1)}, bf16[8,1024,128]{2,1,0:T(8,128)(2,1)}, u32[]{:S(2)}) copy-start(bf16[8,1024,128]{2,1,0:T(8,128)(2,1)} %z_hbm.1) | copy-start | bytes 6291460
  0.0 16.5 %copy-start.25 = (bf16[128,128]{1,0:T(8,128)(2,1)S(1)}, bf16[128,128]{1,0:T(8,128)(2,1)}, u32[]{:S(2)}) copy-start(bf16[128,128]{1,0:T(8,128)(2,1)} %w_ref.2) | copy-start | bytes 98308
  13.2 1.3 copy-start.3
  14.5 1.4 copy-start.4
  15.8 0.6 copy-start.6
  16.5 91.4 %copy-start.22 = (bf16[128,512]{1,0:T(8,128)(2,1)S(1)}, bf16[128,512]{1,0:T(8,128)(2,1)}, u32[]{:S(2)}) copy-start(bf16[128,512]{1,0:T(8,128)(2,1)} %proj_ref.3) | copy-start | bytes 393220
  16.5 91.4 %copy-start.40 = (f32[128]{0:T(128)S(1)}, f32[128]{0:T(128)}, u32[]{:S(2)}) copy-start(f32[128]{0:T(128)} %param.37) | copy-start | bytes 1540
  16.5 91.4 %copy-start.41 = (f32[128]{0:T(128)S(1)}, f32[128]{0:T(128)}, u32[]{:S(2)}) copy-start(f32[128]{0:T(128)} %param.39) | copy-start | bytes 1540
  107.8 14.1 %copy-start.26 = (bf16[128,128]{1,0:T(8,128)(2,1)S(1)}, bf16[128,128]{1,0:T(8,128)(2,1)}, u32[]{:S(2)}) copy-start(bf16[128,128]{1,0:T(8,128)(2,1)} %w_ref.3) | copy-start | bytes 98308
  118.6 1.3 copy-start.1
  120.0 1.4 copy-start.2
  121.3 0.6 copy-start.5
  122.0 90.5 %copy-start.17 = (bf16[128,512]{1,0:T(8,128)(2,1)S(1)}, bf16[128,512]{1,0:T(8,128)(2,1)}, u32[]{:S(2)}) copy-start(bf16[128,512]{1,0:T(8,128)(2,1)} %w1_ref.1) | copy-start | bytes 393220
  122.0 90.5 %copy-start.19 = (bf16[512,128]{1,0:T(8,128)(2,1)S(1)}, bf16[512,128]{1,0:T(8,128)(2,1)}, u32[]{:S(2)}) copy-start(bf16[512,128]{1,0:T(8,128)(2,1)} %w2_ref.1) | copy-start | bytes 393220
  122.0 90.5 %copy-start.32 = (f32[512]{0:T(512)S(1)}, f32[512]{0:T(512)}, u32[]{:S(2)}) copy-start(f32[512]{0:T(512)} %param.44) | copy-start | bytes 6148
  122.0 90.5 %copy-start.36 = (f32[128]{0:T(128)S(1)}, f32[128]{0:T(128)}, u32[]{:S(2)}) copy-start(f32[128]{0:T(128)} %param.42) | copy-start | bytes 1540
  212.5 13.6 %copy-start.34 = (bf16[128,4]{0,1:T(4,128)(2,1)S(1)}, bf16[128,4]{0,1:T(4,128)(2,1)}, u32[]{:S(2)}) copy-start(bf16[128,4]{0,1:T(4,128)(2,1)} %param.35) | copy-start | bytes 3076
  212.5 13.6 %copy-start.38 = (f32[128]{0:T(128)S(1)}, f32[128]{0:T(128)}, u32[]{:S(2)}) copy-start(f32[128]{0:T(128)} %param.32) | copy-start | bytes 1540
  212.5 1.6 copy-start
  214.1 11.9 %copy-start.21 = (bf16[128,512]{1,0:T(8,128)(2,1)S(1)}, bf16[128,512]{1,0:T(8,128)(2,1)}, u32[]{:S(2)}) copy-start(bf16[128,512]{1,0:T(8,128)(2,1)} %proj_ref.2) | copy-start | bytes 393220
  214.1 11.9 %copy-start.35 = (bf16[128,4]{0,1:T(4,128)(2,1)S(1)}, bf16[128,4]{0,1:T(4,128)(2,1)}, u32[]{:S(2)}) copy-start(bf16[128,4]{0,1:T(4,128)(2,1)} %param.40) | copy-start | bytes 3076
  214.1 12.0 %copy-start.39 = (f32[128]{0:T(128)S(1)}, f32[128]{0:T(128)}, u32[]{:S(2)}) copy-start(f32[128]{0:T(128)} %param.34) | copy-start | bytes 1540
  214.1 12.0 %copy-start.42 = (s32[8]{0:T(128)S(1)}, s32[8]{0:T(128)}, u32[]{:S(2)}) copy-start(s32[8]{0:T(128)} %param.31) | copy-start | bytes 100
